TPU v7x, 32 devices: a whole 2x2x4 slice. The times are simulated.
32 devices in a mesh: dp: 16 (over z, y, x), mp: 2 (over core).
Axes of the slice: x: 2, y: 2, z: 4, core: 2. Of those that a mesh axis runs over, the one named last changes fastest.
Arguments:
- tokens: bfloat16 [100864, 384], P(('dp', 'mp')), may hold values from -6 to 6
- w_query: bfloat16 [384, 384], P('dp', 'mp'), may hold values from -0.3125 to 0.3125
- w_key: bfloat16 [384, 384], P('dp', 'mp'), may hold values from -0.3125 to 0.3125
- w_value: bfloat16 [384, 384], P('dp', 'mp'), may hold values from -0.3125 to 0.3125
- w_out: bfloat16 [384, 384], P('mp', 'dp'), may hold values from -1.25 to 1.25
- w_up: bfloat16 [384, 1536], P('dp', 'mp'), may hold values from -0.3125 to 0.3125
- w_down: bfloat16 [1536, 384], P('mp', 'dp'), may hold values from -0.3125 to 0.3125
- ln1_gain: bfloat16 [384], P('dp'), may hold values from 0.5 to 1.5
- ln1_bias: bfloat16 [384], P('dp'), may hold values from -3 to 3
- b_query: bfloat16 [384], P('dp'), may hold values from -3 to 3
- b_value: bfloat16 [384], P('dp'), may hold values from -3 to 3
- b_out: bfloat16 [384], P('dp'), may hold values from -3 to 3
- ln2_gain: bfloat16 [384], P('dp'), may hold values from 0.5 to 1.5
- ln2_bias: bfloat16 [384], P('dp'), may hold values from -3 to 3
- b_up: bfloat16 [1536], P('dp'), may hold values from -3 to 3
- b_down: bfloat16 [384], P('dp'), may hold values from -3 to 3
- cotangent: bfloat16 [100864, 384], P(('dp', 'mp')), may hold values from -6 to 6
Outputs:
- out: bfloat16 [100864, 384], P(('dp', 'mp'))
- grad_tokens: float32 [100864, 384], P(('dp', 'mp'))
- grad_w_query: float32 [384, 384], P('dp', 'mp')
- grad_w_key: float32 [384, 384], P('dp', 'mp')
- grad_w_value: float32 [384, 384], P('dp', 'mp')
- grad_w_out: float32 [384, 384], P('mp', 'dp')
- grad_w_up: float32 [384, 1536], P('dp', 'mp')
- grad_w_down: float32 [1536, 384], P('mp', 'dp')
- grad_ln1_gain: float32 [384], P(('dp', 'mp'))
- grad_ln1_bias: float32 [384], P(('dp', 'mp'))
- grad_b_query: float32 [384], P(('dp', 'mp'))
- grad_b_value: float32 [384], P(('dp', 'mp'))
- grad_b_out: float32 [384], P(('dp', 'mp'))
- grad_ln2_gain: float32 [384], P(('dp', 'mp'))
- grad_ln2_bias: float32 [384], P(('dp', 'mp'))
- grad_b_up: float32 [1536], P(('dp', 'mp'))
- grad_b_down: float32 [384], P(('dp', 'mp'))
All inputs are finite; a program needn't handle non-finite values.
Results may differ from a plain program's by a relative error of at most 0.012.
Values may be sent and summed in bfloat16 or wider, within the bound.
A program may use at most 256 MiB of HBM per device.

v0:
```python
import math

import jax
import jax.numpy as jnp
from jax import lax
from jax.sharding import PartitionSpec as P

D = 384
HD = 64
FF = 1536
S = 197
IMG_BLK = 4


epsilon = 1e-06
inv_root_two = 0.7071067811865476
inv_root_tau = 0.3989422804014327


def cut_along(shard, dim, count):
    shape = shard.shape
    parts = shard.reshape(*shape[:dim], count, shape[dim] // count, *shape[dim + 1 :])
    return jnp.moveaxis(parts, dim, 0)


def sent_and_summed(shard, axis, dim):
    count = lax.axis_size(axis)
    parts = lax.all_to_all(cut_along(shard, dim, count), axis, 0, 0, tiled=True)
    return jnp.sum(parts.astype(jnp.float32), axis=0)


def sent_together(arrays, axis, dim, along):
    ends, at = ([], 0)
    for a in arrays[:-1]:
        at += a.shape[along]
        ends.append(at)
    both = jnp.concatenate(arrays, axis=along)
    return tuple(jnp.split(sent_and_summed(both, axis, dim), ends, axis=along))


def norm_forward(values, gain_row, shift_row):
    row_mean = jnp.mean(values, axis=-1, keepdims=True)
    centred = values - row_mean
    variance = jnp.mean(centred * centred, axis=-1, keepdims=True)
    inv_std = lax.rsqrt(variance + epsilon)
    normed = centred * inv_std
    return (normed, inv_std, normed * gain_row + shift_row)


def norm_backward(grad_out, normed, inv_std, gain_row):
    scaled = grad_out * gain_row
    return inv_std * (
        scaled
        - jnp.mean(scaled, axis=-1, keepdims=True)
        - normed * jnp.mean(scaled * normed, axis=-1, keepdims=True)
    )


def gelu_value(pre_act):
    return 0.5 * pre_act * (1.0 + jax.scipy.special.erf(pre_act * inv_root_two))


def gelu_slope(pre_act):
    return (
        0.5 * (1.0 + jax.scipy.special.erf(pre_act * inv_root_two))
        + pre_act * jnp.exp(-0.5 * pre_act * pre_act) * inv_root_tau
    )


def dot_lead(left, right):
    return lax.dot_general(
        left, right, (((0,), (0,)), ((), ())), preferred_element_type=jnp.float32
    )


def dot_last(left, right):
    return lax.dot_general(
        left, right, (((1,), (1,)), ((), ())), preferred_element_type=jnp.float32
    )


def attend(query_rows, key_rows, value_rows):
    score_scale = 1.0 / math.sqrt(query_rows.shape[-1])
    scores = (
        jnp.einsum("bqhd,bkhd->bhqk", query_rows, key_rows, preferred_element_type=jnp.float32)
        * score_scale
    )
    row_max = jnp.max(scores, axis=-1, keepdims=True)
    log_total = row_max + jnp.log(jnp.sum(jnp.exp(scores - row_max), axis=-1, keepdims=True))
    attn_probs = jnp.exp(scores - log_total).astype(jnp.bfloat16)
    mixed_rows = jnp.einsum(
        "bhqk,bkhd->bqhd", attn_probs, value_rows, preferred_element_type=jnp.float32
    ).astype(jnp.bfloat16)
    return (mixed_rows, log_total[..., 0])


def attend_back(query_rows, key_rows, value_rows, log_total, grad_mixed):
    score_scale = 1.0 / math.sqrt(query_rows.shape[-1])
    scores = (
        jnp.einsum("bqhd,bkhd->bhqk", query_rows, key_rows, preferred_element_type=jnp.float32)
        * score_scale
    )
    attn_probs = jnp.exp(scores - log_total[..., None])
    prob_rows = attn_probs.astype(jnp.bfloat16)
    grad_value = jnp.einsum(
        "bhqk,bqhd->bkhd", prob_rows, grad_mixed, preferred_element_type=jnp.float32
    )
    grad_probs = jnp.einsum(
        "bqhd,bkhd->bhqk", grad_mixed, value_rows, preferred_element_type=jnp.float32
    )
    row_delta = jnp.sum(attn_probs * grad_probs, axis=-1, keepdims=True)
    grad_scores = (attn_probs * (grad_probs - row_delta) * score_scale).astype(jnp.bfloat16)
    grad_query = jnp.einsum(
        "bhqk,bkhd->bqhd", grad_scores, key_rows, preferred_element_type=jnp.float32
    )
    grad_key = jnp.einsum(
        "bhqk,bqhd->bkhd", grad_scores, query_rows, preferred_element_type=jnp.float32
    )
    return (grad_query, grad_key, grad_value)


def on_device(
    tokens,
    w_query,
    w_key,
    w_value,
    w_out,
    w_up,
    w_down,
    ln1_gain,
    ln1_bias,
    b_query,
    b_value,
    b_out,
    ln2_gain,
    ln2_bias,
    b_up,
    b_down,
    cotangent,
):
    local_rows = tokens.shape[0]
    params = (
        lax.all_gather(w_query, "dp", axis=0, tiled=True),
        lax.all_gather(w_key, "dp", axis=0, tiled=True),
        lax.all_gather(w_value, "dp", axis=0, tiled=True),
        lax.all_gather(w_out, "dp", axis=1, tiled=True),
        lax.all_gather(w_up, "dp", axis=0, tiled=True),
        lax.all_gather(w_down, "dp", axis=1, tiled=True),
        lax.all_gather(ln1_gain, "dp", axis=0, tiled=True),
        lax.all_gather(ln1_bias, "dp", axis=0, tiled=True),
        lax.all_gather(b_query, "dp", axis=0, tiled=True),
        lax.all_gather(b_value, "dp", axis=0, tiled=True),
        lax.all_gather(b_out, "dp", axis=0, tiled=True),
        lax.all_gather(ln2_gain, "dp", axis=0, tiled=True),
        lax.all_gather(ln2_bias, "dp", axis=0, tiled=True),
        lax.all_gather(b_up, "dp", axis=0, tiled=True),
        lax.all_gather(b_down, "dp", axis=0, tiled=True),
    )
    matrices = (params[0], params[1], params[2], params[3], params[4], params[5])
    group_rows = local_rows * lax.axis_size("mp")
    head_start = lax.axis_index("mp") * params[0].shape[1]
    hidden_start = lax.axis_index("mp") * params[4].shape[1]
    query_full, key_full, value_full, out_full, up_full, down_full = (
        matrices[0],
        matrices[1],
        matrices[2],
        matrices[3],
        matrices[4],
        matrices[5],
    )
    head_cols = query_full.shape[1]
    hidden_cols = up_full.shape[1]
    heads_local = head_cols // HD
    blocks = group_rows // (IMG_BLK * S)
    gain_one = params[6].astype(jnp.float32)
    shift_one = params[7].astype(jnp.float32)
    bias_query = lax.dynamic_slice_in_dim(params[8], head_start, head_cols, 0).astype(jnp.float32)
    bias_value = lax.dynamic_slice_in_dim(params[9], head_start, head_cols, 0).astype(jnp.float32)
    bias_out = params[10].astype(jnp.float32)
    gain_two = params[11].astype(jnp.float32)
    shift_two = params[12].astype(jnp.float32)
    bias_up = lax.dynamic_slice_in_dim(params[13], hidden_start, hidden_cols, 0).astype(jnp.float32)
    bias_down = params[14].astype(jnp.float32)

    def view(rows):
        return rows.reshape(blocks, IMG_BLK, S, heads_local, HD)

    tok_f = tokens.astype(jnp.float32)
    normed_one, inv_one, pre_one = norm_forward(tok_f, gain_one, shift_one)
    normed_local = pre_one.astype(jnp.bfloat16)
    normed_all = lax.all_gather(normed_local, "mp", axis=0, tiled=True)
    query_rows = (
        jnp.dot(normed_all, query_full, preferred_element_type=jnp.float32) + bias_query
    ).astype(jnp.bfloat16)
    key_rows = jnp.dot(normed_all, key_full, preferred_element_type=jnp.float32).astype(
        jnp.bfloat16
    )
    value_rows = (
        jnp.dot(normed_all, value_full, preferred_element_type=jnp.float32) + bias_value
    ).astype(jnp.bfloat16)
    mixed_heads, log_total = lax.map(
        lambda packed: attend(packed[0], packed[1], packed[2]),
        (view(query_rows), view(key_rows), view(value_rows)),
    )
    mixed_rows = mixed_heads.reshape(group_rows, head_cols)
    attn_part = lax.psum_scatter(
        jnp.dot(mixed_rows, out_full, preferred_element_type=jnp.float32),
        "mp",
        scatter_dimension=0,
        tiled=True,
    )
    resid_one = tok_f + attn_part + bias_out
    normed_two, inv_two, pre_two = norm_forward(resid_one, gain_two, shift_two)
    hidden_local = pre_two.astype(jnp.bfloat16)
    hidden_all = lax.all_gather(hidden_local, "mp", axis=0, tiled=True)
    pre_act = jnp.dot(hidden_all, up_full, preferred_element_type=jnp.float32) + bias_up
    active = gelu_value(pre_act).astype(jnp.bfloat16)
    mlp_part = lax.psum_scatter(
        jnp.dot(active, down_full, preferred_element_type=jnp.float32).astype(jnp.bfloat16),
        "mp",
        scatter_dimension=0,
        tiled=True,
    ).astype(jnp.float32)
    block_out = resid_one + mlp_part + bias_down
    back_params = (
        lax.all_gather(w_query, "dp", axis=0, tiled=True),
        lax.all_gather(w_key, "dp", axis=0, tiled=True),
        lax.all_gather(w_value, "dp", axis=0, tiled=True),
        lax.all_gather(w_out, "dp", axis=1, tiled=True),
        lax.all_gather(w_up, "dp", axis=0, tiled=True),
        lax.all_gather(w_down, "dp", axis=1, tiled=True),
        lax.all_gather(ln1_gain, "dp", axis=0, tiled=True),
        lax.all_gather(ln1_bias, "dp", axis=0, tiled=True),
        lax.all_gather(b_query, "dp", axis=0, tiled=True),
        lax.all_gather(b_value, "dp", axis=0, tiled=True),
        lax.all_gather(b_out, "dp", axis=0, tiled=True),
        lax.all_gather(ln2_gain, "dp", axis=0, tiled=True),
        lax.all_gather(ln2_bias, "dp", axis=0, tiled=True),
        lax.all_gather(b_up, "dp", axis=0, tiled=True),
        lax.all_gather(b_down, "dp", axis=0, tiled=True),
    )
    back_mats = (
        back_params[0],
        back_params[1],
        back_params[2],
        back_params[3],
        back_params[4],
        back_params[5],
    )
    query_back, key_back, value_back, out_back, up_back, down_back = (
        back_mats[0],
        back_mats[1],
        back_mats[2],
        back_mats[3],
        back_mats[4],
        back_mats[5],
    )
    gain_one_back = back_params[6].astype(jnp.float32)
    gain_two_back = back_params[11].astype(jnp.float32)
    grad_top = cotangent.astype(jnp.float32)
    cot_all = lax.all_gather(cotangent, "mp", axis=0, tiled=True)
    grad_active = dot_last(cot_all, down_back)
    grad_pre = grad_active * gelu_slope(pre_act)
    grad_pre_rows = grad_pre.astype(jnp.bfloat16)
    grad_hidden = lax.psum_scatter(
        dot_last(grad_pre_rows, up_back), "mp", scatter_dimension=0, tiled=True
    )
    grad_resid = grad_top + norm_backward(grad_hidden, normed_two, inv_two, gain_two_back)
    resid_local = grad_resid.astype(jnp.bfloat16)
    resid_all = lax.all_gather(resid_local, "mp", axis=0, tiled=True)
    grad_mixed = dot_last(resid_all, out_back).astype(jnp.bfloat16)
    grad_query, grad_key, grad_value = lax.map(
        lambda packed: attend_back(packed[0], packed[1], packed[2], packed[3], packed[4]),
        (view(query_rows), view(key_rows), view(value_rows), log_total, view(grad_mixed)),
    )
    grad_query = grad_query.reshape(group_rows, head_cols)
    grad_key = grad_key.reshape(group_rows, head_cols)
    grad_value = grad_value.reshape(group_rows, head_cols)
    query_grad_rows = grad_query.astype(jnp.bfloat16)
    key_grad_rows = grad_key.astype(jnp.bfloat16)
    value_grad_rows = grad_value.astype(jnp.bfloat16)
    grad_normed = lax.psum_scatter(
        (
            dot_last(query_grad_rows, query_back)
            + dot_last(key_grad_rows, key_back)
            + dot_last(value_grad_rows, value_back)
        ).astype(jnp.bfloat16),
        "mp",
        scatter_dimension=0,
        tiled=True,
    ).astype(jnp.float32)
    grad_input = grad_resid + norm_backward(grad_normed, normed_one, inv_one, gain_one_back)
    local_grads = (
        dot_lead(normed_all, query_grad_rows),
        dot_lead(normed_all, key_grad_rows),
        dot_lead(normed_all, value_grad_rows),
        dot_lead(mixed_rows, resid_all),
        dot_lead(hidden_all, grad_pre_rows),
        dot_lead(active, cot_all),
    )
    matrix_grads = (
        *sent_together(
            (
                local_grads[0].astype(jnp.bfloat16),
                local_grads[1].astype(jnp.bfloat16),
                local_grads[2].astype(jnp.bfloat16),
            ),
            "dp",
            0,
            1,
        ),
        sent_and_summed(local_grads[3].astype(jnp.bfloat16), "dp", 1),
        sent_and_summed(local_grads[4].astype(jnp.bfloat16), "dp", 0),
        sent_and_summed(local_grads[5].astype(jnp.bfloat16), "dp", 1),
    )
    zero_width = jnp.zeros((D,), jnp.float32)
    zero_hidden = jnp.zeros((FF,), jnp.float32)
    query_bias_grad = lax.dynamic_update_slice_in_dim(
        zero_width, jnp.sum(grad_query, axis=0), head_start, 0
    )
    value_bias_grad = lax.dynamic_update_slice_in_dim(
        zero_width, jnp.sum(grad_value, axis=0), head_start, 0
    )
    up_bias_grad = lax.dynamic_update_slice_in_dim(
        zero_hidden, jnp.sum(grad_pre, axis=0), hidden_start, 0
    )
    vector_grads = (
        lax.psum_scatter(
            jnp.sum(grad_normed * normed_one, axis=0), ("dp", "mp"), scatter_dimension=0, tiled=True
        ),
        lax.psum_scatter(
            jnp.sum(grad_normed, axis=0), ("dp", "mp"), scatter_dimension=0, tiled=True
        ),
        lax.psum_scatter(query_bias_grad, ("dp", "mp"), scatter_dimension=0, tiled=True),
        lax.psum_scatter(value_bias_grad, ("dp", "mp"), scatter_dimension=0, tiled=True),
        lax.psum_scatter(
            jnp.sum(grad_resid, axis=0), ("dp", "mp"), scatter_dimension=0, tiled=True
        ),
        lax.psum_scatter(
            jnp.sum(grad_hidden * normed_two, axis=0), ("dp", "mp"), scatter_dimension=0, tiled=True
        ),
        lax.psum_scatter(
            jnp.sum(grad_hidden, axis=0), ("dp", "mp"), scatter_dimension=0, tiled=True
        ),
        lax.psum_scatter(up_bias_grad, ("dp", "mp"), scatter_dimension=0, tiled=True),
        lax.psum_scatter(jnp.sum(grad_top, axis=0), ("dp", "mp"), scatter_dimension=0, tiled=True),
    )
    return (
        block_out.astype(jnp.bfloat16),
        grad_input,
        matrix_grads[0],
        matrix_grads[1],
        matrix_grads[2],
        matrix_grads[3],
        matrix_grads[4],
        matrix_grads[5],
        vector_grads[0],
        vector_grads[1],
        vector_grads[2],
        vector_grads[3],
        vector_grads[4],
        vector_grads[5],
        vector_grads[6],
        vector_grads[7],
        vector_grads[8],
    )


def solution(mesh):
    placed = (
        P(("dp", "mp"), None),
        P("dp", "mp"),
        P("dp", "mp"),
        P("dp", "mp"),
        P("mp", "dp"),
        P("dp", "mp"),
        P("mp", "dp"),
        P("dp"),
        P("dp"),
        P("dp"),
        P("dp"),
        P("dp"),
        P("dp"),
        P("dp"),
        P("dp"),
        P("dp"),
        P(("dp", "mp"), None),
    )
    return jax.shard_map(
        on_device,
        mesh=mesh,
        in_specs=placed,
        out_specs=(
            P(("dp", "mp"), None),
            P(("dp", "mp"), None),
            P("dp", "mp"),
            P("dp", "mp"),
            P("dp", "mp"),
            P("mp", "dp"),
            P("dp", "mp"),
            P("mp", "dp"),
            P(("dp", "mp")),
            P(("dp", "mp")),
            P(("dp", "mp")),
            P(("dp", "mp")),
            P(("dp", "mp")),
            P(("dp", "mp")),
            P(("dp", "mp")),
            P(("dp", "mp")),
            P(("dp", "mp")),
        ),
        check_vma=False,
    )
```

profile of v0, /device:TPU:0, one launch (start us, length us, event | category | flops | bytes accessed | tf_op | source)
XLA Modules:
  0.0 928.1 jit_solution(14674667465462407066)
XLA Ops:
  17.6 78.6 %all-reduce.19 = (bf16[384]{0:T(512)(128)(2,1)S(1)}, bf16[384]{0:T(512)(128)(2,1)S(1)}, bf16[384]{0:T(512)(128)(2,1)S(1)}, bf16[384]{0:T(512)(128)(2,1)S(1)}, bf...) all-reduce(bf16[384]{0:T(512)(128)(2,1)S(1)} %dynamic-update-slice., ...), channel_id=1, replica_groups=mesh['dp'=16,'mp'=2] {'dp'}, use_global_device_ids=true, to_apply=%add.1 | all-reduce | flops 4608 | bytes 18432
  104.8 36.5 %all_gather.70 = bf16[384,192]{1,0:T(8,128)(2,1)S(1)} all-gather(bf16[24,192]{1,0:T(8,128)(2,1)S(1)} %copy-done.21), channel_id=1, replica_groups=mesh['dp'=16,'mp'=2] {'dp'}, dimensions={0}, use_global_device_ids=true | all-gather | bytes 156672 | tf_op jit(solution)/shard_map/all_gather | solution.py:143
  141.3 38.7 %all_gather.72 = bf16[384,192]{1,0:T(8,128)(2,1)S(1)} all-gather(bf16[24,192]{1,0:T(8,128)(2,1)S(1)} %copy-done.22), channel_id=1, replica_groups=mesh['dp'=16,'mp'=2] {'dp'}, dimensions={0}, use_global_device_ids=true | all-gather | bytes 156672 | tf_op jit(solution)/shard_map/all_gather | solution.py:144
  180.1 36.5 %all_gather.68 = bf16[384,192]{1,0:T(8,128)(2,1)S(1)} all-gather(bf16[24,192]{1,0:T(8,128)(2,1)S(1)} %copy-done.23), channel_id=1, replica_groups=mesh['dp'=16,'mp'=2] {'dp'}, dimensions={0}, use_global_device_ids=true | all-gather | bytes 156672 | tf_op jit(solution)/shard_map/all_gather | solution.py:145
  216.6 38.5 %all_gather.73 = bf16[192,384]{0,1:T(8,128)(2,1)S(1)} all-gather(bf16[192,24]{0,1:T(8,128)(2,1)S(1)} %copy-done.24), channel_id=1, replica_groups=mesh['dp'=16,'mp'=2] {'dp'}, dimensions={1}, use_global_device_ids=true | all-gather | bytes 156672 | tf_op jit(solution)/shard_map/all_gather | solution.py:146
  260.9 12.4 %reshape.151 = bf16[8,4,197,3,64]{2,1,0,4,3:T(4,128)(2,1)} reshape(bf16[6304,192]{0,1:T(8,128)(2,1)} %fusion.65) | data formatting | bytes 4841472 | tf_op jit(solution)/shard_map/reshape | solution.py:186
  282.2 12.2 %reshape.150 = bf16[8,4,197,3,64]{2,1,0,4,3:T(4,128)(2,1)} reshape(bf16[6304,192]{0,1:T(8,128)(2,1)} %fusion.64) | data formatting | bytes 4841472 | tf_op jit(solution)/shard_map/reshape | solution.py:186
  305.5 12.6 %reshape.152 = bf16[8,4,197,3,64]{2,1,0,4,3:T(4,128)(2,1)} reshape(bf16[6304,192]{0,1:T(8,128)(2,1)} %convolution_convert_fusion.3) | data formatting | bytes 4841472 | tf_op jit(solution)/shard_map/reshape | solution.py:186
  323.4 38.6 %while.26 = (s32[]{:T(128)}, bf16[8,4,197,3,64]{2,1,0,4,3:T(4,128)(2,1)}, f32[8,4,3,197]{3,2,1,0:T(4,128)S(1)}, bf16[8,4,197,3,64]{2,4,3,1,0:T(8,128)(2,1)}, bf1...) while((s32[]{:T(128)}, bf16[8,4,197,3,64]{2,1,0,4,3:T(4,128)(2,1)}, ...), condition=%wide.region_5.6_spmd, body=%wide.region_2.5_spmd.sunk | while | flops 123095840 | bytes 7871025 | solution.py:201
  376.1 14.6 %reduce-scatter.5.cloned.1.call-done = f32[3152,384]{1,0:T(8,128)} async-done(((f32[6304,384]{1,0:T(8,128)}), f32[3152,384]{1,0:T(8,128)}) %reduce-scatter.5.cloned.1.call-update) | async-done | bytes 4841488 | tf_op jit(solution)/shard_map/reduce_scatter | solution.py:206
  399.7 43.3 %all_gather.78 = bf16[384,768]{1,0:T(8,128)(2,1)S(1)} all-gather(bf16[24,768]{1,0:T(8,128)(2,1)S(1)} %copy-done.16), channel_id=1, replica_groups=mesh['dp'=16,'mp'=2] {'dp'}, dimensions={0}, use_global_device_ids=true | all-gather | bytes 626688 | tf_op jit(solution)/shard_map/all_gather | solution.py:147
  443.0 38.9 %all_gather.80 = bf16[768,384]{0,1:T(8,128)(2,1)S(1)} all-gather(bf16[768,24]{0,1:T(8,128)(2,1)S(1)} %copy-done.17), channel_id=1, replica_groups=mesh['dp'=16,'mp'=2] {'dp'}, dimensions={1}, use_global_device_ids=true | all-gather | bytes 626688 | tf_op jit(solution)/shard_map/all_gather | solution.py:148
  482.0 12.9 %multiply_convert_fusion.1 = (bf16[6304,768]{1,0:T(8,128)(2,1)}, f32[6304,768]{1,0:T(8,128)}) fusion(f32[768]{0:T(1024)S(1)} %dynamic-slice_convert_fusion, bf16[6304,384]{1,0:T(8,128)(2,1)} %all-gather.7.cloned.1.call-done, bf16[384,768]{1,0:T(8,128)(2,1)S(1)} %all_gather.78), kind=kOutput, calls=%fused_computation.64 | convolution fusion | flops 3747299328 | bytes 34483200 | tf_op jit(solution)/shard_map/dot_general | solution.py:216
  494.9 14.1 %fusion.95 = (f32[768]{0:T(1024)}, bf16[6304,768]{1,0:T(8,128)(2,1)S(1)}) fusion(f32[6304,768]{1,0:T(8,128)} %get-tuple-element.223, f32[768]{0:T(1024)S(1)} %dynamic-slice_convert_fusion, bf16[6304,384]{1,0:T(8,128)(2,1)} %all-gather.9.cloned.1.call-done, bf16[768,384]{0,1:T(8,128)(2,1)S(1)} %all_gather.80), kind=kOutput, calls=%fused_computation.138 | convolution fusion | flops 3776347392 | bytes 34486272 | tf_op jit(solution)/shard_map/dot_general | solution.py:77
  520.2 9.2 convolution_convert_fusion.1
  543.8 8.5 reduce-scatter.7.cloned.1.call-done
  552.3 9.1 fusion.89
  565.6 15.8 %all-gather.11.cloned.1.call-done = bf16[6304,384]{1,0:T(8,128)(2,1)} async-done(((bf16[3152,384]{1,0:T(8,128)(2,1)}), bf16[6304,384]{1,0:T(8,128)(2,1)}) %all-gather.11.cloned.1.call-update) | async-done | bytes 4841488 | tf_op jit(solution)/shard_map/all_gather | solution.py:270
  585.6 10.7 %reshape.154 = bf16[8,4,197,3,64]{2,1,0,4,3:T(4,128)(2,1)} reshape(bf16[6304,192]{0,1:T(8,128)(2,1)S(1)} %convolution_convert_fusion.2) | data formatting | bytes 4841472 | tf_op jit(solution)/shard_map/reshape | solution.py:186
  596.3 125.0 %while.27 = (s32[]{:T(128)}, f32[8,4,197,3,64]{2,4,3,1,0:T(8,128)}, bf16[8,4,197,3,64]{2,4,3,1,0:T(8,128)(2,1)}, f32[8,4,197,3,64]{2,4,3,1,0:T(8,128)}, bf16[8,4...) while((s32[]{:T(128)}, f32[8,4,197,3,64]{2,4,3,1,0:T(8,128)}, ...), condition=%wide.region_15.16_spmd, body=%wide.region_13.15_spmd.sunk | while | flops 304112448 | bytes 30816604 | solution.py:272
  721.3 11.7 %fusion.92 = (f32[3,64]{1,0:T(4,128)}, bf16[8,4,197,3,64]{2,4,3,1,0:T(8,128)(2,1)S(1)}, bf16[8,4,197,3,64]{2,4,3,1,0:T(8,128)(2,1)}, f32[3,64]{1,0:T(4,128)}) fusion(f32[8,4,197,3,64]{2,4,3,1,0:T(8,128)} %get-tuple-element.103, f32[8,4,197,3,64]{2,4,3,1,0:T(8,128)} %get-tuple-element.101), kind=kLoop, calls=%fused_computation.135 | loop fusion | flops 4841088 | bytes 14525952 | tf_op jit(solution)/shard_map/reduce_sum | solution.py:322
  778.7 10.0 %convolution_convert_fusion.4 = bf16[768,384]{0,1:T(8,128)(2,1)} fusion(bf16[6304,768]{1,0:T(8,128)(2,1)} %get-tuple-element.222, bf16[6304,384]{1,0:T(8,128)(2,1)} %all-gather.9.cloned.1.call-done), kind=kOutput, calls=%fused_computation.112 | convolution fusion | flops 3718545408 | bytes 15114240 | tf_op jit(solution)/shard_map/dot_general | solution.py:71
  795.7 10.1 %fusion.86 = bf16[384,768]{1,0:T(8,128)(2,1)} fusion(bf16[6304,384]{1,0:T(8,128)(2,1)} %all-gather.7.cloned.1.call-done, bf16[6304,768]{1,0:T(8,128)(2,1)} %copy-done.28), kind=kOutput, calls=%fused_computation.111 | convolution fusion | flops 3718545408 | bytes 15114240 | tf_op jit(solution)/shard_map/dot_general | solution.py:71
  869.4 39.5 %all-reduce.18 = (f32[384]{0:T(512)S(1)}, f32[384]{0:T(512)S(1)}, f32[384]{0:T(512)S(1)}, f32[384]{0:T(512)S(1)}, f32[384]{0:T(512)S(1)}, /*index=5*/f32[384]{0:...) all-reduce(f32[384]{0:T(512)S(1)} %get-tuple-element.151, ...), channel_id=6, replica_groups=mesh['dp'=16,'mp'=2] {'dp','mp'}, use_global_device_ids=true, to_apply=%region_24.25.clone | all-reduce | flops 4608 | bytes 36864
  (282 shorter events, 397.1 us)
Async XLA Ops:
  7.2 94.8 %copy-start.2 = (bf16[3152,384]{1,0:T(8,128)(2,1)S(1)}, bf16[3152,384]{1,0:T(8,128)(2,1)}, u32[]{:S(2)}) copy-start(bf16[3152,384]{1,0:T(8,128)(2,1)} %param.21) | copy-start | bytes 7262212
  7.2 248.0 %all-gather.5.cloned.1.call-start = ((), (), s32[]{:S(2)}) async-start(), calls=%async_computation.8 | async-start | bytes 7262208 | tf_op jit(solution)/shard_map/all_gather | solution.py:191
  98.4 42.9 %copy-start.22 = (bf16[24,192]{1,0:T(8,128)(2,1)S(1)}, bf16[24,192]{1,0:T(8,128)(2,1)}, u32[]{:S(2)}) copy-start(bf16[24,192]{1,0:T(8,128)(2,1)} %param.23) | copy-start | bytes 27652
  98.4 81.6 %copy-start.23 = (bf16[24,192]{1,0:T(8,128)(2,1)S(1)}, bf16[24,192]{1,0:T(8,128)(2,1)}, u32[]{:S(2)}) copy-start(bf16[24,192]{1,0:T(8,128)(2,1)} %param.24) | copy-start | bytes 27652
  98.5 118.1 %copy-start.24 = (bf16[192,24]{0,1:T(8,128)(2,1)S(1)}, bf16[192,24]{0,1:T(8,128)(2,1)}, u32[]{:S(2)}) copy-start(bf16[192,24]{0,1:T(8,128)(2,1)} %param.25) | copy-start | bytes 27652
  104.7 286.0 %reduce-scatter.5.cloned.1.call-start = ((), (), s32[]{:S(2)}) async-start(), calls=%async_computation.9 | async-start | bytes 14524416 | tf_op jit(solution)/shard_map/reduce_scatter | solution.py:206
  141.3 119.6 %copy-start.9 = (bf16[384,192]{1,0:T(8,128)(2,1)}, bf16[384,192]{1,0:T(8,128)(2,1)S(1)}, u32[]{:S(2)}) copy-start(bf16[384,192]{1,0:T(8,128)(2,1)S(1)} %all_gather.70) | copy-start | bytes 442372
  216.6 62.2 %copy-start.7 = (bf16[384,192]{1,0:T(8,128)(2,1)}, bf16[384,192]{1,0:T(8,128)(2,1)S(1)}, u32[]{:S(2)}) copy-start(bf16[384,192]{1,0:T(8,128)(2,1)S(1)} %all_gather.68) | copy-start | bytes 442372
  376.1 105.9 %all-gather.7.cloned.1.call-start = ((), (), s32[]{:S(2)}) async-start(), calls=%async_computation.10 | async-start | bytes 7262208 | tf_op jit(solution)/shard_map/all_gather | solution.py:215
  396.0 47.0 %copy-start.17 = (bf16[768,24]{0,1:T(8,128)(2,1)S(1)}, bf16[768,24]{0,1:T(8,128)(2,1)}, u32[]{:S(2)}) copy-start(bf16[768,24]{0,1:T(8,128)(2,1)} %param.27) | copy-start | bytes 110596
  399.0 95.9 %all-gather.9.cloned.1.call-start = ((), (), s32[]{:S(2)}) async-start(), calls=%async_computation.12 | async-start | bytes 7262208 | tf_op jit(solution)/shard_map/all_gather | solution.py:261
  399.6 137.5 %reduce-scatter.9.cloned.1.call-start = ((), (), s32[]{:S(2)}) async-start(), calls=%async_computation.13 | async-start | bytes 14524416 | tf_op jit(solution)/shard_map/reduce_scatter | solution.py:265
  520.2 32.1 %reduce-scatter.7.cloned.1.call-start = ((), (), s32[]{:S(2)}) async-start(), calls=%async_computation.11 | async-start | bytes 7262208 | tf_op jit(solution)/shard_map/reduce_scatter | solution.py:218
  529.5 51.9 %all-gather.11.cloned.1.call-start = ((), (), s32[]{:S(2)}) async-start(), calls=%async_computation.14 | async-start | bytes 7262208 | tf_op jit(solution)/shard_map/all_gather | solution.py:270
  529.5 22.8 %copy-start.6 = (bf16[3152,384]{1,0:T(8,128)(2,1)S(1)}, bf16[3152,384]{1,0:T(8,128)(2,1)}, u32[]{:S(2)}) copy-start(bf16[3152,384]{1,0:T(8,128)(2,1)} %param.37) | copy-start | bytes 7262212
  565.5 299.8 %reduce-scatter.11.cloned.1.call-start = ((), (), s32[]{:S(2)}) async-start(), calls=%async_computation.15 | async-start | bytes 7262208 | tf_op jit(solution)/shard_map/reduce_scatter | solution.py:282
  788.7 23.6 %all-to-all-start.3 = ((bf16[16,768,24]{1,2,0:T(8,128)(2,1)}), bf16[16,768,24]{1,2,0:T(8,128)(2,1)S(1)}, u32[]{:S(2)}, u32[]{:S(2)}) async-start(bf16[16,768,24]{1,2,0:T(8,128)(2,1)} %bitcast.151), calls=%async_computation.7 | async-start | bytes 1179648 | tf_op jit(solution)/shard_map/all_to_all | solution.py:28
  812.3 19.8 %all-to-all-start.2 = ((bf16[16,24,768]{2,1,0:T(8,128)(2,1)}), bf16[16,24,768]{2,1,0:T(8,128)(2,1)}, u32[]{:S(2)}, u32[]{:S(2)}) async-start(bf16[16,24,768]{2,1,0:T(8,128)(2,1)} %bitcast.150), calls=%async_computation.6 | async-start | bytes 1179648 | tf_op jit(solution)/shard_map/all_to_all | solution.py:28
  832.1 14.1 %all-to-all-start.1 = ((bf16[16,192,24]{1,2,0:T(8,128)(2,1)}), bf16[16,192,24]{1,2,0:T(8,128)(2,1)}, u32[]{:S(2)}, u32[]{:S(2)}) async-start(bf16[16,192,24]{1,2,0:T(8,128)(2,1)} %bitcast.21), calls=%async_computation.5 | async-start | bytes 393216 | tf_op jit(solution)/shard_map/all_to_all | solution.py:28
  838.1 16.8 %copy-start.25 = (f32[3,64]{1,0:T(4,128)S(1)}, f32[3,64]{1,0:T(4,128)}, u32[]{:S(2)}) copy-start(f32[3,64]{1,0:T(4,128)} %get-tuple-element.227) | copy-start | bytes 2308
  838.1 27.2 %copy-start.3 = (bf16[3152,384]{1,0:T(8,128)(2,1)S(1)}, bf16[3152,384]{1,0:T(8,128)(2,1)}, u32[]{:S(2)}) copy-start(bf16[3152,384]{1,0:T(8,128)(2,1)} %param.21) | copy-start | bytes 7262212
  838.1 27.2 %copy-start.12 = (f32[3152]{0:T(1024)S(1)}, f32[3152]{0:T(1024)}, u32[]{:S(2)}) copy-start(f32[3152]{0:T(1024)} %copy-done.11) | copy-start | bytes 37828
  838.1 27.2 %copy-start.14 = (f32[3152]{0:T(1024)S(1)}, f32[3152]{0:T(1024)}, u32[]{:S(2)}) copy-start(f32[3152]{0:T(1024)} %copy-done.13) | copy-start | bytes 37828
  846.2 18.3 %all-to-all-start = ((bf16[16,24,576]{2,1,0:T(8,128)(2,1)}), bf16[16,24,576]{2,1,0:T(8,128)(2,1)S(1)}, u32[]{:S(2)}, u32[]{:S(2)}) async-start(bf16[16,24,576]{2,1,0:T(8,128)(2,1)} %bitcast.19), calls=%async_computation.4 | async-start | bytes 983040 | tf_op jit(solution)/shard_map/all_to_all | solution.py:28
  (17 other events, 98.2 us)
Sparse Core Ops, SparseCore 0:
  104.8 10.4 all-gather.4
  376.2 14.4 reduce-scatter.4
  399.1 14.7 all-gather.6
  415.3 15.7 all-gather.8
  520.3 16.7 reduce-scatter.8
  539.2 13.0 reduce-scatter.6
  565.6 15.6 all-gather.10
  778.8 14.1 reduce-scatter.10
where the time goes:
time: 937 us; the launch traced here: 928 us
  blocking collectives  351 us (37%)
  matrix products  260 us (28%)
  local copies, waits for them, and re-layouts  147 us (16%)
  other arithmetic  66.7 us (7%)
  waiting for transfers between devices  63.5 us (7%)
  starting transfers between devices  23.3 us (2%)
  between operations  16.4 us (2%)
    unnamed x2, blocking collectives  118 us
    reshape x4, local copies, waits for them, and re-layouts, view(): return rows.reshape(blocks, IMG_BLK, S, heads_local, HD)  47.9 us
    all_gather x1, blocking collectives, on_device(): lax.all_gather(w_up, 'dp', axis=0, tiled=True)  43.3 us
    all_gather x1, blocking collectives, on_device(): lax.all_gather(w_down, 'dp', axis=1, tiled=True)  38.9 us
    all_gather x1, blocking collectives, on_device(): lax.all_gather(w_key, 'dp', axis=0, tiled=True)  38.7 us
    all_gather x1, blocking collectives, on_device(): lax.all_gather(w_out, 'dp', axis=1, tiled=True)  38.5 us
    dot_general x6, matrix products, dot_lead(): lax.dot_general(left, right, (((0,), (0,)), ((), ())), preferred_element_...  38.4 us
    all_gather x1, blocking collectives, on_device(): lax.all_gather(w_query, 'dp', axis=0, tiled=True)  36.5 us
  transfers between devices with their start and end apart: 12, of which 8 were waited for; matrix products, arithmetic and copies ran while one was open for 8% of the time, Pallas kernels for 0%

commit v1 on v0

v1 whole, which is shorter than its diff:
```python
import functools
import math

import jax
import jax.numpy as jnp
from jax import lax
from jax.experimental import pallas as pl
from jax.experimental.pallas import tpu as pltpu
from jax.sharding import PartitionSpec as P

D = 384
HD = 64
FF = 1536
S = 197
HEADS = D // HD
PAIRS = HEADS // 2

SP = 208
WIN = 224

EPS = 1e-06
RSQRT2 = 0.7071067811865476
RSQRT_TAU = 0.3989422804014327
LOG2E = 1.4426950408889634
Q_SCALE = LOG2E / math.sqrt(HD)
BF = jnp.bfloat16
F32 = jnp.float32


def dot_nn(a, b):
    return lax.dot_general(a, b, (((1,), (0,)), ((), ())), preferred_element_type=F32)


def dot_nt(a, b):
    return lax.dot_general(a, b, (((1,), (1,)), ((), ())), preferred_element_type=F32)


def dot_tn(a, b):
    return lax.dot_general(a, b, (((0,), (0,)), ((), ())), preferred_element_type=F32)


def window_of(i, rows):
    start = i * S
    base = jnp.minimum((start // 16) * 16, rows - WIN)
    return pl.multiple_of(base, 16), start - base


def load_image(ref, i):
    base, off = window_of(i, ref.shape[0])
    rows = ref[pl.ds(base, WIN), :].astype(F32)
    rows = pltpu.roll(rows, WIN - off, axis=0)[:SP]
    live = lax.broadcasted_iota(jnp.int32, rows.shape, 0) < S
    return jnp.where(live, rows, 0.0)


def store_image(ref, i, rows):
    base, off = window_of(i, ref.shape[0])
    rows = jnp.concatenate([rows, jnp.zeros((WIN - SP, rows.shape[1]), F32)], axis=0)
    rows = pltpu.roll(rows, off, axis=0)
    old = ref[pl.ds(base, WIN), :].astype(F32)
    mine = lax.broadcasted_iota(jnp.int32, rows.shape, 0) >= off
    ref[pl.ds(base, WIN), :] = jnp.where(mine, rows, old).astype(ref.dtype)


def norm_stats(x):
    mean = jnp.mean(x, axis=-1, keepdims=True)
    centred = x - mean
    inv = lax.rsqrt(jnp.mean(centred * centred, axis=-1, keepdims=True) + EPS)
    return centred * inv, inv


def norm_backward(grad, normed, inv, gain):
    e = grad * gain
    return inv * (
        e
        - jnp.mean(e, axis=-1, keepdims=True)
        - normed * jnp.mean(e * normed, axis=-1, keepdims=True)
    )


def row_sum(x):
    return jnp.sum(x, axis=0, keepdims=True)


def attn_fwd_kernel(tok_ref, w_ref, vec_ref, qkv_ref, e_ref, mixed_ref, linv_ref):
    i = pl.program_id(0)
    x = load_image(tok_ref, i)
    normed, _ = norm_stats(x)
    h1 = (normed * vec_ref[0:1, :] + vec_ref[1:2, :]).astype(BF)
    q = ((dot_nn(h1, w_ref[:, 0:D]) + vec_ref[2:3, :]) * Q_SCALE).astype(BF)
    k = dot_nn(h1, w_ref[:, D : 2 * D]).astype(BF)
    v = (dot_nn(h1, w_ref[:, 2 * D :]) + vec_ref[3:4, :]).astype(BF)
    qkv_ref[0, :, 0:D] = q
    qkv_ref[0, :, D : 2 * D] = k
    qkv_ref[0, :, 2 * D :] = v
    lane = lax.broadcasted_iota(jnp.int32, (SP, 2 * HD), 1)
    is_key = lax.broadcasted_iota(jnp.int32, (SP, SP), 1) < S
    zero = jnp.zeros((SP, 2 * HD), BF)
    one = jnp.ones((SP, 2 * HD), BF)
    for p in range(PAIRS):
        cols = slice(2 * HD * p, 2 * HD * (p + 1))
        total = None
        for h in range(2):
            own = (lane < HD) if h == 0 else (lane >= HD)
            kh = jnp.where(own, k[:, cols], zero)
            vh = jnp.where(own, v[:, cols], zero)
            scores = dot_nt(q[:, cols], kh)
            scores = jnp.where(is_key, scores, -1e30)
            top = jnp.max(scores, axis=-1, keepdims=True)
            e = jnp.exp2(scores - top).astype(BF)
            e_ref[0, 2 * p + h] = e
            part = dot_nn(e, jnp.concatenate([vh, jnp.where(own, one, zero)], axis=1))
            total = part if total is None else total + part
        linv = 1.0 / total[:, 2 * HD :]
        linv_ref[0, :, cols] = linv
        mixed_ref[0, :, cols] = (total[:, : 2 * HD] * linv).astype(BF)


def mlp_kernel(
    tok_ref, cot_ref, mixed_ref, wot_ref, wup_ref, wdt_ref, vec_ref, bup_ref,
    out_ref, gres_ref, gmix_ref, dwot_ref, dwup_ref, dwdt_ref, dvec_ref, dbup_ref,
    act_ref, gp_ref,
):
    i = pl.program_id(0)

    @pl.when(i == 0)
    def _():
        dwot_ref[...] = jnp.zeros_like(dwot_ref)
        dwup_ref[...] = jnp.zeros_like(dwup_ref)
        dwdt_ref[...] = jnp.zeros_like(dwdt_ref)
        dvec_ref[...] = jnp.zeros_like(dvec_ref)
        dbup_ref[...] = jnp.zeros_like(dbup_ref)

    mixed = mixed_ref[0]
    cot_f = load_image(cot_ref, i)
    cot = cot_f.astype(BF)
    resid = load_image(tok_ref, i) + dot_nt(mixed, wot_ref[...]) + vec_ref[4:5, :]
    normed, inv = norm_stats(resid)
    h2 = (normed * vec_ref[5:6, :] + vec_ref[6:7, :]).astype(BF)
    step = 256
    for j in range(FF // step):
        cols = slice(step * j, step * (j + 1))
        u = dot_nn(h2, wup_ref[:, cols]) + bup_ref[:, cols]
        ga = dot_nn(cot, wdt_ref[:, cols])
        cdf = 0.5 * (1.0 + lax.erf(u * RSQRT2))
        act_ref[:, cols] = (u * cdf).astype(BF)
        gp = ga * (cdf + u * jnp.exp(-0.5 * u * u) * RSQRT_TAU)
        dbup_ref[:, cols] += row_sum(gp)
        gp_ref[:, cols] = gp.astype(BF)
    out = resid + dot_nt(act_ref[...], wdt_ref[...]) + vec_ref[7:8, :]
    store_image(out_ref, i, out)
    gh2 = dot_nt(gp_ref[...], wup_ref[...])
    gres = cot_f + norm_backward(gh2, normed, inv, vec_ref[5:6, :])
    gres_ref[0] = gres
    gr = gres.astype(BF)
    gmix_ref[0] = dot_nn(gr, wot_ref[...]).astype(BF)
    dwot_ref[...] += dot_tn(gr, mixed)
    dwup_ref[...] += dot_tn(h2, gp_ref[...])
    dwdt_ref[...] += dot_tn(cot, act_ref[...])
    dvec_ref[0:1, :] += row_sum(gres)
    dvec_ref[1:2, :] += row_sum(gh2 * normed)
    dvec_ref[2:3, :] += row_sum(gh2)
    dvec_ref[3:4, :] += row_sum(cot_f)


def attn_bwd_kernel(
    tok_ref, qkv_ref, e_ref, mixed_ref, linv_ref, gmix_ref, gres_ref, w_ref, vec_ref,
    gtok_ref, dw_ref, dvec_ref, g_ref,
):
    i = pl.program_id(0)

    @pl.when(i == 0)
    def _():
        dw_ref[...] = jnp.zeros_like(dw_ref)
        dvec_ref[...] = jnp.zeros_like(dvec_ref)

    lane = lax.broadcasted_iota(jnp.int32, (SP, 2 * HD), 1)
    zero = jnp.zeros((SP, 2 * HD), BF)
    minus = jnp.full((SP, 2 * HD), -1.0, BF)
    for p in range(PAIRS):
        lo, hi = 2 * HD * p, 2 * HD * (p + 1)
        q = qkv_ref[0, :, lo:hi]
        k = qkv_ref[0, :, D + lo : D + hi]
        v = qkv_ref[0, :, 2 * D + lo : 2 * D + hi]
        go_f = gmix_ref[0, :, lo:hi].astype(F32) * linv_ref[0, :, lo:hi]
        go = go_f.astype(BF)
        god = jnp.concatenate(
            [go, (go_f * mixed_ref[0, :, lo:hi].astype(F32)).astype(BF)], axis=1
        )
        gq = gk = gv = None
        for h in range(2):
            own = (lane < HD) if h == 0 else (lane >= HD)
            e = e_ref[0, 2 * p + h]
            vd = jnp.concatenate(
                [jnp.where(own, v, zero), jnp.where(own, minus, zero)], axis=1
            )
            ds = e * dot_nt(god, vd).astype(BF)
            part_q = dot_nn(ds, jnp.where(own, k, zero))
            part_k = dot_tn(ds, jnp.where(own, q, zero))
            part_v = dot_tn(e, jnp.where(own, go, zero))
            gq = part_q if gq is None else gq + part_q
            gk = part_k if gk is None else gk + part_k
            gv = part_v if gv is None else gv + part_v
        gq = gq * (1.0 / math.sqrt(HD))
        dvec_ref[0:1, lo:hi] += row_sum(gq)
        dvec_ref[1:2, lo:hi] += row_sum(gv)
        g_ref[:, lo:hi] = gq.astype(BF)
        g_ref[:, D + lo : D + hi] = (gk * (1.0 / LOG2E)).astype(BF)
        g_ref[:, 2 * D + lo : 2 * D + hi] = gv.astype(BF)
    normed, inv = norm_stats(load_image(tok_ref, i))
    h1 = (normed * vec_ref[0:1, :] + vec_ref[1:2, :]).astype(BF)
    dw_ref[...] += dot_tn(h1, g_ref[...])
    gh1 = dot_nt(g_ref[...], w_ref[...])
    gtok = gres_ref[0] + norm_backward(gh1, normed, inv, vec_ref[0:1, :])
    store_image(gtok_ref, i, gtok)
    dvec_ref[2:3, :] += row_sum(gh1 * normed)
    dvec_ref[3:4, :] += row_sum(gh1)


def whole(shape):
    return pl.BlockSpec(shape, lambda i: (0,) * len(shape))


def per_image(*shape):
    return pl.BlockSpec((1, *shape), lambda i: (i,) + (0,) * len(shape))


def params():
    return pltpu.CompilerParams(
        dimension_semantics=("arbitrary",), vmem_limit_bytes=62 * 1024 * 1024
    )


def attn_fwd(tokens, wqkv, vec):
    rows = tokens.shape[0]
    n = rows // S
    return pl.pallas_call(
        attn_fwd_kernel,
        grid=(n,),
        in_specs=[whole((rows, D)), whole((D, 3 * D)), whole((8, D))],
        out_specs=[
            per_image(SP, 3 * D), per_image(HEADS, SP, SP), per_image(SP, D), per_image(SP, D),
        ],
        out_shape=[
            jax.ShapeDtypeStruct((n, SP, 3 * D), BF),
            jax.ShapeDtypeStruct((n, HEADS, SP, SP), BF),
            jax.ShapeDtypeStruct((n, SP, D), BF),
            jax.ShapeDtypeStruct((n, SP, D), F32),
        ],
        compiler_params=params(),
        name="attn_fwd",
    )(tokens, wqkv, vec)


def mlp(tokens, cot, mixed, wot, wup, wdt, vec, bup):
    rows = tokens.shape[0]
    n = rows // S
    return pl.pallas_call(
        mlp_kernel,
        grid=(n,),
        in_specs=[
            whole((rows, D)), whole((rows, D)), per_image(SP, D), whole((D, D)), whole((D, FF)),
            whole((D, FF)), whole((8, D)), whole((1, FF)),
        ],
        out_specs=[
            whole((rows, D)), per_image(SP, D), per_image(SP, D), whole((D, D)), whole((D, FF)),
            whole((D, FF)), whole((8, D)), whole((1, FF)),
        ],
        out_shape=[
            jax.ShapeDtypeStruct((rows, D), BF),
            jax.ShapeDtypeStruct((n, SP, D), F32),
            jax.ShapeDtypeStruct((n, SP, D), BF),
            jax.ShapeDtypeStruct((D, D), F32),
            jax.ShapeDtypeStruct((D, FF), F32),
            jax.ShapeDtypeStruct((D, FF), F32),
            jax.ShapeDtypeStruct((8, D), F32),
            jax.ShapeDtypeStruct((1, FF), F32),
        ],
        scratch_shapes=[pltpu.VMEM((SP, FF), BF), pltpu.VMEM((SP, FF), BF)],
        compiler_params=params(),
        name="mlp",
    )(tokens, cot, mixed, wot, wup, wdt, vec, bup)


def attn_bwd(tokens, qkv, e, mixed, linv, gmix, gres, wqkv, vec):
    rows = tokens.shape[0]
    n = rows // S
    return pl.pallas_call(
        attn_bwd_kernel,
        grid=(n,),
        in_specs=[
            whole((rows, D)), per_image(SP, 3 * D), per_image(HEADS, SP, SP), per_image(SP, D),
            per_image(SP, D), per_image(SP, D), per_image(SP, D), whole((D, 3 * D)), whole((8, D)),
        ],
        out_specs=[whole((rows, D)), whole((D, 3 * D)), whole((8, D))],
        out_shape=[
            jax.ShapeDtypeStruct((rows, D), F32),
            jax.ShapeDtypeStruct((D, 3 * D), F32),
            jax.ShapeDtypeStruct((8, D), F32),
        ],
        scratch_shapes=[pltpu.VMEM((SP, 3 * D), BF)],
        compiler_params=params(),
        name="attn_bwd",
    )(tokens, qkv, e, mixed, linv, gmix, gres, wqkv, vec)


PARTS = (D // 2, D // 2, D // 2, D // 2, FF // 2, FF // 2)
WIDE = sum(PARTS)
CUT = WIDE // 2
MESH = pl.DeviceIdType.MESH


def chip_grid(dp):
    side = math.isqrt(dp // 4)
    return 4, side, side


class Mover:
    def __init__(self, send, recv):
        self.send, self.recv, self.used = send, recv, 0

    def start(self, src, dst, device):
        copy = pltpu.make_async_remote_copy(
            src_ref=src, dst_ref=dst, send_sem=self.send.at[self.used],
            recv_sem=self.recv.at[self.used], device_id=device, device_id_type=MESH,
        )
        copy.start()
        self.used += 1
        return copy


def place_of(dims):
    _, ny, nx = dims
    dp, mp = lax.axis_index("dp"), lax.axis_index("mp")
    return dp // (ny * nx), (dp // nx) % ny, dp % nx, mp


def peers_of(dims, place):
    (nz, ny, nx), (z, y, x, mp) = dims, place

    def at(a, b, c, m):
        return ((a * ny + b) * nx + c, m)

    along = {
        "z": [((z + o) % nz, at((z + o) % nz, y, x, mp)) for o in range(1, nz)],
        "y": [((y + o) % ny, at(z, (y + o) % ny, x, mp)) for o in range(1, ny)],
        "x": [((x + o) % nx, at(z, y, (x + o) % nx, mp)) for o in range(1, nx)],
    }
    return along, at(z, y, x, 1 - mp)


def meet(along, other):
    barrier = pltpu.get_barrier_semaphore()
    devices = [d for peers in along.values() for _, d in peers] + [other]
    for device in devices:
        pl.semaphore_signal(barrier, inc=1, device_id=device, device_id_type=MESH)
    pl.semaphore_wait(barrier, len(devices))


def gather_kernel(dims, *refs):
    (wq, wk, wv, wo, wu, wd), vectors, bup = refs[:6], refs[6:14], refs[14]
    wqkv_ref, wot_ref, wup_ref, wdt_ref, vec_ref, bup_ref = refs[15:21]
    w, v, send, recv = refs[21:]
    nz, ny, nx = dims
    place = place_of(dims)
    z, y, x, mp = place
    rows = w.shape[4]
    along, other = peers_of(dims, place)
    w[z, y, x, mp] = jnp.concatenate(
        [wq[...], wk[...], wv[...], wo[...].astype(F32).T.astype(BF), wu[...],
         wd[...].astype(F32).T.astype(BF)],
        axis=1,
    )
    for j, vector in enumerate(vectors):
        v[z, y, x, j : j + 1, :rows] = vector[...].astype(F32)
    v[z, y, x, 8:9, : bup.shape[1]] = bup[...].astype(F32)
    meet(along, other)

    mover = Mover(send, recv)
    low, high = pl.ds(0, CUT), pl.ds(CUT, WIDE - CUT)
    sent = []

    def spread(buffer, index, axis):
        return [mover.start(buffer.at[index], buffer.at[index], d) for _, d in along[axis]]

    def share(index):
        sent.append(mover.start(w.at[index], w.at[index], other))
        return sent[-1]

    def arrived(copies):
        for c in copies:
            c.wait_recv()
        sent.extend(copies)

    every = slice(None)
    first = spread(w, (z, y, x, mp), "z") + spread(v, (z, y, x), "z")
    arrived(first)
    shared = [share((every, y, x, mp))]
    second_low = spread(w, (every, y, x, mp, every, low), "y") + spread(v, (every, y, x), "y")
    second_high = spread(w, (every, y, x, mp, every, high), "x")
    arrived(second_low)
    third_low = spread(w, (every, every, x, mp, every, low), "x") + spread(
        v, (every, every, x), "x"
    )
    arrived(second_high)
    third_high = spread(w, (every, y, every, mp, every, high), "y")
    for b, _ in along["y"]:
        shared.append(share((every, b, x, mp, every, low)))
    for c, _ in along["x"]:
        shared.append(share((every, y, c, mp, every, high)))
    arrived(third_low)
    for c, _ in along["x"]:
        shared.append(share((every, every, c, mp, every, low)))
    arrived(third_high)
    for b, _ in along["y"]:
        shared.append(share((every, b, every, mp, every, high)))

    n = nz * ny * nx
    spots = [(a, b, c) for a in range(nz) for b in range(ny) for c in range(nx)]
    vec_ref[...] = jnp.concatenate([v[s][0:8, :rows] for s in spots], axis=1)
    bup_ref[...] = jnp.concatenate([v[s][8:9, : bup.shape[1]] for s in spots], axis=1)
    for c in shared:
        c.wait_recv()

    group = 48 // rows
    ends = [sum(PARTS[: i + 1]) for i in range(len(PARTS))]
    for t in range(n // group):
        block = [
            jnp.concatenate(
                [w[s + (m,)].astype(F32) for s in spots[t * group : (t + 1) * group]], axis=0
            )
            for m in range(2)
        ]
        at = pl.ds(48 * t, 48)

        def both(i):
            lo, hi = ends[i] - PARTS[i], ends[i]
            return jnp.concatenate([half[:, lo:hi] for half in block], axis=1).astype(BF)

        for i in range(3):
            wqkv_ref[at, D * i : D * (i + 1)] = both(i)
        wot_ref[at, :] = both(3)
        wup_ref[at, :] = both(4)
        wdt_ref[at, :] = both(5)
    for c in sent:
        c.wait_send()


def gather(mats, vectors, bup, dp):
    dims = chip_grid(dp)
    nz, ny, nx = dims
    rows = D // dp
    copies = 2 * (nz + ny + nx) + 3 * (ny + nx) + 2
    vmem = pl.BlockSpec(memory_space=pltpu.VMEM)
    return pl.pallas_call(
        functools.partial(gather_kernel, dims),
        in_specs=[vmem] * 15,
        out_specs=[vmem] * 6,
        out_shape=[
            jax.ShapeDtypeStruct((D, 3 * D), BF),
            jax.ShapeDtypeStruct((D, D), BF),
            jax.ShapeDtypeStruct((D, FF), BF),
            jax.ShapeDtypeStruct((D, FF), BF),
            jax.ShapeDtypeStruct((8, D), F32),
            jax.ShapeDtypeStruct((1, FF), F32),
        ],
        scratch_shapes=[
            pltpu.VMEM((nz, ny, nx, 2, rows, WIDE), BF),
            pltpu.VMEM((nz, ny, nx, 16, 128), F32),
            pltpu.SemaphoreType.DMA((copies,)),
            pltpu.SemaphoreType.DMA((copies,)),
        ],
        compiler_params=pltpu.CompilerParams(
            collective_id=0, has_side_effects=True, vmem_limit_bytes=62 * 1024 * 1024
        ),
        name="gather",
    )(*mats, *vectors, bup)


def reduce_kernel(
    dims, dqkv, dwot, dwup, dwdt, dvec1, dvec2, dbup, out_ref, vec_ref,
    s, p, a1, b1, a2, b2, ra1, rb1, ra2, rb2, rz, f, vs, vr, send, recv,
):
    nz, ny, nx = dims
    place = place_of(dims)
    z, y, x, mp = place
    rows = s.shape[4]
    along, other = peers_of(dims, place)
    spots = [(i, j, k) for i in range(nz) for j in range(ny) for k in range(nx)]
    group = 48 // rows
    for t in range(len(spots) // group):
        at = pl.ds(48 * t, 48)
        for m in range(2):
            parts = [dqkv[at, D * i : D * (i + 1)] for i in range(3)]
            parts += [dwot[at, :], dwup[at, :], dwdt[at, :]]
            block = jnp.concatenate(
                [q[:, m * n : (m + 1) * n] for q, n in zip(parts, PARTS)], axis=1
            )
            for g in range(group):
                s[(m,) + spots[t * group + g]] = block[g * rows : (g + 1) * rows].astype(BF)
    vs[0, 0:4] = dvec1[0:4]
    vs[0, 4:8] = dvec2[0:4]
    for j in range(FF // D):
        vs[0, 8 + j : 9 + j] = dbup[:, D * j : D * (j + 1)]
    vs[0, 12:16] = jnp.zeros((4, D), F32)
    meet(along, other)

    mover = Mover(send, recv)
    sent = []

    def arrived(copies):
        for c in copies:
            c.wait_recv()
        sent.extend(copies)

    def vec_send(stage, devices, base):
        return [
            mover.start(vs.at[stage], vr.at[base + i], d) for i, d in enumerate(devices)
        ]

    def vec_add(stage, base, n):
        total = vs[stage]
        for i in range(n):
            total = total + vr[base + i]
        if stage < 3:
            vs[stage + 1] = total
        else:
            vec_ref[...] = total

    pair = [mover.start(s.at[1 - mp], p, other)] + vec_send(0, [other], 0)
    arrived(pair)
    for i in range(nz):
        for j in range(ny):
            for k in range(nx):
                p[i, j, k] = (s[mp, i, j, k].astype(F32) + p[i, j, k].astype(F32)).astype(BF)
    vec_add(0, 0, 1)

    every = slice(None)
    low, high = pl.ds(0, CUT), pl.ds(CUT, WIDE - CUT)
    first_low = [
        mover.start(p.at[every, every, c, every, low], ra1.at[o], d)
        for o, (c, d) in enumerate(along["x"])
    ] + vec_send(1, [d for _, d in along["x"]], 1)
    first_high = [
        mover.start(p.at[every, b, every, every, high], rb1.at[o], d)
        for o, (b, d) in enumerate(along["y"])
    ]
    arrived(first_low)
    for i in range(nz):
        for j in range(ny):
            total = p[i, j, x, :, :CUT].astype(F32)
            for o in range(nx - 1):
                total = total + ra1[o, i, j].astype(F32)
            a1[i, j] = total.astype(BF)
    vec_add(1, 1, nx - 1)
    second_low = [
        mover.start(a1.at[every, b], ra2.at[o], d) for o, (b, d) in enumerate(along["y"])
    ] + vec_send(2, [d for _, d in along["y"]], nx)
    arrived(first_high)
    for i in range(nz):
        for k in range(nx):
            total = p[i, y, k, :, CUT:].astype(F32)
            for o in range(ny - 1):
                total = total + rb1[o, i, k].astype(F32)
            b1[i, k] = total.astype(BF)
    second_high = [
        mover.start(b1.at[every, c], rb2.at[o], d) for o, (c, d) in enumerate(along["x"])
    ]
    arrived(second_low)
    for i in range(nz):
        total = a1[i, y].astype(F32)
        for o in range(ny - 1):
            total = total + ra2[o, i].astype(F32)
        f[i, :, :CUT] = total.astype(BF)
    vec_add(2, nx, ny - 1)
    arrived(second_high)
    for i in range(nz):
        total = b1[i, x].astype(F32)
        for o in range(nx - 1):
            total = total + rb2[o, i].astype(F32)
        f[i, :, CUT:] = total.astype(BF)
    third = [
        mover.start(f.at[a], rz.at[o], d) for o, (a, d) in enumerate(along["z"])
    ] + vec_send(3, [d for _, d in along["z"]], nx + ny - 1)
    arrived(third)
    total = f[z].astype(F32)
    for o in range(nz - 1):
        total = total + rz[o].astype(F32)
    out_ref[...] = total
    vec_add(3, nx + ny - 1, nz - 1)
    for c in sent:
        c.wait_send()


def reduce(dqkv, dwot, dwup, dwdt, dvec1, dvec2, dbup, dp):
    dims = chip_grid(dp)
    nz, ny, nx = dims
    rows = D // dp
    copies = 2 * (nz + ny + nx) + ny + nx
    vmem = pl.BlockSpec(memory_space=pltpu.VMEM)

    def buf(*shape):
        return pltpu.VMEM((*shape, rows, CUT), BF)

    return pl.pallas_call(
        functools.partial(reduce_kernel, dims),
        in_specs=[vmem] * 7,
        out_specs=[vmem] * 2,
        out_shape=[
            jax.ShapeDtypeStruct((rows, WIDE), F32),
            jax.ShapeDtypeStruct((16, D), F32),
        ],
        scratch_shapes=[
            pltpu.VMEM((2, nz, ny, nx, rows, WIDE), BF),
            pltpu.VMEM((nz, ny, nx, rows, WIDE), BF),
            buf(nz, ny), buf(nz, nx), buf(nz), buf(nz),
            buf(nx - 1, nz, ny), buf(ny - 1, nz, nx), buf(ny - 1, nz), buf(nx - 1, nz),
            pltpu.VMEM((nz - 1, rows, WIDE), BF),
            pltpu.VMEM((nz, rows, WIDE), BF),
            pltpu.VMEM((4, 16, D), F32),
            pltpu.VMEM((nz + ny + nx, 16, D), F32),
            pltpu.SemaphoreType.DMA((copies,)),
            pltpu.SemaphoreType.DMA((copies,)),
        ],
        compiler_params=pltpu.CompilerParams(
            collective_id=1, has_side_effects=True, vmem_limit_bytes=62 * 1024 * 1024
        ),
        name="reduce",
    )(dqkv, dwot, dwup, dwdt, dvec1, dvec2, dbup)


def split_kernel(n, mat_ref, vec_ref, *outs):
    at = 0
    for i, (width, out) in enumerate(zip(PARTS, outs)):
        part = mat_ref[:, at : at + width]
        out[...] = part.T if i in (3, 5) else part
        at += width
    index = lax.axis_index("dp") * 2 + lax.axis_index("mp")
    per = D // n
    vec = pltpu.roll(vec_ref[...], D - index * per, axis=1)
    for row, out in zip((2, 3, 0, 1, 4, 5, 6, 7), outs[6:]):
        out[...] = vec[row : row + 1, :per]
    wide = jnp.concatenate([vec_ref[8 + j : 9 + j, :] for j in range(FF // D)], axis=1)
    wide = pltpu.roll(jnp.broadcast_to(wide, (8, FF)), FF - index * (FF // n), axis=1)
    outs[14][...] = wide[0:1, : FF // n]


def split(mat, vec, n):
    rows = mat.shape[0]
    vmem = pl.BlockSpec(memory_space=pltpu.VMEM)
    shapes = [(w, rows) if i in (3, 5) else (rows, w) for i, w in enumerate(PARTS)]
    shapes += [(1, D // n)] * 8 + [(1, FF // n)]
    return pl.pallas_call(
        functools.partial(split_kernel, n),
        in_specs=[vmem] * 2,
        out_specs=[vmem] * 15,
        out_shape=[jax.ShapeDtypeStruct(s, F32) for s in shapes],
        name="split",
    )(mat, vec)


def on_device(
    tokens, w_query, w_key, w_value, w_out, w_up, w_down, ln1_gain, ln1_bias, b_query, b_value,
    b_out, ln2_gain, ln2_bias, b_up, b_down, cotangent,
):
    dp = lax.axis_size("dp")
    vectors = (ln1_gain, ln1_bias, b_query, b_value, b_out, ln2_gain, ln2_bias, b_down)
    wqkv, wot, wup, wdt, vec, bup = gather(
        (w_query, w_key, w_value, w_out, w_up, w_down), [v[None] for v in vectors], b_up[None], dp
    )
    qkv, e, mixed, linv = attn_fwd(tokens, wqkv, vec)
    out, gres, gmix, dwot, dwup, dwdt, dvec2, dbup = mlp(
        tokens, cotangent, mixed, wot, wup, wdt, vec, bup
    )
    gtok, dwqkv, dvec1 = attn_bwd(tokens, qkv, e, mixed, linv, gmix, gres, wqkv, vec)
    mat, sums = reduce(dwqkv, dwot, dwup, dwdt, dvec1, dvec2, dbup, dp)
    grads = split(mat, sums, dp * lax.axis_size("mp"))
    vecs = [g.reshape(-1) for g in grads[6:]]
    return (out, gtok, *grads[:6], *vecs[:7], vecs[8], vecs[7])


def solution(mesh):
    row, mat, tam, vec = P(("dp", "mp"), None), P("dp", "mp"), P("mp", "dp"), P("dp")
    part = P(("dp", "mp"))
    return jax.shard_map(
        on_device,
        mesh=mesh,
        in_specs=(row, mat, mat, mat, tam, mat, tam, *([vec] * 9), row),
        out_specs=(row, row, mat, mat, mat, tam, mat, tam, *([part] * 9)),
        check_vma=False,
    )
```

time: 937 us -> 217 us (0.23)
  blocking collectives: 351 us -> 0 us
  matrix products: 260 us -> 0 us
  Pallas kernels: 0 us -> 209 us
  local copies, waits for them, and re-layouts: 147 us -> 6.35 us
  other arithmetic: 66.7 us -> 0 us
  waiting for transfers between devices: 63.5 us -> 0 us
  starting transfers between devices: 23.3 us -> 0 us
  between operations: 16.4 us -> 0.68 us
    dot_general x74 -> x0, matrix products: 260 us -> none  [the longest x6 38.4 us: dot_lead(): lax.dot_general(left, right, (((0,), (0,)), ((), ())), preferred_element_...]
    all_gather x6 -> x0, blocking collectives: 233 us -> none  [the longest x1 43.3 us: on_device(): lax.all_gather(w_up, 'dp', axis=0, tiled=True)]
    pallas_call x0 -> x6, Pallas kernels: none -> 209 us  [the longest x1 58.2 us: mlp(): pl.pallas_call(mlp_kernel, grid=(n,), in_specs=[whole((rows, D)), whole((...]
    unnamed x2 -> x0, blocking collectives: 118 us -> none
    reshape x5 -> x0, local copies, waits for them, and re-layouts: 54.7 us -> none  [the longest x4 47.9 us: view(): return rows.reshape(blocks, IMG_BLK, S, heads_local, HD)]
    reduce_sum x20 -> x0, other arithmetic: 48.9 us -> none  [the longest x1 11.7 us: on_device(): jnp.sum(grad_value, axis=0)]
    convert_element_type x7 -> x0, local copies, waits for them, and re-layouts: 36.5 us -> none  [the longest x2 13 us: on_device(): query_grad_rows = grad_query.astype(jnp.bfloat16)]
    reduce_scatter x4 -> x0, waiting for transfers between devices: 30.6 us -> none  [the longest x1 14.6 us: on_device(): lax.psum_scatter(jnp.dot(mixed_rows, out_full, preferred_element_type=jnp...]
  transfers between devices with their start and end apart: 12 -> 0, of which waited for: 8 -> 0; matrix products, arithmetic and copies ran while one was open for 8% -> 0% of each run, Pallas kernels for 0% -> 0%
where the time goes in v1:
time: 217 us; the launch traced here: 216 us
  Pallas kernels  209 us (96%)
  local copies, waits for them, and re-layouts  6.35 us (3%)
    pallas_call x1, Pallas kernels, mlp(): pl.pallas_call(mlp_kernel, grid=(n,), in_specs=[whole((rows, D)), whole((...  58.2 us
    pallas_call x1, Pallas kernels, attn_bwd(): pl.pallas_call(attn_bwd_kernel, grid=(n,), in_specs=[whole((rows, D)), pe...  43.3 us
    pallas_call x1, Pallas kernels, reduce(): pl.pallas_call(functools.partial(reduce_kernel, dims), in_specs=[vmem] *...  41 us
    pallas_call x1, Pallas kernels, gather(): pl.pallas_call(functools.partial(gather_kernel, dims), in_specs=[vmem] *...  40.6 us
    pallas_call x1, Pallas kernels, attn_fwd(): pl.pallas_call(attn_fwd_kernel, grid=(n,), in_specs=[whole((rows, D)), wh...  24.3 us
    unnamed x4, local copies, waits for them, and re-layouts  6.35 us

profile of v1, /device:TPU:0, one launch (start us, length us, event | category | flops | bytes accessed | tf_op | source)
XLA Modules:
  0.0 216.5 jit_solution(11673669795348984133)
XLA Ops:
  0.7 1.4 copy.34.refs_3_
  2.1 1.6 copy.35.refs_5_
  3.7 40.6 %gather.1 = (bf16[384,1152]{1,0:T(8,128)(2,1)}, bf16[384,384]{1,0:T(8,128)(2,1)}, bf16[384,1536]{1,0:T(8,128)(2,1)}, bf16[384,1536]{1,0:T(8,128)(2,1)}, f32[8,384]{1,0:T(8,128)}, /*index=5*/f32[1,1536]{1,0:T(1,128)}) custom-call(bf16[24,192]{1,0:T(8,128)(2,1)} %refs_0_.1, bf16[24,192]{1,0:T(8,128)(2,1)} %refs_1_.1, bf16[24,192]{1,0:T(8,128)(2,1)} %refs_2_.1, ...), custom_call_target="tpu_custom_call" | custom-call | tf_op jit(solution)/shard_map/gather/pallas_call | solution.py:455
  44.3 24.3 %attn_fwd.1 = (bf16[16,208,1152]{2,1,0:T(8,128)(2,1)}, bf16[16,6,208,208]{3,2,1,0:T(8,128)(2,1)}, bf16[16,208,384]{2,1,0:T(8,128)(2,1)}, f32[16,208,384]{2,1,0:T(8,128)}) custom-call(bf16[3152,384]{1,0:T(8,128)(2,1)} %tok_ref.5, bf16[384,1152]{1,0:T(8,128)(2,1)} %get-tuple-element.55.w_ref, f32[8,384]{1,0:T(8,128)} %get-tuple-element.56.vec_ref), custom_call_target="tpu_custom_call" | custom-call | tf_op jit(solution)/shard_map/attn_fwd/pallas_call | solution.py:237
  68.6 58.2 %mlp.1 = (bf16[3152,384]{1,0:T(8,128)(2,1)}, f32[16,208,384]{2,1,0:T(8,128)}, bf16[16,208,384]{2,1,0:T(8,128)(2,1)}, f32[384,384]{1,0:T(8,128)}, f32[384,1536]{1...) custom-call(bf16[3152,384]{1,0:T(8,128)(2,1)} %tok_ref.5, bf16[3152,384]{1,0:T(8,128)(2,1)} %cot_ref.1, ...), custom_call_target="tpu_custom_call" | custom-call | tf_op jit(solution)/shard_map/mlp/pallas_call | solution.py:258
  126.9 43.3 %attn_bwd.1 = (f32[3152,384]{1,0:T(8,128)}, f32[384,1152]{1,0:T(8,128)}, f32[8,384]{1,0:T(8,128)}) custom-call(bf16[3152,384]{1,0:T(8,128)(2,1)} %tok_ref.5, bf16[16,208,1152]{2,1,0:T(8,128)(2,1)} %get-tuple-element.63.qkv_ref, bf16[16,6,208,208]{3,2,1,0:T(8,128)(2,1)} %get-tuple-element.64.e_ref, bf16[16,208,384]{2,1,0:T(8,128)(2,1)} %get-tuple-element.57.mixed_ref, ...), custom_call_target="tpu_custom_call" | custom-call | tf_op jit(solution)/shard_map/attn_bwd/pallas_call | solution.py:288
  170.1 41.0 %reduce.1 = (f32[24,2304]{1,0:T(8,128)}, f32[16,384]{1,0:T(8,128)}) custom-call(f32[384,1152]{1,0:T(8,128)} %get-tuple-element.69.dqkv, f32[384,384]{1,0:T(8,128)} %get-tuple-element.70.dwot, f32[384,1536]{1,0:T(8,128)} %get-tuple-element.71.dwup, f32[384,1536]{1,0:T(8,128)} %get-tuple-element.72.dwdt, f32[8,384]{1,0:T(8,128)} %get-tuple-element.73.dvec1, ...), custom_call_target="tpu_custom_call" | custom-call | tf_op jit(solution)/shard_map/reduce/pallas_call | solution.py:605
  211.1 2.0 split.1
  213.1 1.6 copy.36
  214.7 1.8 copy.37

commit v2 on v1

v2 whole, which is shorter than its diff:
```python
import functools
import math

import jax
import jax.numpy as jnp
from jax import lax
from jax.experimental import pallas as pl
from jax.experimental.pallas import tpu as pltpu
from jax.sharding import PartitionSpec as P

D = 384
HD = 64
FF = 1536
S = 197
HEADS = D // HD
PAIRS = HEADS // 2

SP = 208
WIN = 224

EPS = 1e-06
RSQRT2 = 0.7071067811865476
RSQRT_TAU = 0.3989422804014327
LOG2E = 1.4426950408889634
Q_SCALE = LOG2E / math.sqrt(HD)
BF = jnp.bfloat16
F32 = jnp.float32


def dot_nn(a, b):
    return lax.dot_general(a, b, (((1,), (0,)), ((), ())), preferred_element_type=F32)


def dot_nt(a, b):
    return lax.dot_general(a, b, (((1,), (1,)), ((), ())), preferred_element_type=F32)


def dot_tn(a, b):
    return lax.dot_general(a, b, (((0,), (0,)), ((), ())), preferred_element_type=F32)


def window_of(i, rows):
    start = i * S
    base = jnp.minimum((start // 16) * 16, rows - WIN)
    return pl.multiple_of(base, 16), start - base


def load_image(ref, i):
    base, off = window_of(i, ref.shape[0])
    rows = ref[pl.ds(base, WIN), :].astype(F32)
    rows = pltpu.roll(rows, WIN - off, axis=0)[:SP]
    live = lax.broadcasted_iota(jnp.int32, rows.shape, 0) < S
    return jnp.where(live, rows, 0.0)


def store_image(ref, i, rows):
    base, off = window_of(i, ref.shape[0])
    rows = jnp.concatenate([rows, jnp.zeros((WIN - SP, rows.shape[1]), F32)], axis=0)
    rows = pltpu.roll(rows, off, axis=0)
    old = ref[pl.ds(base, WIN), :].astype(F32)
    mine = lax.broadcasted_iota(jnp.int32, rows.shape, 0) >= off
    ref[pl.ds(base, WIN), :] = jnp.where(mine, rows, old).astype(ref.dtype)


def norm_stats(x):
    mean = jnp.mean(x, axis=-1, keepdims=True)
    centred = x - mean
    inv = lax.rsqrt(jnp.mean(centred * centred, axis=-1, keepdims=True) + EPS)
    return centred * inv, inv


def norm_backward(grad, normed, inv, gain):
    e = grad * gain
    return inv * (
        e
        - jnp.mean(e, axis=-1, keepdims=True)
        - normed * jnp.mean(e * normed, axis=-1, keepdims=True)
    )


def row_sum(x):
    return jnp.sum(x, axis=0, keepdims=True)


THIRD = D // 2
HALF = FF // 2
NARROW = 640
NARROW_CUT = 384
OUT_PAD = 256
WIDE = OUT_PAD + 2 * HALF
WIDE_CUT = 896
MESH = pl.DeviceIdType.MESH
EVERY = slice(None)


def chip_grid(dp):
    side = math.isqrt(dp // 4)
    return 4, side, side


def place_of(dims):
    _, ny, nx = dims
    dp, mp = lax.axis_index("dp"), lax.axis_index("mp")
    return dp // (ny * nx), (dp // nx) % ny, dp % nx, mp


def peers_of(dims, place):
    (nz, ny, nx), (z, y, x, mp) = dims, place

    def at(a, b, c, m):
        return ((a * ny + b) * nx + c, m)

    along = {
        "z": [((z + o) % nz, at((z + o) % nz, y, x, mp)) for o in range(1, nz)],
        "y": [((y + o) % ny, at(z, (y + o) % ny, x, mp)) for o in range(1, ny)],
        "x": [((x + o) % nx, at(z, y, (x + o) % nx, mp)) for o in range(1, nx)],
    }
    return along, at(z, y, x, 1 - mp)


def meet(along, other):
    barrier = pltpu.get_barrier_semaphore()
    devices = [d for peers in along.values() for _, d in peers] + [other]
    for device in devices:
        pl.semaphore_signal(barrier, inc=1, device_id=device, device_id_type=MESH)
    pl.semaphore_wait(barrier, len(devices))


class Copies:
    def __init__(self, send, recv):
        self.send, self.recv, self.groups, self.count = send, recv, {}, 0

    def plan(self, name, makers):
        self.groups[name] = [(self.count + i, m) for i, m in enumerate(makers)]
        self.count += len(makers)

    def each(self, names):
        for name in names:
            for index, make in self.groups[name]:
                src, dst, device = make()
                yield pltpu.make_async_remote_copy(
                    src_ref=src, dst_ref=dst, send_sem=self.send.at[index],
                    recv_sem=self.recv.at[index], device_id=device, device_id_type=MESH,
                )

    def start(self, *names):
        for copy in self.each(names):
            copy.start()

    def arrived(self, *names):
        for copy in self.each(names):
            copy.wait_recv()

    def left(self, *names):
        for copy in self.each(names):
            copy.wait_send()


def plan_gather(copies, tag, w, own, cut, along, other, place):
    z, y, x, mp = place
    low, high = pl.ds(0, cut), pl.ds(cut, w.shape[-1] - cut)

    def same(index, device):
        return lambda: (w.at[index], w.at[index], device)

    def spread(index, axis):
        return [same(index, d) for _, d in along[axis]]

    def shares(indices):
        return [same(index, other) for index in indices]

    copies.plan(tag + "1", [lambda d=d: (own, w.at[mp, z, y, x], d) for _, d in along["z"]])
    copies.plan(tag + "2l", spread((mp, EVERY, y, x, EVERY, low), "y"))
    copies.plan(tag + "2h", spread((mp, EVERY, y, x, EVERY, high), "x"))
    copies.plan(tag + "3l", spread((mp, EVERY, EVERY, x, EVERY, low), "x"))
    copies.plan(tag + "3h", spread((mp, EVERY, y, EVERY, EVERY, high), "y"))
    copies.plan(tag + "s1", shares([(mp, EVERY, y, x)]))
    copies.plan(tag + "s2l", shares([(mp, EVERY, b, x, EVERY, low) for b, _ in along["y"]]))
    copies.plan(tag + "s2h", shares([(mp, EVERY, y, c, EVERY, high) for c, _ in along["x"]]))
    copies.plan(tag + "s3l", shares([(mp, EVERY, EVERY, c, EVERY, low) for c, _ in along["x"]]))
    copies.plan(tag + "s3h", shares([(mp, EVERY, b, EVERY, EVERY, high) for b, _ in along["y"]]))


def attn_fwd_kernel(dims, n, *refs):
    (wq, wk, wv, wot, wu, wdt), vectors, bup_in, tok_ref = refs[:6], refs[6:14], refs[14], refs[15]
    (qkv_ref, e_ref, mixed_ref, linv_ref, normed_ref, inv_ref, w_ref, vec_ref, bup_ref, wide) = refs[
        16:26
    ]
    narrow, v, own, normed_all, inv_all, send, recv, sem = refs[26:]
    i = pl.program_id(0)
    nz, ny, nx = dims
    place = place_of(dims)
    z, y, x, mp = place
    rows = own.shape[0]
    along, other = peers_of(dims, place)
    copies = Copies(send, recv)
    plan_gather(copies, "n", narrow, narrow.at[mp, z, y, x], NARROW_CUT, along, other, place)
    plan_gather(copies, "w", wide, own, WIDE_CUT, along, other, place)

    def vec_spread(index, axis):
        return [lambda d=d: (v.at[index], v.at[index], d) for _, d in along[axis]]

    copies.plan("v1", vec_spread((z, y, x), "z"))
    copies.plan("v2", vec_spread((EVERY, y, x), "y"))
    copies.plan("v3", vec_spread((EVERY, EVERY, x), "x"))
    keep = pltpu.make_async_copy(own, wide.at[mp, z, y, x], sem)

    def norms(first, last):
        @pl.loop(first, last)
        def _(j):
            normed, inv = norm_stats(load_image(tok_ref, j))
            normed_all[j] = normed
            inv_all[j] = jnp.broadcast_to(inv, (SP, 128))

    @pl.when(i == 0)
    def _():
        narrow[mp, z, y, x] = jnp.concatenate(
            [wq[...], wk[...], wv[...], jnp.zeros((rows, NARROW - 3 * THIRD), BF)], axis=1
        )
        own[...] = jnp.concatenate(
            [wot[...], jnp.zeros((rows, OUT_PAD - THIRD), BF), wu[...], wdt[...]], axis=1
        )
        v[z, y, x] = jnp.zeros((16, 128), F32)
        for j, vector in enumerate(vectors):
            v[z, y, x, j : j + 1, :rows] = vector[...].astype(F32)
        v[z, y, x, 8:9, : bup_in.shape[1]] = bup_in[...].astype(F32)
        meet(along, other)
        copies.start("v1", "n1")
        keep.start()
        norms(0, n // 4)
        copies.arrived("v1", "n1")
        copies.start("v2", "n2l", "n2h", "w1", "ns1")
        norms(n // 4, n // 2)
        copies.arrived("v2", "n2l", "n2h")
        copies.start("v3", "n3l", "n3h", "ns2l", "ns2h")
        norms(n // 2, n)
        copies.arrived("v3", "n3l")
        copies.start("ns3l")
        copies.arrived("n3h")
        copies.start("ns3h")
        spots = [(a, b, c) for a in range(nz) for b in range(ny) for c in range(nx)]
        vec_ref[...] = jnp.concatenate([v[s][0:8, :rows] for s in spots], axis=1)
        bup_ref[...] = jnp.concatenate([v[s][8:9, : bup_in.shape[1]] for s in spots], axis=1)
        copies.arrived("ns1", "ns2l", "ns2h", "ns3l", "ns3h")
        group = 48 // rows
        for t in range(len(spots) // group):
            block = [
                jnp.concatenate(
                    [narrow[(m,) + s].astype(F32) for s in spots[t * group : (t + 1) * group]], axis=0
                )
                for m in range(2)
            ]
            for j in range(3):
                cols = slice(THIRD * j, THIRD * (j + 1))
                w_ref[48 * t : 48 * (t + 1), D * j : D * (j + 1)] = jnp.concatenate(
                    [half[:, cols] for half in block], axis=1
                ).astype(BF)

    @pl.when(i == 2)
    def _():
        keep.wait()
        copies.arrived("w1")
        copies.start("w2l", "w2h", "ws1")

    @pl.when(i == n // 4 + 1)
    def _():
        copies.arrived("w2l", "w2h")
        copies.start("w3l", "w3h", "ws2l", "ws2h")

    normed = normed_all[i]
    normed_ref[0] = normed
    inv_ref[0] = inv_all[i]
    h1 = (normed * vec_ref[0:1, :] + vec_ref[1:2, :]).astype(BF)
    q = ((dot_nn(h1, w_ref[:, 0:D]) + vec_ref[2:3, :]) * Q_SCALE).astype(BF)
    k = dot_nn(h1, w_ref[:, D : 2 * D]).astype(BF)
    value = (dot_nn(h1, w_ref[:, 2 * D :]) + vec_ref[3:4, :]).astype(BF)
    qkv_ref[0, :, 0:D] = q
    qkv_ref[0, :, D : 2 * D] = k
    qkv_ref[0, :, 2 * D :] = value
    lane = lax.broadcasted_iota(jnp.int32, (SP, 2 * HD), 1)
    is_key = lax.broadcasted_iota(jnp.int32, (SP, SP), 1) < S
    zero = jnp.zeros((SP, 2 * HD), BF)
    one = jnp.ones((SP, 2 * HD), BF)
    for p in range(PAIRS):
        cols = slice(2 * HD * p, 2 * HD * (p + 1))
        total = None
        for h in range(2):
            mine = (lane < HD) if h == 0 else (lane >= HD)
            kh = jnp.where(mine, k[:, cols], zero)
            vh = jnp.where(mine, value[:, cols], zero)
            scores = dot_nt(q[:, cols], kh)
            scores = jnp.where(is_key, scores, -1e30)
            top = jnp.max(scores, axis=-1, keepdims=True)
            e = jnp.exp2(scores - top).astype(BF)
            e_ref[0, 2 * p + h] = e
            part = dot_nn(e, jnp.concatenate([vh, jnp.where(mine, one, zero)], axis=1))
            total = part if total is None else total + part
        linv = 1.0 / total[:, 2 * HD :]
        linv_ref[0, :, cols] = linv
        mixed_ref[0, :, cols] = (total[:, : 2 * HD] * linv).astype(BF)

    @pl.when(i == (3 * n) // 4)
    def _():
        copies.arrived("w3l", "w3h")
        copies.start("ws3l", "ws3h")

    @pl.when(i == n - 1)
    def _():
        copies.arrived("ws1", "ws2l", "ws2h", "ws3l", "ws3h")
        copies.left(*copies.groups)


def attn_fwd(mats, vectors, bup, tokens, dp):
    dims = chip_grid(dp)
    nz, ny, nx = dims
    rows = D // dp
    n = tokens.shape[0] // S
    count = 2 * (nz - 1 + 4 * (ny - 1) + 4 * (nx - 1) + 1) + nz + ny + nx - 3
    inputs = (*mats, *vectors, bup, tokens)
    return pl.pallas_call(
        functools.partial(attn_fwd_kernel, dims, n),
        grid=(n,),
        in_specs=[whole(a.shape) for a in inputs],
        out_specs=[
            per_image(SP, 3 * D), per_image(HEADS, SP, SP), per_image(SP, D), per_image(SP, D),
            per_image(SP, D), per_image(SP, 128), whole((D, 3 * D)), whole((8, D)), whole((1, FF)),
            pl.BlockSpec(memory_space=pl.ANY),
        ],
        out_shape=[
            jax.ShapeDtypeStruct((n, SP, 3 * D), BF),
            jax.ShapeDtypeStruct((n, HEADS, SP, SP), BF),
            jax.ShapeDtypeStruct((n, SP, D), BF),
            jax.ShapeDtypeStruct((n, SP, D), F32),
            jax.ShapeDtypeStruct((n, SP, D), F32),
            jax.ShapeDtypeStruct((n, SP, 128), F32),
            jax.ShapeDtypeStruct((D, 3 * D), BF),
            jax.ShapeDtypeStruct((8, D), F32),
            jax.ShapeDtypeStruct((1, FF), F32),
            jax.ShapeDtypeStruct((2, nz, ny, nx, rows, WIDE), BF),
        ],
        scratch_shapes=[
            pltpu.VMEM((2, nz, ny, nx, rows, NARROW), BF),
            pltpu.VMEM((nz, ny, nx, 16, 128), F32),
            pltpu.VMEM((rows, WIDE), BF),
            pltpu.VMEM((n, SP, D), F32),
            pltpu.VMEM((n, SP, 128), F32),
            pltpu.SemaphoreType.DMA((count,)),
            pltpu.SemaphoreType.DMA((count,)),
            pltpu.SemaphoreType.DMA,
        ],
        compiler_params=params(collective_id=0),
        name="attn_fwd",
    )(*inputs)


def mlp_kernel(
    dims, n, tok_ref, cot_ref, mixed_ref, w_ref, vec_ref, bup_ref,
    out_ref, gres_ref, gmix_ref, grads_ref, dvec_ref, dbup_ref,
    act_ref, gp_ref, wot_ref, dwot_ref, dwup_ref, dwdt_ref,
):
    i = pl.program_id(0)

    @pl.when(i == 0)
    def _():
        wot_ref[...] = jnp.concatenate([w_ref[0, :, :THIRD], w_ref[1, :, :THIRD]], axis=1)
        dwot_ref[...] = jnp.zeros_like(dwot_ref)
        dwup_ref[...] = jnp.zeros_like(dwup_ref)
        dwdt_ref[...] = jnp.zeros_like(dwdt_ref)
        dvec_ref[...] = jnp.zeros_like(dvec_ref)
        dbup_ref[...] = jnp.zeros_like(dbup_ref)

    mixed = mixed_ref[0]
    cot_f = load_image(cot_ref, i)
    cot = cot_f.astype(BF)
    resid = load_image(tok_ref, i) + dot_nt(mixed, wot_ref[...]) + vec_ref[4:5, :]
    normed, inv = norm_stats(resid)
    h2 = (normed * vec_ref[5:6, :] + vec_ref[6:7, :]).astype(BF)
    step = 256
    for j in range(FF // step):
        cols = slice(step * j, step * (j + 1))
        m, at = divmod(step * j, HALF)
        u = dot_nn(h2, w_ref[m, :, OUT_PAD + at : OUT_PAD + at + step]) + bup_ref[:, cols]
        ga = dot_nn(cot, w_ref[m, :, OUT_PAD + HALF + at : OUT_PAD + HALF + at + step])
        cdf = 0.5 * (1.0 + lax.erf(u * RSQRT2))
        act_ref[:, cols] = (u * cdf).astype(BF)
        gp = ga * (cdf + u * jnp.exp(-0.5 * u * u) * RSQRT_TAU)
        dbup_ref[:, cols] += row_sum(gp)
        gp_ref[:, cols] = gp.astype(BF)
    out = resid + vec_ref[7:8, :]
    gh2 = None
    for m in range(2):
        cols = slice(HALF * m, HALF * (m + 1))
        out = out + dot_nt(act_ref[:, cols], w_ref[m, :, OUT_PAD + HALF :])
        part = dot_nt(gp_ref[:, cols], w_ref[m, :, OUT_PAD : OUT_PAD + HALF])
        gh2 = part if gh2 is None else gh2 + part
    store_image(out_ref, i, out)
    gres = cot_f + norm_backward(gh2, normed, inv, vec_ref[5:6, :])
    gres_ref[0] = gres
    gr = gres.astype(BF)
    gmix_ref[0] = dot_nn(gr, wot_ref[...]).astype(BF)
    dwot_ref[...] += dot_tn(gr, mixed)
    dwup_ref[...] += dot_tn(h2, gp_ref[...])
    dwdt_ref[...] += dot_tn(cot, act_ref[...])
    dvec_ref[0:1, :] += row_sum(gres)
    dvec_ref[1:2, :] += row_sum(gh2 * normed)
    dvec_ref[2:3, :] += row_sum(gh2)
    dvec_ref[3:4, :] += row_sum(cot_f)

    @pl.when(i == n - 1)
    def _():
        nz, ny, nx = dims
        rows = grads_ref.shape[4]
        spots = [(a, b, c) for a in range(nz) for b in range(ny) for c in range(nx)]
        group = 48 // rows
        for t in range(len(spots) // group):
            at = slice(48 * t, 48 * (t + 1))
            for m in range(2):
                parts = [
                    dwot_ref[at, THIRD * m : THIRD * (m + 1)],
                    jnp.zeros((48, OUT_PAD - THIRD), F32),
                    dwup_ref[at, HALF * m : HALF * (m + 1)],
                    dwdt_ref[at, HALF * m : HALF * (m + 1)],
                ]
                block = jnp.concatenate(parts, axis=1)
                for g in range(group):
                    grads_ref[(m,) + spots[t * group + g]] = block[
                        g * rows : (g + 1) * rows
                    ].astype(BF)


def mlp(tokens, cot, mixed, wide, vec, bup, dp):
    dims = chip_grid(dp)
    rows = tokens.shape[0]
    n = rows // S
    packed = (2, *dims, D // dp, WIDE)
    return pl.pallas_call(
        functools.partial(mlp_kernel, dims, n),
        grid=(n,),
        in_specs=[
            whole((rows, D)), whole((rows, D)), per_image(SP, D), whole((2, D, WIDE)), whole((8, D)),
            whole((1, FF)),
        ],
        out_specs=[
            whole((rows, D)), per_image(SP, D), per_image(SP, D), whole(packed), whole((8, D)),
            whole((1, FF)),
        ],
        out_shape=[
            jax.ShapeDtypeStruct((rows, D), BF),
            jax.ShapeDtypeStruct((n, SP, D), F32),
            jax.ShapeDtypeStruct((n, SP, D), BF),
            jax.ShapeDtypeStruct(packed, BF),
            jax.ShapeDtypeStruct((8, D), F32),
            jax.ShapeDtypeStruct((1, FF), F32),
        ],
        scratch_shapes=[
            pltpu.VMEM((SP, FF), BF), pltpu.VMEM((SP, FF), BF), pltpu.VMEM((D, D), BF),
            pltpu.VMEM((D, D), F32), pltpu.VMEM((D, FF), F32), pltpu.VMEM((D, FF), F32),
        ],
        compiler_params=params(),
        name="mlp",
    )(tokens, cot, mixed, wide, vec, bup)


class Reduction:
    def __init__(self, dims, copies, packed, bufs, cut):
        self.dims, self.copies, self.packed, self.cut = dims, copies, packed, cut
        self.place = place_of(dims)
        self.along, self.other = peers_of(dims, self.place)
        z, y, x, mp = self.place
        self.p, self.a1, self.b1, self.ra1, self.rb1, self.ra2, self.rb2, self.f, self.rz = bufs
        low, high = pl.ds(0, cut), pl.ds(cut, packed.shape[-1] - cut)
        along = self.along
        copies.plan("pair", [lambda: (packed.at[1 - mp], self.p, self.other)])
        copies.plan("1l", [
            lambda o=o, c=c, d=d: (self.p.at[EVERY, EVERY, c, EVERY, low], self.ra1.at[o], d)
            for o, (c, d) in enumerate(along["x"])
        ])
        copies.plan("1h", [
            lambda o=o, b=b, d=d: (self.p.at[EVERY, b, EVERY, EVERY, high], self.rb1.at[o], d)
            for o, (b, d) in enumerate(along["y"])
        ])
        copies.plan("2l", [
            lambda o=o, b=b, d=d: (self.a1.at[EVERY, b], self.ra2.at[o], d)
            for o, (b, d) in enumerate(along["y"])
        ])
        copies.plan("2h", [
            lambda o=o, c=c, d=d: (self.b1.at[EVERY, c], self.rb2.at[o], d)
            for o, (c, d) in enumerate(along["x"])
        ])
        copies.plan("3", [
            lambda o=o, a=a, d=d: (self.f.at[a], self.rz.at[o], d)
            for o, (a, d) in enumerate(along["z"])
        ])

    @staticmethod
    def count(dims):
        nz, ny, nx = dims
        return 1 + 2 * (ny - 1) + 2 * (nx - 1) + nz - 1

    @staticmethod
    def scratch(dims, rows, width, cut):
        nz, ny, nx = dims

        def buf(w, *shape):
            return pltpu.VMEM((*shape, rows, w), BF)

        rest = width - cut
        return [
            buf(width, nz, ny, nx), buf(cut, nz, ny), buf(rest, nz, nx),
            buf(cut, nx - 1, nz, ny), buf(rest, ny - 1, nz, nx),
            buf(cut, ny - 1, nz), buf(rest, nx - 1, nz), buf(width, nz), buf(width, nz - 1),
        ]

    def add_pair(self, mine):
        nz, ny, nx = self.dims
        for i in range(nz):
            for j in range(ny):
                for k in range(nx):
                    total = mine[i, j, k].astype(F32) + self.p[i, j, k].astype(F32)
                    self.p[i, j, k] = total.astype(BF)

    def add_first_low(self):
        nz, ny, nx = self.dims
        x = self.place[2]
        for i in range(nz):
            for j in range(ny):
                total = self.p[i, j, x, :, : self.cut].astype(F32)
                for o in range(nx - 1):
                    total = total + self.ra1[o, i, j].astype(F32)
                self.a1[i, j] = total.astype(BF)

    def add_first_high(self):
        nz, ny, nx = self.dims
        y = self.place[1]
        for i in range(nz):
            for k in range(nx):
                total = self.p[i, y, k, :, self.cut :].astype(F32)
                for o in range(ny - 1):
                    total = total + self.rb1[o, i, k].astype(F32)
                self.b1[i, k] = total.astype(BF)

    def add_second(self):
        nz, ny, nx = self.dims
        _, y, x, _ = self.place
        for i in range(nz):
            total = self.a1[i, y].astype(F32)
            for o in range(ny - 1):
                total = total + self.ra2[o, i].astype(F32)
            self.f[i, :, : self.cut] = total.astype(BF)
            total = self.b1[i, x].astype(F32)
            for o in range(nx - 1):
                total = total + self.rb2[o, i].astype(F32)
            self.f[i, :, self.cut :] = total.astype(BF)

    def add_third(self):
        total = self.f[self.place[0]].astype(F32)
        for o in range(self.dims[0] - 1):
            total = total + self.rz[o].astype(F32)
        return total


def attn_bwd_kernel(dims, n, qkv_ref, e_ref, mixed_ref, linv_ref, gmix_ref, packed, *refs):
    g_ref, dvec_ref, sum_ref = refs[:3]
    bufs, mine, send, recv, sem = refs[3:12], refs[12], refs[13], refs[14], refs[15]
    i = pl.program_id(0)
    copies = Copies(send, recv)
    red = Reduction(dims, copies, packed, bufs, WIDE_CUT)
    keep = pltpu.make_async_copy(packed.at[red.place[3]], mine, sem)

    @pl.when(i == 0)
    def _():
        dvec_ref[...] = jnp.zeros_like(dvec_ref)
        meet(red.along, red.other)
        copies.start("pair")
        keep.start()

    @pl.when(i == 2)
    def _():
        keep.wait()
        copies.arrived("pair")
        red.add_pair(mine)
        copies.start("1l", "1h")

    @pl.when(i == n // 2 - 1)
    def _():
        copies.arrived("1l", "1h")
        red.add_first_low()
        red.add_first_high()
        copies.start("2l", "2h")

    @pl.when(i == n // 2 + 2)
    def _():
        copies.arrived("2l", "2h")
        red.add_second()
        copies.start("3")

    lane = lax.broadcasted_iota(jnp.int32, (SP, 2 * HD), 1)
    zero = jnp.zeros((SP, 2 * HD), BF)
    minus = jnp.full((SP, 2 * HD), -1.0, BF)
    for p in range(PAIRS):
        lo, hi = 2 * HD * p, 2 * HD * (p + 1)
        q = qkv_ref[0, :, lo:hi]
        k = qkv_ref[0, :, D + lo : D + hi]
        v = qkv_ref[0, :, 2 * D + lo : 2 * D + hi]
        go_f = gmix_ref[0, :, lo:hi].astype(F32) * linv_ref[0, :, lo:hi]
        go = go_f.astype(BF)
        god = jnp.concatenate(
            [go, (go_f * mixed_ref[0, :, lo:hi].astype(F32)).astype(BF)], axis=1
        )
        gq = gk = gv = None
        for h in range(2):
            own = (lane < HD) if h == 0 else (lane >= HD)
            e = e_ref[0, 2 * p + h]
            vd = jnp.concatenate(
                [jnp.where(own, v, zero), jnp.where(own, minus, zero)], axis=1
            )
            ds = e * dot_nt(god, vd).astype(BF)
            part_q = dot_nn(ds, jnp.where(own, k, zero))
            part_k = dot_tn(ds, jnp.where(own, q, zero))
            part_v = dot_tn(e, jnp.where(own, go, zero))
            gq = part_q if gq is None else gq + part_q
            gk = part_k if gk is None else gk + part_k
            gv = part_v if gv is None else gv + part_v
        gq = gq * (1.0 / math.sqrt(HD))
        dvec_ref[0:1, lo:hi] += row_sum(gq)
        dvec_ref[1:2, lo:hi] += row_sum(gv)
        g_ref[0, :, lo:hi] = gq.astype(BF)
        g_ref[0, :, D + lo : D + hi] = (gk * (1.0 / LOG2E)).astype(BF)
        g_ref[0, :, 2 * D + lo : 2 * D + hi] = gv.astype(BF)

    @pl.when(i == n - 1)
    def _():
        copies.arrived("3")
        sum_ref[...] = red.add_third()
        copies.left(*copies.groups)


def attn_bwd(qkv, e, mixed, linv, gmix, packed, dp):
    dims = chip_grid(dp)
    n = qkv.shape[0]
    rows = D // dp
    count = Reduction.count(dims)
    return pl.pallas_call(
        functools.partial(attn_bwd_kernel, dims, n),
        grid=(n,),
        in_specs=[
            per_image(SP, 3 * D), per_image(HEADS, SP, SP), per_image(SP, D), per_image(SP, D),
            per_image(SP, D), pl.BlockSpec(memory_space=pl.ANY),
        ],
        out_specs=[per_image(SP, 3 * D), whole((8, D)), whole((rows, WIDE))],
        out_shape=[
            jax.ShapeDtypeStruct((n, SP, 3 * D), BF),
            jax.ShapeDtypeStruct((8, D), F32),
            jax.ShapeDtypeStruct((rows, WIDE), F32),
        ],
        scratch_shapes=[
            *Reduction.scratch(dims, rows, WIDE, WIDE_CUT),
            pltpu.VMEM((*dims, rows, WIDE), BF),
            pltpu.SemaphoreType.DMA((count,)),
            pltpu.SemaphoreType.DMA((count,)),
            pltpu.SemaphoreType.DMA,
        ],
        compiler_params=params(collective_id=1),
        name="attn_bwd",
    )(qkv, e, mixed, linv, gmix, packed)


def tokens_kernel(
    dims, n, g_ref, normed_ref, inv_ref, gres_ref, w_ref, vec_ref, dvec1_ref, dvec2_ref, dbup_ref,
    gtok_ref, packed_ref, sums_ref, dw_ref, dvec_ref,
):
    i = pl.program_id(0)

    @pl.when(i == 0)
    def _():
        dw_ref[...] = jnp.zeros_like(dw_ref)
        dvec_ref[...] = jnp.zeros_like(dvec_ref)

    g = g_ref[0]
    normed = normed_ref[0]
    inv = inv_ref[0]
    inv = jnp.concatenate([inv, inv, inv], axis=1)
    h1 = (normed * vec_ref[0:1, :] + vec_ref[1:2, :]).astype(BF)
    gh1 = dot_nt(g, w_ref[...])
    dw_ref[...] += dot_tn(h1, g)
    gtok = gres_ref[0] + norm_backward(gh1, normed, inv, vec_ref[0:1, :])
    store_image(gtok_ref, i, gtok)
    dvec_ref[0:1, :] += row_sum(gh1 * normed)
    dvec_ref[1:2, :] += row_sum(gh1)

    @pl.when(i == n - 1)
    def _():
        nz, ny, nx = dims
        rows = packed_ref.shape[4]
        spots = [(a, b, c) for a in range(nz) for b in range(ny) for c in range(nx)]
        group = 48 // rows
        for t in range(len(spots) // group):
            at = slice(48 * t, 48 * (t + 1))
            for m in range(2):
                parts = [
                    dw_ref[at, D * j + THIRD * m : D * j + THIRD * (m + 1)] for j in range(3)
                ]
                parts.append(jnp.zeros((48, NARROW - 3 * THIRD), F32))
                block = jnp.concatenate(parts, axis=1)
                for k in range(group):
                    packed_ref[(m,) + spots[t * group + k]] = block[
                        k * rows : (k + 1) * rows
                    ].astype(BF)
        sums_ref[0:2] = dvec1_ref[0:2]
        sums_ref[2:4] = dvec_ref[0:2]
        sums_ref[4:8] = dvec2_ref[0:4]
        for j in range(FF // D):
            sums_ref[8 + j : 9 + j] = dbup_ref[:, D * j : D * (j + 1)]
        sums_ref[12:16] = jnp.zeros((4, D), F32)


def tokens_grad(g, normed, inv, gres, wqkv, vec, dvec1, dvec2, dbup, rows, dp):
    dims = chip_grid(dp)
    n = g.shape[0]
    packed = (2, *dims, D // dp, NARROW)
    return pl.pallas_call(
        functools.partial(tokens_kernel, dims, n),
        grid=(n,),
        in_specs=[
            per_image(SP, 3 * D), per_image(SP, D), per_image(SP, 128), per_image(SP, D),
            whole((D, 3 * D)), whole((8, D)), whole((8, D)), whole((8, D)), whole((1, FF)),
        ],
        out_specs=[whole((rows, D)), whole(packed), whole((16, D))],
        out_shape=[
            jax.ShapeDtypeStruct((rows, D), F32),
            jax.ShapeDtypeStruct(packed, BF),
            jax.ShapeDtypeStruct((16, D), F32),
        ],
        scratch_shapes=[pltpu.VMEM((D, 3 * D), F32), pltpu.VMEM((8, D), F32)],
        compiler_params=params(),
        name="tokens_grad",
    )(g, normed, inv, gres, wqkv, vec, dvec1, dvec2, dbup)


def reduce_kernel(dims, packed, sums, out_ref, vec_ref, *refs):
    bufs, vs, vr, send, recv = refs[:9], refs[9], refs[10], refs[11], refs[12]
    nz, ny, nx = dims
    copies = Copies(send, recv)
    red = Reduction(dims, copies, packed, bufs, NARROW_CUT)
    mp = red.place[3]
    along, other = red.along, red.other
    stages = [[other], *([d for _, d in along[axis]] for axis in "xyz")]
    base = 0
    bases = []
    for s, devices in enumerate(stages):
        copies.plan("v%d" % s, [
            lambda s=s, at=base + o, d=d: (sums if s == 0 else vs.at[s - 1], vr.at[at], d)
            for o, d in enumerate(devices)
        ])
        bases.append((base, len(devices)))
        base += len(devices)

    def vec_add(stage):
        total = sums[...] if stage == 0 else vs[stage - 1]
        first, count = bases[stage]
        for o in range(count):
            total = total + vr[first + o]
        if stage < 3:
            vs[stage] = total
        else:
            vec_ref[...] = total

    meet(along, other)
    copies.start("pair", "v0")
    copies.arrived("pair", "v0")
    red.add_pair(packed.at[mp])
    vec_add(0)
    copies.start("1l", "1h", "v1")
    copies.arrived("1l", "v1")
    red.add_first_low()
    vec_add(1)
    copies.start("2l", "v2")
    copies.arrived("1h")
    red.add_first_high()
    copies.start("2h")
    copies.arrived("2l", "2h", "v2")
    red.add_second()
    vec_add(2)
    copies.start("3", "v3")
    copies.arrived("3", "v3")
    out_ref[...] = red.add_third()
    vec_add(3)
    copies.left(*copies.groups)


def reduce(packed, sums, dp):
    dims = chip_grid(dp)
    nz, ny, nx = dims
    rows = D // dp
    count = Reduction.count(dims) + nz + ny + nx - 2
    vmem = pl.BlockSpec(memory_space=pltpu.VMEM)
    return pl.pallas_call(
        functools.partial(reduce_kernel, dims),
        in_specs=[vmem] * 2,
        out_specs=[vmem] * 2,
        out_shape=[
            jax.ShapeDtypeStruct((rows, NARROW), F32),
            jax.ShapeDtypeStruct((16, D), F32),
        ],
        scratch_shapes=[
            *Reduction.scratch(dims, rows, NARROW, NARROW_CUT),
            pltpu.VMEM((3, 16, D), F32),
            pltpu.VMEM((nz + ny + nx - 2, 16, D), F32),
            pltpu.SemaphoreType.DMA((count,)),
            pltpu.SemaphoreType.DMA((count,)),
        ],
        compiler_params=pltpu.CompilerParams(
            collective_id=2, has_side_effects=True, vmem_limit_bytes=48 * 1024 * 1024
        ),
        name="reduce",
    )(packed, sums)


def split_kernel(n, narrow_ref, wide_ref, vec_ref, *outs):
    for j in range(3):
        outs[j][...] = narrow_ref[:, THIRD * j : THIRD * (j + 1)]
    outs[3][...] = wide_ref[:, :THIRD]
    outs[4][...] = wide_ref[:, OUT_PAD : OUT_PAD + HALF]
    outs[5][...] = wide_ref[:, OUT_PAD + HALF :]
    index = lax.axis_index("dp") * 2 + lax.axis_index("mp")
    per = D // n
    vec = pltpu.roll(vec_ref[...], D - index * per, axis=1)
    for row, out in zip((2, 3, 0, 1, 4, 5, 6, 7), outs[6:]):
        out[...] = vec[row : row + 1, :per]
    wide = jnp.concatenate([vec_ref[8 + j : 9 + j, :] for j in range(FF // D)], axis=1)
    wide = pltpu.roll(jnp.broadcast_to(wide, (8, FF)), FF - index * (FF // n), axis=1)
    outs[14][...] = wide[0:1, : FF // n]


def split(narrow, wide, vec, n):
    rows = narrow.shape[0]
    vmem = pl.BlockSpec(memory_space=pltpu.VMEM)
    shapes = [(rows, THIRD)] * 4 + [(rows, HALF)] * 2 + [(1, D // n)] * 8 + [(1, FF // n)]
    return pl.pallas_call(
        functools.partial(split_kernel, n),
        in_specs=[vmem] * 3,
        out_specs=[vmem] * 15,
        out_shape=[jax.ShapeDtypeStruct(s, F32) for s in shapes],
        name="split",
    )(narrow, wide, vec)


def whole(shape):
    return pl.BlockSpec(shape, lambda i: (0,) * len(shape))


def per_image(*shape):
    return pl.BlockSpec((1, *shape), lambda i: (i,) + (0,) * len(shape))


def params(collective_id=None):
    return pltpu.CompilerParams(
        dimension_semantics=("arbitrary",), vmem_limit_bytes=62 * 1024 * 1024,
        collective_id=collective_id, has_side_effects=collective_id is not None,
    )


def on_device(
    tokens, w_query, w_key, w_value, w_out, w_up, w_down, ln1_gain, ln1_bias, b_query, b_value,
    b_out, ln2_gain, ln2_bias, b_up, b_down, cotangent,
):
    dp = lax.axis_size("dp")
    vectors = (ln1_gain, ln1_bias, b_query, b_value, b_out, ln2_gain, ln2_bias, b_down)
    qkv, e, mixed, linv, normed, inv, wqkv, vec, bup, wide = attn_fwd(
        (w_query, w_key, w_value, w_out.T, w_up, w_down.T), [v[None] for v in vectors], b_up[None],
        tokens, dp,
    )
    out, gres, gmix, packed, dvec2, dbup = mlp(
        tokens, cotangent, mixed, wide.reshape(2, D, WIDE), vec, bup, dp
    )
    g, dvec1, wide_sum = attn_bwd(qkv, e, mixed, linv, gmix, packed, dp)
    gtok, packed, sums = tokens_grad(
        g, normed, inv, gres, wqkv, vec, dvec1, dvec2, dbup, tokens.shape[0], dp
    )
    narrow_sum, sums = reduce(packed, sums, dp)
    grads = split(narrow_sum, wide_sum, sums, dp * lax.axis_size("mp"))
    vecs = [v.reshape(-1) for v in grads[6:]]
    return (
        out, gtok, grads[0], grads[1], grads[2], grads[3].T, grads[4], grads[5].T,
        *vecs[:7], vecs[8], vecs[7],
    )


def solution(mesh):
    row, mat, tam, vec = P(("dp", "mp"), None), P("dp", "mp"), P("mp", "dp"), P("dp")
    part = P(("dp", "mp"))
    return jax.shard_map(
        on_device,
        mesh=mesh,
        in_specs=(row, mat, mat, mat, tam, mat, tam, *([vec] * 9), row),
        out_specs=(row, row, mat, mat, mat, tam, mat, tam, *([part] * 9)),
        check_vma=False,
    )
```

time: 217 us -> 186 us (0.86)
  Pallas kernels: 209 us -> 181 us
  local copies, waits for them, and re-layouts: 6.35 us -> 3.15 us
    pallas_call x1, Pallas kernels: 41 us -> 19.1 us  [reduce(): pl.pallas_call(functools.partial(reduce_kernel, dims), in_specs=[vmem] *...]
    pallas_call x5, Pallas kernels: 168 us -> 162 us  [the longest x1 59.3 us: mlp(): pl.pallas_call(functools.partial(mlp_kernel, dims, n), grid=(n,), in_spec...]
    unnamed x4 -> x8, local copies, waits for them, and re-layouts: 6.35 us -> 3.15 us
where the time goes in v2:
time: 186 us; the launch traced here: 185 us
  Pallas kernels  181 us (97%)
  local copies, waits for them, and re-layouts  3.15 us (2%)
    pallas_call x1, Pallas kernels, mlp(): pl.pallas_call(functools.partial(mlp_kernel, dims, n), grid=(n,), in_spec...  59.3 us
    pallas_call x1, Pallas kernels, attn_fwd(): pl.pallas_call(functools.partial(attn_fwd_kernel, dims, n), grid=(n,), in...  46.2 us
    pallas_call x1, Pallas kernels, attn_bwd(): pl.pallas_call(functools.partial(attn_bwd_kernel, dims, n), grid=(n,), in...  32.8 us
    pallas_call x1, Pallas kernels, tokens_grad(): pl.pallas_call(functools.partial(tokens_kernel, dims, n), grid=(n,), in_s...  21.6 us
    pallas_call x1, Pallas kernels, reduce(): pl.pallas_call(functools.partial(reduce_kernel, dims), in_specs=[vmem] *...  19.1 us

profile of v2, /device:TPU:0, one launch (start us, length us, event | category | flops | bytes accessed | tf_op | source)
XLA Modules:
  0.0 184.6 jit_solution(634557139784713578)
XLA Ops:
  0.7 46.2 %attn_fwd.1 = (bf16[16,208,1152]{2,1,0:T(8,128)(2,1)}, bf16[16,6,208,208]{3,2,1,0:T(8,128)(2,1)}, bf16[16,208,384]{2,1,0:T(8,128)(2,1)}, f32[16,208,384]{2,1,0:T...) custom-call(bf16[24,192]{1,0:T(8,128)(2,1)} %refs_0_.1, ...), custom_call_target="tpu_custom_call" | custom-call | tf_op jit(solution)/shard_map/attn_fwd/pallas_call | solution.py:320
  46.9 59.3 %mlp.1 = (bf16[3152,384]{1,0:T(8,128)(2,1)}, f32[16,208,384]{2,1,0:T(8,128)}, bf16[16,208,384]{2,1,0:T(8,128)(2,1)}, bf16[2,4,2,2,24,1792]{5,4,3,2,1,0:T(8,128)(...) custom-call(bf16[3152,384]{1,0:T(8,128)(2,1)} %tok_ref.1, bf16[3152,384]{1,0:T(8,128)(2,1)} %cot_ref.1, ...), custom_call_target="tpu_custom_call" | custom-call | tf_op jit(solution)/shard_map/mlp/pallas_call | solution.py:436
  106.2 32.8 %attn_bwd.1 = (bf16[16,208,1152]{2,1,0:T(8,128)(2,1)}, f32[8,384]{1,0:T(8,128)}, f32[24,1792]{1,0:T(8,128)}) custom-call(bf16[16,208,1152]{2,1,0:T(8,128)(2,1)} %get-tuple-element.61.qkv_ref, bf16[16,6,208,208]{3,2,1,0:T(8,128)(2,1)} %get-tuple-element.62.e_ref, bf16[16,208,384]{2,1,0:T(8,128)(2,1)} %get-tuple-element.56.mixed_ref, ...), custom_call_target="tpu_custom_call" | custom-call | tf_op jit(solution)/shard_map/attn_bwd/pallas_call | solution.py:643
  139.1 21.6 %tokens_grad.1 = (f32[3152,384]{1,0:T(8,128)}, bf16[2,4,2,2,24,640]{5,4,3,2,1,0:T(8,128)(2,1)}, f32[16,384]{1,0:T(8,128)}) custom-call(bf16[16,208,1152]{2,1,0:T(8,128)(2,1)} %get-tuple-element.66.g_ref, f32[16,208,384]{2,1,0:T(8,128)} %get-tuple-element.67.normed_ref, f32[16,208,128]{2,1,0:T(8,128)} %get-tuple-element.68.inv_ref, ...), custom_call_target="tpu_custom_call" | custom-call | tf_op jit(solution)/shard_map/tokens_grad/pallas_call | solution.py:721
  160.7 0.0 copy-start
  160.7 1.2 copy-done
  161.9 0.0 copy-start.3
  161.9 0.7 copy-done.3
  162.6 19.1 %reduce.1 = (f32[24,640]{1,0:T(8,128)S(1)}, f32[16,384]{1,0:T(8,128)S(1)}) custom-call(bf16[2,4,2,2,24,640]{5,4,3,2,1,0:T(8,128)(2,1)S(1)} %copy-done, f32[16,384]{1,0:T(8,128)S(1)} %copy-done.3), custom_call_target="tpu_custom_call" | custom-call | tf_op jit(solution)/shard_map/reduce/pallas_call | solution.py:797
  181.7 0.0 copy-start.1
  181.7 0.6 copy-done.1
  182.3 0.0 copy-start.2
  182.3 0.6 copy-done.2
  182.9 1.7 split.1
Async XLA Ops:
  160.7 1.2 copy-start
  161.9 0.7 copy-start.3
  181.7 0.6 copy-start.1
  182.3 0.6 copy-start.2

commit v3 on v2

--- a/solution.py
+++ b/solution.py
@@ -118,12 +118,16 @@
     return along, at(z, y, x, 1 - mp)
 
 
-def meet(along, other):
-    barrier = pltpu.get_barrier_semaphore()
-    devices = [d for peers in along.values() for _, d in peers] + [other]
-    for device in devices:
-        pl.semaphore_signal(barrier, inc=1, device_id=device, device_id_type=MESH)
-    pl.semaphore_wait(barrier, len(devices))
+def greet(along, other):
+    for device in [d for peers in along.values() for _, d in peers] + [other]:
+        pl.semaphore_signal(
+            pltpu.get_barrier_semaphore(), inc=1, device_id=device, device_id_type=MESH
+        )
+
+
+def met(along):
+    count = sum(len(peers) for peers in along.values()) + 1
+    pl.semaphore_wait(pltpu.get_barrier_semaphore(), count)
 
 
 class Copies:
@@ -224,20 +228,25 @@
         for j, vector in enumerate(vectors):
             v[z, y, x, j : j + 1, :rows] = vector[...].astype(F32)
         v[z, y, x, 8:9, : bup_in.shape[1]] = bup_in[...].astype(F32)
-        meet(along, other)
-        copies.start("v1", "n1")
+        greet(along, other)
         keep.start()
         norms(0, n // 4)
+        met(along)
+        copies.start("v1", "n1")
+        norms(n // 4, n // 2)
         copies.arrived("v1", "n1")
         copies.start("v2", "n2l", "n2h", "w1", "ns1")
-        norms(n // 4, n // 2)
+        norms(n // 2, (3 * n) // 4)
         copies.arrived("v2", "n2l", "n2h")
         copies.start("v3", "n3l", "n3h", "ns2l", "ns2h")
-        norms(n // 2, n)
+        norms((3 * n) // 4, n)
         copies.arrived("v3", "n3l")
         copies.start("ns3l")
         copies.arrived("n3h")
         copies.start("ns3h")
+        keep.wait()
+        copies.arrived("w1")
+        copies.start("w2l", "w2h", "ws1")
         spots = [(a, b, c) for a in range(nz) for b in range(ny) for c in range(nx)]
         vec_ref[...] = jnp.concatenate([v[s][0:8, :rows] for s in spots], axis=1)
         bup_ref[...] = jnp.concatenate([v[s][8:9, : bup_in.shape[1]] for s in spots], axis=1)
@@ -256,13 +265,7 @@
                     [half[:, cols] for half in block], axis=1
                 ).astype(BF)
 
-    @pl.when(i == 2)
-    def _():
-        keep.wait()
-        copies.arrived("w1")
-        copies.start("w2l", "w2h", "ws1")
-
-    @pl.when(i == n // 4 + 1)
+    @pl.when(i == 3)
     def _():
         copies.arrived("w2l", "w2h")
         copies.start("w3l", "w3h", "ws2l", "ws2h")
@@ -299,7 +302,7 @@
         linv_ref[0, :, cols] = linv
         mixed_ref[0, :, cols] = (total[:, : 2 * HD] * linv).astype(BF)
 
-    @pl.when(i == (3 * n) // 4)
+    @pl.when(i == n - 5)
     def _():
         copies.arrived("w3l", "w3h")
         copies.start("ws3l", "ws3h")
@@ -559,9 +562,12 @@
         return total
 
 
-def attn_bwd_kernel(dims, n, qkv_ref, e_ref, mixed_ref, linv_ref, gmix_ref, packed, *refs):
-    g_ref, dvec_ref, sum_ref = refs[:3]
-    bufs, mine, send, recv, sem = refs[3:12], refs[12], refs[13], refs[14], refs[15]
+def attn_bwd_kernel(
+    dims, n, qkv_ref, e_ref, mixed_ref, linv_ref, gmix_ref, normed_ref, w_ref, vec_ref, dvec2_ref,
+    dbup_ref, packed, *refs,
+):
+    g_ref, narrow_ref, sums_ref, sum_ref = refs[:4]
+    acc_ref, gsum_ref, bufs, mine, send, recv, sem = refs[4], refs[5], refs[6:15], *refs[15:]
     i = pl.program_id(0)
     copies = Copies(send, recv)
     red = Reduction(dims, copies, packed, bufs, WIDE_CUT)
@@ -569,12 +575,17 @@
 
     @pl.when(i == 0)
     def _():
-        dvec_ref[...] = jnp.zeros_like(dvec_ref)
-        meet(red.along, red.other)
+        acc_ref[...] = jnp.zeros_like(acc_ref)
+        gsum_ref[...] = jnp.zeros_like(gsum_ref)
+        greet(red.along, red.other)
+        keep.start()
+
+    @pl.when(i == 1)
+    def _():
+        met(red.along)
         copies.start("pair")
-        keep.start()
-
-    @pl.when(i == 2)
+
+    @pl.when(i == 3)
     def _():
         keep.wait()
         copies.arrived("pair")
@@ -622,38 +633,78 @@
             gk = part_k if gk is None else gk + part_k
             gv = part_v if gv is None else gv + part_v
         gq = gq * (1.0 / math.sqrt(HD))
-        dvec_ref[0:1, lo:hi] += row_sum(gq)
-        dvec_ref[1:2, lo:hi] += row_sum(gv)
-        g_ref[0, :, lo:hi] = gq.astype(BF)
-        g_ref[0, :, D + lo : D + hi] = (gk * (1.0 / LOG2E)).astype(BF)
-        g_ref[0, :, 2 * D + lo : 2 * D + hi] = gv.astype(BF)
+        gk = gk * (1.0 / LOG2E)
+        for j, grad in enumerate((gq, gk, gv)):
+            gsum_ref[0:1, D * j + lo : D * j + hi] += row_sum(grad)
+            g_ref[0, :, D * j + lo : D * j + hi] = grad.astype(BF)
+    acc_ref[...] += dot_tn(normed_ref[0].astype(BF), g_ref[0])
 
     @pl.when(i == n - 1)
     def _():
         copies.arrived("3")
         sum_ref[...] = red.add_third()
+        nz, ny, nx = dims
+        rows = narrow_ref.shape[4]
+        spots = [(a, b, c) for a in range(nz) for b in range(ny) for c in range(nx)]
+        group = 48 // rows
+        turned = vec_ref[...].T
+        gsum = gsum_ref[0:1, :]
+        gains = []
+        for t in range(len(spots) // group):
+            at = slice(48 * t, 48 * (t + 1))
+            acc = acc_ref[at, :]
+            gains.append(jnp.sum(acc * w_ref[at, :].astype(F32), axis=1, keepdims=True))
+            dw = acc * turned[at, 0:1] + turned[at, 1:2] * gsum
+            for m in range(2):
+                parts = [dw[:, D * j + THIRD * m : D * j + THIRD * (m + 1)] for j in range(3)]
+                parts.append(jnp.zeros((48, NARROW - 3 * THIRD), F32))
+                block = jnp.concatenate(parts, axis=1)
+                for k in range(group):
+                    narrow_ref[(m,) + spots[t * group + k]] = block[
+                        k * rows : (k + 1) * rows
+                    ].astype(BF)
+        high = gsum.astype(BF)
+        low = (gsum - high.astype(F32)).astype(BF)
+        row = lax.broadcasted_iota(jnp.int32, (16, 3 * D), 0)
+        both = jnp.where(row == 0, high, jnp.where(row == 1, low, jnp.zeros((16, 3 * D), BF)))
+        sums_ref[0:1] = gsum[:, :D]
+        sums_ref[1:2] = gsum[:, 2 * D :]
+        gain = jnp.broadcast_to(jnp.concatenate(gains, axis=0), (D, 128)).T
+        sums_ref[2:3] = gain[0:1, :]
+        sums_ref[3:4] = row_sum(dot_nt(both, w_ref[...]))
+        sums_ref[4:8] = dvec2_ref[0:4]
+        for j in range(FF // D):
+            sums_ref[8 + j : 9 + j] = dbup_ref[:, D * j : D * (j + 1)]
+        sums_ref[12:16] = jnp.zeros((4, D), F32)
         copies.left(*copies.groups)
 
 
-def attn_bwd(qkv, e, mixed, linv, gmix, packed, dp):
+def attn_bwd(qkv, e, mixed, linv, gmix, normed, wqkv, vec, dvec2, dbup, packed, dp):
     dims = chip_grid(dp)
     n = qkv.shape[0]
     rows = D // dp
     count = Reduction.count(dims)
+    narrow = (2, *dims, rows, NARROW)
     return pl.pallas_call(
         functools.partial(attn_bwd_kernel, dims, n),
         grid=(n,),
         in_specs=[
             per_image(SP, 3 * D), per_image(HEADS, SP, SP), per_image(SP, D), per_image(SP, D),
-            per_image(SP, D), pl.BlockSpec(memory_space=pl.ANY),
-        ],
-        out_specs=[per_image(SP, 3 * D), whole((8, D)), whole((rows, WIDE))],
+            per_image(SP, D), per_image(SP, D), whole((D, 3 * D)), whole((8, D)), whole((8, D)),
+            whole((1, FF)), pl.BlockSpec(memory_space=pl.ANY),
+        ],
+        out_specs=[
+            per_image(SP, 3 * D), whole(narrow), whole((16, D)), whole((rows, WIDE)),
+        ],
         out_shape=[
             jax.ShapeDtypeStruct((n, SP, 3 * D), BF),
-            jax.ShapeDtypeStruct((8, D), F32),
+            jax.ShapeDtypeStruct(narrow, BF),
+            jax.ShapeDtypeStruct((16, D), F32),
             jax.ShapeDtypeStruct((rows, WIDE), F32),
         ],
         scratch_shapes=[
+            pltpu.VMEM((D, 3 * D), F32),
+            pltpu.VMEM((8, 3 * D), F32),
             *Reduction.scratch(dims, rows, WIDE, WIDE_CUT),
             pltpu.VMEM((*dims, rows, WIDE), BF),
             pltpu.SemaphoreType.DMA((count,)),
@@ -662,158 +713,116 @@
         ],
         compiler_params=params(collective_id=1),
         name="attn_bwd",
-    )(qkv, e, mixed, linv, gmix, packed)
+    )(qkv, e, mixed, linv, gmix, normed, wqkv, vec, dvec2, dbup, packed)
 
 
 def tokens_kernel(
-    dims, n, g_ref, normed_ref, inv_ref, gres_ref, w_ref, vec_ref, dvec1_ref, dvec2_ref, dbup_ref,
-    gtok_ref, packed_ref, sums_ref, dw_ref, dvec_ref,
+    dims, n, g_ref, normed_ref, inv_ref, gres_ref, w_ref, vec_ref, sums, packed, *refs
 ):
+    gtok_ref, sum_ref, total_ref = refs[:3]
+    bufs, mine, vs, vr, send, recv, sem = refs[3:12], *refs[12:]
     i = pl.program_id(0)
+    copies = Copies(send, recv)
+    red = Reduction(dims, copies, packed, bufs, NARROW_CUT)
+    keep = pltpu.make_async_copy(packed.at[red.place[3]], mine, sem)
+    stages = [[red.other], *([d for _, d in red.along[axis]] for axis in "xyz")]
+    bases = [sum(len(s) for s in stages[:k]) for k in range(4)]
+    for k, devices in enumerate(stages):
+        copies.plan("v%d" % k, [
+            lambda k=k, o=o, d=d: (sums if k == 0 else vs.at[k - 1], vr.at[bases[k] + o], d)
+            for o, d in enumerate(devices)
+        ])
+
+    def vec_add(k):
+        total = sums[...] if k == 0 else vs[k - 1]
+        for o in range(len(stages[k])):
+            total = total + vr[bases[k] + o]
+        if k < 3:
+            vs[k] = total
+        else:
+            total_ref[...] = total
 
     @pl.when(i == 0)
     def _():
-        dw_ref[...] = jnp.zeros_like(dw_ref)
-        dvec_ref[...] = jnp.zeros_like(dvec_ref)
-
-    g = g_ref[0]
-    normed = normed_ref[0]
+        greet(red.along, red.other)
+        keep.start()
+
+    @pl.when(i == 2)
+    def _():
+        met(red.along)
+        copies.start("pair", "v0")
+
+    @pl.when(i == 5)
+    def _():
+        keep.wait()
+        copies.arrived("pair", "v0")
+        red.add_pair(mine)
+        vec_add(0)
+        copies.start("1l", "1h", "v1")
+
+    @pl.when(i == n - 6)
+    def _():
+        copies.arrived("1l", "v1")
+        red.add_first_low()
+        vec_add(1)
+        copies.start("2l", "v2")
+        copies.arrived("1h")
+        red.add_first_high()
+        copies.start("2h")
+
+    @pl.when(i == n - 2)
+    def _():
+        copies.arrived("2l", "2h", "v2")
+        red.add_second()
+        vec_add(2)
+        copies.start("3", "v3")
+
     inv = inv_ref[0]
     inv = jnp.concatenate([inv, inv, inv], axis=1)
-    h1 = (normed * vec_ref[0:1, :] + vec_ref[1:2, :]).astype(BF)
-    gh1 = dot_nt(g, w_ref[...])
-    dw_ref[...] += dot_tn(h1, g)
-    gtok = gres_ref[0] + norm_backward(gh1, normed, inv, vec_ref[0:1, :])
-    store_image(gtok_ref, i, gtok)
-    dvec_ref[0:1, :] += row_sum(gh1 * normed)
-    dvec_ref[1:2, :] += row_sum(gh1)
+    gh1 = dot_nt(g_ref[0], w_ref[...])
+    store_image(
+        gtok_ref, i, gres_ref[0] + norm_backward(gh1, normed_ref[0], inv, vec_ref[0:1, :])
+    )
 
     @pl.when(i == n - 1)
     def _():
-        nz, ny, nx = dims
-        rows = packed_ref.shape[4]
-        spots = [(a, b, c) for a in range(nz) for b in range(ny) for c in range(nx)]
-        group = 48 // rows
-        for t in range(len(spots) // group):
-            at = slice(48 * t, 48 * (t + 1))
-            for m in range(2):
-                parts = [
-                    dw_ref[at, D * j + THIRD * m : D * j + THIRD * (m + 1)] for j in range(3)
-                ]
-                parts.append(jnp.zeros((48, NARROW - 3 * THIRD), F32))
-                block = jnp.concatenate(parts, axis=1)
-                for k in range(group):
-                    packed_ref[(m,) + spots[t * group + k]] = block[
-                        k * rows : (k + 1) * rows
-                    ].astype(BF)
-        sums_ref[0:2] = dvec1_ref[0:2]
-        sums_ref[2:4] = dvec_ref[0:2]
-        sums_ref[4:8] = dvec2_ref[0:4]
-        for j in range(FF // D):
-            sums_ref[8 + j : 9 + j] = dbup_ref[:, D * j : D * (j + 1)]
-        sums_ref[12:16] = jnp.zeros((4, D), F32)
-
-
-def tokens_grad(g, normed, inv, gres, wqkv, vec, dvec1, dvec2, dbup, rows, dp):
+        copies.arrived("3", "v3")
+        sum_ref[...] = red.add_third()
+        vec_add(3)
+        copies.left(*copies.groups)
+
+
+def tokens_grad(g, normed, inv, gres, wqkv, vec, sums, packed, rows, dp):
     dims = chip_grid(dp)
+    nz, ny, nx = dims
     n = g.shape[0]
-    packed = (2, *dims, D // dp, NARROW)
+    part = D // dp
+    count = Reduction.count(dims) + nz + ny + nx - 2
     return pl.pallas_call(
         functools.partial(tokens_kernel, dims, n),
         grid=(n,),
         in_specs=[
             per_image(SP, 3 * D), per_image(SP, D), per_image(SP, 128), per_image(SP, D),
-            whole((D, 3 * D)), whole((8, D)), whole((8, D)), whole((8, D)), whole((1, FF)),
-        ],
-        out_specs=[whole((rows, D)), whole(packed), whole((16, D))],
+            whole((D, 3 * D)), whole((8, D)), whole((16, D)), pl.BlockSpec(memory_space=pl.ANY),
+        ],
+        out_specs=[whole((rows, D)), whole((part, NARROW)), whole((16, D))],
         out_shape=[
             jax.ShapeDtypeStruct((rows, D), F32),
-            jax.ShapeDtypeStruct(packed, BF),
+            jax.ShapeDtypeStruct((part, NARROW), F32),
             jax.ShapeDtypeStruct((16, D), F32),
         ],
-        scratch_shapes=[pltpu.VMEM((D, 3 * D), F32), pltpu.VMEM((8, D), F32)],
-        compiler_params=params(),
-        name="tokens_grad",
-    )(g, normed, inv, gres, wqkv, vec, dvec1, dvec2, dbup)
-
-
-def reduce_kernel(dims, packed, sums, out_ref, vec_ref, *refs):
-    bufs, vs, vr, send, recv = refs[:9], refs[9], refs[10], refs[11], refs[12]
-    nz, ny, nx = dims
-    copies = Copies(send, recv)
-    red = Reduction(dims, copies, packed, bufs, NARROW_CUT)
-    mp = red.place[3]
-    along, other = red.along, red.other
-    stages = [[other], *([d for _, d in along[axis]] for axis in "xyz")]
-    base = 0
-    bases = []
-    for s, devices in enumerate(stages):
-        copies.plan("v%d" % s, [
-            lambda s=s, at=base + o, d=d: (sums if s == 0 else vs.at[s - 1], vr.at[at], d)
-            for o, d in enumerate(devices)
-        ])
-        bases.append((base, len(devices)))
-        base += len(devices)
-
-    def vec_add(stage):
-        total = sums[...] if stage == 0 else vs[stage - 1]
-        first, count = bases[stage]
-        for o in range(count):
-            total = total + vr[first + o]
-        if stage < 3:
-            vs[stage] = total
-        else:
-            vec_ref[...] = total
-
-    meet(along, other)
-    copies.start("pair", "v0")
-    copies.arrived("pair", "v0")
-    red.add_pair(packed.at[mp])
-    vec_add(0)
-    copies.start("1l", "1h", "v1")
-    copies.arrived("1l", "v1")
-    red.add_first_low()
-    vec_add(1)
-    copies.start("2l", "v2")
-    copies.arrived("1h")
-    red.add_first_high()
-    copies.start("2h")
-    copies.arrived("2l", "2h", "v2")
-    red.add_second()
-    vec_add(2)
-    copies.start("3", "v3")
-    copies.arrived("3", "v3")
-    out_ref[...] = red.add_third()
-    vec_add(3)
-    copies.left(*copies.groups)
-
-
-def reduce(packed, sums, dp):
-    dims = chip_grid(dp)
-    nz, ny, nx = dims
-    rows = D // dp
-    count = Reduction.count(dims) + nz + ny + nx - 2
-    vmem = pl.BlockSpec(memory_space=pltpu.VMEM)
-    return pl.pallas_call(
-        functools.partial(reduce_kernel, dims),
-        in_specs=[vmem] * 2,
-        out_specs=[vmem] * 2,
-        out_shape=[
-            jax.ShapeDtypeStruct((rows, NARROW), F32),
-            jax.ShapeDtypeStruct((16, D), F32),
-        ],
         scratch_shapes=[
-            *Reduction.scratch(dims, rows, NARROW, NARROW_CUT),
+            *Reduction.scratch(dims, part, NARROW, NARROW_CUT),
+            pltpu.VMEM((*dims, part, NARROW), BF),
             pltpu.VMEM((3, 16, D), F32),
             pltpu.VMEM((nz + ny + nx - 2, 16, D), F32),
             pltpu.SemaphoreType.DMA((count,)),
             pltpu.SemaphoreType.DMA((count,)),
-        ],
-        compiler_params=pltpu.CompilerParams(
-            collective_id=2, has_side_effects=True, vmem_limit_bytes=48 * 1024 * 1024
-        ),
-        name="reduce",
-    )(packed, sums)
+            pltpu.SemaphoreType.DMA,
+        ],
+        compiler_params=params(collective_id=2),
+        name="tokens_grad",
+    )(g, normed, inv, gres, wqkv, vec, sums, packed)
 
 
 def split_kernel(n, narrow_ref, wide_ref, vec_ref, *outs):
@@ -873,11 +882,12 @@
     out, gres, gmix, packed, dvec2, dbup = mlp(
         tokens, cotangent, mixed, wide.reshape(2, D, WIDE), vec, bup, dp
     )
-    g, dvec1, wide_sum = attn_bwd(qkv, e, mixed, linv, gmix, packed, dp)
-    gtok, packed, sums = tokens_grad(
-        g, normed, inv, gres, wqkv, vec, dvec1, dvec2, dbup, tokens.shape[0], dp
+    g, packed, sums, wide_sum = attn_bwd(
+        qkv, e, mixed, linv, gmix, normed, wqkv, vec, dvec2, dbup, packed, dp
     )
-    narrow_sum, sums = reduce(packed, sums, dp)
+    gtok, narrow_sum, sums = tokens_grad(
+        g, normed, inv, gres, wqkv, vec, sums, packed, tokens.shape[0], dp
+    )
     grads = split(narrow_sum, wide_sum, sums, dp * lax.axis_size("mp"))
     vecs = [v.reshape(-1) for v in grads[6:]]
     return (

time: 186 us -> 176 us (0.946)
  Pallas kernels: 181 us -> 170 us
    pallas_call x1 -> x0, Pallas kernels: 19.1 us -> none  [reduce(): pl.pallas_call(functools.partial(reduce_kernel, dims), in_specs=[vmem] *...]
    pallas_call x1, Pallas kernels: 32.8 us -> 39.3 us  [attn_bwd(): pl.pallas_call(functools.partial(attn_bwd_kernel, dims, n), grid=(n,), in...]
    pallas_call x1, Pallas kernels: 21.6 us -> 24.7 us  [tokens_grad(): pl.pallas_call(functools.partial(tokens_kernel, dims, n), grid=(n,), in_s...]
    unnamed x8 -> x1, local copies, waits for them, and re-layouts: 3.15 us -> 4.91 us
where the time goes in v3:
time: 176 us
  Pallas kernels  170 us (97%)
  local copies, waits for them, and re-layouts  4.91 us (3%)
    pallas_call x1, Pallas kernels, mlp(): pl.pallas_call(functools.partial(mlp_kernel, dims, n), grid=(n,), in_spec...  59.3 us
    pallas_call x1, Pallas kernels, attn_fwd(): pl.pallas_call(functools.partial(attn_fwd_kernel, dims, n), grid=(n,), in...  45.2 us
    pallas_call x1, Pallas kernels, attn_bwd(): pl.pallas_call(functools.partial(attn_bwd_kernel, dims, n), grid=(n,), in...  39.3 us
    pallas_call x1, Pallas kernels, tokens_grad(): pl.pallas_call(functools.partial(tokens_kernel, dims, n), grid=(n,), in_s...  24.7 us
    unnamed x1, local copies, waits for them, and re-layouts  4.91 us

profile of v3, /device:TPU:0, one launch (start us, length us, event | category | flops | bytes accessed | tf_op | source)
XLA Modules:
  0.0 175.8 jit_solution(12617856191986561748)
XLA Ops:
  0.7 45.2 %attn_fwd.1 = (bf16[16,208,1152]{2,1,0:T(8,128)(2,1)}, bf16[16,6,208,208]{3,2,1,0:T(8,128)(2,1)}, bf16[16,208,384]{2,1,0:T(8,128)(2,1)}, f32[16,208,384]{2,1,0:T...) custom-call(bf16[24,192]{1,0:T(8,128)(2,1)} %refs_0_.1, ...), custom_call_target="tpu_custom_call" | custom-call | tf_op jit(solution)/shard_map/attn_fwd/pallas_call | solution.py:323
  45.9 59.3 %mlp.1 = (bf16[3152,384]{1,0:T(8,128)(2,1)}, f32[16,208,384]{2,1,0:T(8,128)}, bf16[16,208,384]{2,1,0:T(8,128)(2,1)}, bf16[2,4,2,2,24,1792]{5,4,3,2,1,0:T(8,128)(...) custom-call(bf16[3152,384]{1,0:T(8,128)(2,1)} %tok_ref.1, bf16[3152,384]{1,0:T(8,128)(2,1)} %cot_ref.1, ...), custom_call_target="tpu_custom_call" | custom-call | tf_op jit(solution)/shard_map/mlp/pallas_call | solution.py:439
  105.2 39.3 %attn_bwd.1 = (bf16[16,208,1152]{2,1,0:T(8,128)(2,1)}, bf16[2,4,2,2,24,640]{5,4,3,2,1,0:T(8,128)(2,1)}, f32[16,384]{1,0:T(8,128)}, f32[24,1792]{1,0:T(8,128)}) custom-call(bf16[16,208,1152]{2,1,0:T(8,128)(2,1)} %get-tuple-element.60.qkv_ref, bf16[16,6,208,208]{3,2,1,0:T(8,128)(2,1)} %get-tuple-element.61.e_ref, ...), custom_call_target="tpu_custom_call" | custom-call | tf_op jit(solution)/shard_map/attn_bwd/pallas_call | solution.py:688
  144.5 24.7 %tokens_grad.1 = (f32[3152,384]{1,0:T(8,128)}, f32[24,640]{1,0:T(8,128)}, f32[16,384]{1,0:T(8,128)}) custom-call(bf16[16,208,1152]{2,1,0:T(8,128)(2,1)} %get-tuple-element.69.g_ref, f32[16,208,384]{2,1,0:T(8,128)} %get-tuple-element.64.normed_ref, f32[16,208,128]{2,1,0:T(8,128)} %get-tuple-element.70.inv_ref, f32[16,208,384]{2,1,0:T(8,128)} %get-tuple-element.71.gres_ref, ...), custom_call_target="tpu_custom_call" | custom-call | tf_op jit(solution)/shard_map/tokens_grad/pallas_call | solution.py:801
  169.2 1.7 split.1
  170.9 4.9 %copy.35 = f32[3152,384]{1,0:T(8,128)} copy(f32[3152,384]{1,0:T(8,128)} %get-tuple-element.111) | data formatting | bytes 9682944

commit v4 on v3

--- a/solution.py
+++ b/solution.py
@@ -54,12 +54,23 @@
 
 
 def store_image(ref, i, rows):
-    base, off = window_of(i, ref.shape[0])
-    rows = jnp.concatenate([rows, jnp.zeros((WIN - SP, rows.shape[1]), F32)], axis=0)
-    rows = pltpu.roll(rows, off, axis=0)
-    old = ref[pl.ds(base, WIN), :].astype(F32)
-    mine = lax.broadcasted_iota(jnp.int32, rows.shape, 0) >= off
-    ref[pl.ds(base, WIN), :] = jnp.where(mine, rows, old).astype(ref.dtype)
+    start = i * S
+    r = start % 8
+    base = start - r
+    total = ref.shape[0]
+    groups = SP // 8
+    turned = pltpu.roll(rows.reshape(groups, 8, D), r, axis=1)
+    first = lax.broadcasted_iota(jnp.int32, (8, D), 0) < r
+    old = ref[pl.ds(pl.multiple_of(base, 8), 8), :]
+    ref[pl.ds(pl.multiple_of(base, 8), 8), :] = jnp.where(first, old, turned[0])
+    for g in range(1, groups - 1):
+        ref[pl.ds(pl.multiple_of(base + 8 * g, 8), 8), :] = jnp.where(
+            first, turned[g - 1], turned[g]
+        )
+    over = base + SP > total
+    here = jnp.where(over, total - 8, base + SP - 8)
+    tail = [jnp.where(first, turned[g - 1], turned[g]) for g in (groups - 2, groups - 1)]
+    ref[pl.ds(pl.multiple_of(here, 8), 8), :] = jnp.where(over, tail[0], tail[1])
 
 
 def norm_stats(x):
@@ -186,11 +197,13 @@
 
 
 def attn_fwd_kernel(dims, n, *refs):
-    (wq, wk, wv, wot, wu, wdt), vectors, bup_in, tok_ref = refs[:6], refs[6:14], refs[14], refs[15]
-    (qkv_ref, e_ref, mixed_ref, linv_ref, normed_ref, inv_ref, w_ref, vec_ref, bup_ref, wide) = refs[
-        16:26
-    ]
-    narrow, v, own, normed_all, inv_all, send, recv, sem = refs[26:]
+    (wq, wk, wv, wot, wu, wdt), vectors, bup_in = refs[:6], refs[6:14], refs[14]
+    tok_ref, cot_ref = refs[15:17]
+    (
+        qkv_ref, e_ref, mixed_ref, linv_ref, normed_ref, inv_ref, tokp_ref, cotp_ref, w_ref, vec_ref,
+        bup_ref, wide,
+    ) = refs[17:29]
+    narrow, v, own, normed_all, inv_all, tok_all, cot_all, send, recv, sem = refs[29:]
     i = pl.program_id(0)
     nz, ny, nx = dims
     place = place_of(dims)
@@ -212,7 +225,10 @@
     def norms(first, last):
         @pl.loop(first, last)
         def _(j):
-            normed, inv = norm_stats(load_image(tok_ref, j))
+            tok = load_image(tok_ref, j)
+            normed, inv = norm_stats(tok)
+            tok_all[j] = tok.astype(BF)
+            cot_all[j] = load_image(cot_ref, j).astype(BF)
             normed_all[j] = normed
             inv_all[j] = jnp.broadcast_to(inv, (SP, 128))
 
@@ -273,6 +289,8 @@
     normed = normed_all[i]
     normed_ref[0] = normed
     inv_ref[0] = inv_all[i]
+    tokp_ref[0] = tok_all[i]
+    cotp_ref[0] = cot_all[i]
     h1 = (normed * vec_ref[0:1, :] + vec_ref[1:2, :]).astype(BF)
     q = ((dot_nn(h1, w_ref[:, 0:D]) + vec_ref[2:3, :]) * Q_SCALE).astype(BF)
     k = dot_nn(h1, w_ref[:, D : 2 * D]).astype(BF)
@@ -313,21 +331,21 @@
         copies.left(*copies.groups)
 
 
-def attn_fwd(mats, vectors, bup, tokens, dp):
+def attn_fwd(mats, vectors, bup, tokens, cot, dp):
     dims = chip_grid(dp)
     nz, ny, nx = dims
     rows = D // dp
     n = tokens.shape[0] // S
     count = 2 * (nz - 1 + 4 * (ny - 1) + 4 * (nx - 1) + 1) + nz + ny + nx - 3
-    inputs = (*mats, *vectors, bup, tokens)
+    inputs = (*mats, *vectors, bup, tokens, cot)
     return pl.pallas_call(
         functools.partial(attn_fwd_kernel, dims, n),
         grid=(n,),
         in_specs=[whole(a.shape) for a in inputs],
         out_specs=[
             per_image(SP, 3 * D), per_image(HEADS, SP, SP), per_image(SP, D), per_image(SP, D),
-            per_image(SP, D), per_image(SP, 128), whole((D, 3 * D)), whole((8, D)), whole((1, FF)),
-            pl.BlockSpec(memory_space=pl.ANY),
+            per_image(SP, D), per_image(SP, 128), per_image(SP, D), per_image(SP, D),
+            whole((D, 3 * D)), whole((8, D)), whole((1, FF)), pl.BlockSpec(memory_space=pl.ANY),
         ],
         out_shape=[
             jax.ShapeDtypeStruct((n, SP, 3 * D), BF),
@@ -336,6 +354,8 @@
             jax.ShapeDtypeStruct((n, SP, D), F32),
             jax.ShapeDtypeStruct((n, SP, D), F32),
             jax.ShapeDtypeStruct((n, SP, 128), F32),
+            jax.ShapeDtypeStruct((n, SP, D), BF),
+            jax.ShapeDtypeStruct((n, SP, D), BF),
             jax.ShapeDtypeStruct((D, 3 * D), BF),
             jax.ShapeDtypeStruct((8, D), F32),
             jax.ShapeDtypeStruct((1, FF), F32),
@@ -347,6 +367,8 @@
             pltpu.VMEM((rows, WIDE), BF),
             pltpu.VMEM((n, SP, D), F32),
             pltpu.VMEM((n, SP, 128), F32),
+            pltpu.VMEM((n, SP, D), BF),
+            pltpu.VMEM((n, SP, D), BF),
             pltpu.SemaphoreType.DMA((count,)),
             pltpu.SemaphoreType.DMA((count,)),
             pltpu.SemaphoreType.DMA,
@@ -354,32 +376,79 @@
         compiler_params=params(collective_id=0),
         name="attn_fwd",
     )(*inputs)
+
+
+def fold(x):
+    return jnp.sum(x.reshape(x.shape[0] // 8, 8, x.shape[1]), axis=0)
+
+
+CHUNK = 16
 
 
 def mlp_kernel(
     dims, n, tok_ref, cot_ref, mixed_ref, w_ref, vec_ref, bup_ref,
     out_ref, gres_ref, gmix_ref, grads_ref, dvec_ref, dbup_ref,
     act_ref, gp_ref, wot_ref, dwot_ref, dwup_ref, dwdt_ref,
+    h2_ref, h2t_ref, cott_ref, mix_ref, gr_ref, outf_ref, out_old, gh2_ref, cotf_ref, norm_ref,
+    inv_ref, sums_ref, upsum_ref,
 ):
     i = pl.program_id(0)
+    step = 256
+    tiles = FF // step
+    chunks = [slice(c, c + CHUNK) for c in range(0, SP, CHUNK)]
 
     @pl.when(i == 0)
     def _():
         wot_ref[...] = jnp.concatenate([w_ref[0, :, :THIRD], w_ref[1, :, :THIRD]], axis=1)
-        dwot_ref[...] = jnp.zeros_like(dwot_ref)
-        dwup_ref[...] = jnp.zeros_like(dwup_ref)
-        dwdt_ref[...] = jnp.zeros_like(dwdt_ref)
-        dvec_ref[...] = jnp.zeros_like(dvec_ref)
-        dbup_ref[...] = jnp.zeros_like(dbup_ref)
-
-    mixed = mixed_ref[0]
-    cot_f = load_image(cot_ref, i)
-    cot = cot_f.astype(BF)
-    resid = load_image(tok_ref, i) + dot_nt(mixed, wot_ref[...]) + vec_ref[4:5, :]
-    normed, inv = norm_stats(resid)
-    h2 = (normed * vec_ref[5:6, :] + vec_ref[6:7, :]).astype(BF)
-    step = 256
-    for j in range(FF // step):
+        for ref in (
+            dwot_ref, dwup_ref, dwdt_ref, act_ref, gp_ref, h2t_ref, cott_ref, mix_ref, out_old,
+            gh2_ref, cotf_ref, norm_ref, inv_ref, sums_ref, upsum_ref,
+        ):
+            ref[...] = jnp.zeros_like(ref)
+
+    def weight_tile(j):
+        cols = slice(step * j, step * (j + 1))
+        dwup_ref[:, cols] += dot_nn(h2t_ref[...], gp_ref[:, cols])
+        dwdt_ref[:, cols] += dot_nn(cott_ref[...], act_ref[:, cols])
+
+    def finish(image, beside):
+        beside(0)
+        slot = image % 2
+        for at in chunks:
+            gh2, normed, cot = gh2_ref[at, :], norm_ref[at, :], cotf_ref[at, :]
+            gres = cot + norm_backward(gh2, normed, inv_ref[at, 0:1], vec_ref[5:6, :])
+            gres_ref[slot, at, :] = gres
+            gr_ref[at, :] = gres.astype(BF)
+            sums_ref[0] += fold(gres)
+            sums_ref[1] += fold(gh2 * normed)
+            sums_ref[2] += fold(gh2)
+            sums_ref[3] += fold(cot)
+        beside(1)
+        gmix_ref[slot] = dot_nn(gr_ref[...], wot_ref[...]).astype(BF)
+        beside(2)
+        store_image(outf_ref, image, out_old[...])
+        dwot_ref[...] += dot_tn(gr_ref[...], mix_ref[...])
+        beside(3)
+
+    finish(jnp.maximum(i - 1, 0), weight_tile)
+    weight_tile(4)
+    attended = dot_nt(mixed_ref[0], wot_ref[...])
+    for at in chunks:
+        cot = cot_ref[0, at, :].astype(F32)
+        resid = tok_ref[0, at, :].astype(F32) + attended[at] + vec_ref[4:5, :]
+        normed, inv = norm_stats(resid)
+        h2_ref[at, :] = (normed * vec_ref[5:6, :] + vec_ref[6:7, :]).astype(BF)
+        cotf_ref[at, :] = cot
+        norm_ref[at, :] = normed
+        inv_ref[at, :] = jnp.broadcast_to(inv, (CHUNK, 128))
+        out_old[at, :] = resid + vec_ref[7:8, :]
+    weight_tile(5)
+    mix_ref[...] = mixed_ref[0]
+    h2 = h2_ref[...]
+    cot = cot_ref[0]
+    h2t_ref[...] = h2.T
+    cott_ref[...] = cot.T
+    for j in range(tiles):
         cols = slice(step * j, step * (j + 1))
         m, at = divmod(step * j, HALF)
         u = dot_nn(h2, w_ref[m, :, OUT_PAD + at : OUT_PAD + at + step]) + bup_ref[:, cols]
@@ -387,30 +456,28 @@
         cdf = 0.5 * (1.0 + lax.erf(u * RSQRT2))
         act_ref[:, cols] = (u * cdf).astype(BF)
         gp = ga * (cdf + u * jnp.exp(-0.5 * u * u) * RSQRT_TAU)
-        dbup_ref[:, cols] += row_sum(gp)
+        upsum_ref[:, cols] += fold(gp)
         gp_ref[:, cols] = gp.astype(BF)
-    out = resid + vec_ref[7:8, :]
+    out = out_old[...]
     gh2 = None
     for m in range(2):
         cols = slice(HALF * m, HALF * (m + 1))
         out = out + dot_nt(act_ref[:, cols], w_ref[m, :, OUT_PAD + HALF :])
         part = dot_nt(gp_ref[:, cols], w_ref[m, :, OUT_PAD : OUT_PAD + HALF])
         gh2 = part if gh2 is None else gh2 + part
-    store_image(out_ref, i, out)
-    gres = cot_f + norm_backward(gh2, normed, inv, vec_ref[5:6, :])
-    gres_ref[0] = gres
-    gr = gres.astype(BF)
-    gmix_ref[0] = dot_nn(gr, wot_ref[...]).astype(BF)
-    dwot_ref[...] += dot_tn(gr, mixed)
-    dwup_ref[...] += dot_tn(h2, gp_ref[...])
-    dwdt_ref[...] += dot_tn(cot, act_ref[...])
-    dvec_ref[0:1, :] += row_sum(gres)
-    dvec_ref[1:2, :] += row_sum(gh2 * normed)
-    dvec_ref[2:3, :] += row_sum(gh2)
-    dvec_ref[3:4, :] += row_sum(cot_f)
+    out_old[...] = out
+    gh2_ref[...] = gh2
 
     @pl.when(i == n - 1)
     def _():
+        finish(i, weight_tile)
+        weight_tile(4)
+        weight_tile(5)
+        out_ref[...] = outf_ref[...].astype(BF)
+        for k in range(4):
+            dvec_ref[k : k + 1, :] = row_sum(sums_ref[k])
+        dvec_ref[4:8, :] = jnp.zeros((4, D), F32)
+        dbup_ref[...] = row_sum(upsum_ref[...])
         nz, ny, nx = dims
         rows = grads_ref.shape[4]
         spots = [(a, b, c) for a in range(nz) for b in range(ny) for c in range(nx)]
@@ -431,22 +498,19 @@
                     ].astype(BF)
 
 
-def mlp(tokens, cot, mixed, wide, vec, bup, dp):
+def mlp(tok, cot, mixed, wide, vec, bup, rows, dp):
     dims = chip_grid(dp)
-    rows = tokens.shape[0]
     n = rows // S
     packed = (2, *dims, D // dp, WIDE)
+    late = pl.BlockSpec((2, SP, D), lambda i: (jnp.maximum(i - 1, 0) // 2, 0, 0))
     return pl.pallas_call(
         functools.partial(mlp_kernel, dims, n),
         grid=(n,),
         in_specs=[
-            whole((rows, D)), whole((rows, D)), per_image(SP, D), whole((2, D, WIDE)), whole((8, D)),
+            per_image(SP, D), per_image(SP, D), per_image(SP, D), whole((2, D, WIDE)), whole((8, D)),
             whole((1, FF)),
         ],
-        out_specs=[
-            whole((rows, D)), per_image(SP, D), per_image(SP, D), whole(packed), whole((8, D)),
-            whole((1, FF)),
-        ],
+        out_specs=[whole((rows, D)), late, late, whole(packed), whole((8, D)), whole((1, FF))],
         out_shape=[
             jax.ShapeDtypeStruct((rows, D), BF),
             jax.ShapeDtypeStruct((n, SP, D), F32),
@@ -458,10 +522,15 @@
         scratch_shapes=[
             pltpu.VMEM((SP, FF), BF), pltpu.VMEM((SP, FF), BF), pltpu.VMEM((D, D), BF),
             pltpu.VMEM((D, D), F32), pltpu.VMEM((D, FF), F32), pltpu.VMEM((D, FF), F32),
+            pltpu.VMEM((SP, D), BF), pltpu.VMEM((D, SP), BF), pltpu.VMEM((D, SP), BF),
+            pltpu.VMEM((SP, D), BF), pltpu.VMEM((SP, D), BF), pltpu.VMEM((rows, D), F32),
+            pltpu.VMEM((SP, D), F32), pltpu.VMEM((SP, D), F32), pltpu.VMEM((SP, D), F32),
+            pltpu.VMEM((SP, D), F32), pltpu.VMEM((SP, 128), F32), pltpu.VMEM((4, 8, D), F32),
+            pltpu.VMEM((8, FF), F32),
         ],
         compiler_params=params(),
         name="mlp",
-    )(tokens, cot, mixed, wide, vec, bup)
+    )(tok, cot, mixed, wide, vec, bup)
 
 
 class Reduction:
@@ -875,12 +944,12 @@
 ):
     dp = lax.axis_size("dp")
     vectors = (ln1_gain, ln1_bias, b_query, b_value, b_out, ln2_gain, ln2_bias, b_down)
-    qkv, e, mixed, linv, normed, inv, wqkv, vec, bup, wide = attn_fwd(
+    qkv, e, mixed, linv, normed, inv, tok, cot, wqkv, vec, bup, wide = attn_fwd(
         (w_query, w_key, w_value, w_out.T, w_up, w_down.T), [v[None] for v in vectors], b_up[None],
-        tokens, dp,
+        tokens, cotangent, dp,
     )
     out, gres, gmix, packed, dvec2, dbup = mlp(
-        tokens, cotangent, mixed, wide.reshape(2, D, WIDE), vec, bup, dp
+        tok, cot, mixed, wide.reshape(2, D, WIDE), vec, bup, tokens.shape[0], dp
     )
     g, packed, sums, wide_sum = attn_bwd(
         qkv, e, mixed, linv, gmix, normed, wqkv, vec, dvec2, dbup, packed, dp

time: 176 us -> 171 us (0.972)
  Pallas kernels: 170 us -> 165 us
    pallas_call x1, Pallas kernels: 59.3 us -> 54 us  [mlp(): pl.pallas_call(functools.partial(mlp_kernel, dims, n), grid=(n,), in_spec...]
    pallas_call x1, Pallas kernels: 45.2 us -> 47.3 us  [attn_fwd(): pl.pallas_call(functools.partial(attn_fwd_kernel, dims, n), grid=(n,), in...]
where the time goes in v4:
time: 171 us
  Pallas kernels  165 us (96%)
  local copies, waits for them, and re-layouts  4.91 us (3%)
    pallas_call x1, Pallas kernels, mlp(): pl.pallas_call(functools.partial(mlp_kernel, dims, n), grid=(n,), in_spec...  54 us
    pallas_call x1, Pallas kernels, attn_fwd(): pl.pallas_call(functools.partial(attn_fwd_kernel, dims, n), grid=(n,), in...  47.3 us
    pallas_call x1, Pallas kernels, attn_bwd(): pl.pallas_call(functools.partial(attn_bwd_kernel, dims, n), grid=(n,), in...  38.3 us
    pallas_call x1, Pallas kernels, tokens_grad(): pl.pallas_call(functools.partial(tokens_kernel, dims, n), grid=(n,), in_s...  24 us
    unnamed x1, local copies, waits for them, and re-layouts  4.91 us

profile of v4, /device:TPU:0, one launch (start us, length us, event | category | flops | bytes accessed | tf_op | source)
XLA Modules:
  0.0 170.8 jit_solution(15731178860033706124)
XLA Ops:
  0.7 47.3 %attn_fwd.1 = (bf16[16,208,1152]{2,1,0:T(8,128)(2,1)}, bf16[16,6,208,208]{3,2,1,0:T(8,128)(2,1)}, bf16[16,208,384]{2,1,0:T(8,128)(2,1)}, f32[16,208,384]{2,1,0:T...) custom-call(bf16[24,192]{1,0:T(8,128)(2,1)} %refs_0_.1, ...), custom_call_target="tpu_custom_call" | custom-call | tf_op jit(solution)/shard_map/attn_fwd/pallas_call | solution.py:341
  47.9 54.0 %mlp.1 = (bf16[3152,384]{1,0:T(8,128)(2,1)}, f32[16,208,384]{2,1,0:T(8,128)}, bf16[16,208,384]{2,1,0:T(8,128)(2,1)}, bf16[2,4,2,2,24,1792]{5,4,3,2,1,0:T(8,128)(...) custom-call(bf16[16,208,384]{2,1,0:T(8,128)(2,1)} %get-tuple-element.57.tok_ref, ...), custom_call_target="tpu_custom_call" | custom-call | tf_op jit(solution)/shard_map/mlp/pallas_call | solution.py:506
  101.9 38.3 %attn_bwd.1 = (bf16[16,208,1152]{2,1,0:T(8,128)(2,1)}, bf16[2,4,2,2,24,640]{5,4,3,2,1,0:T(8,128)(2,1)}, f32[16,384]{1,0:T(8,128)}, f32[24,1792]{1,0:T(8,128)}) custom-call(bf16[16,208,1152]{2,1,0:T(8,128)(2,1)} %get-tuple-element.64.qkv_ref, bf16[16,6,208,208]{3,2,1,0:T(8,128)(2,1)} %get-tuple-element.65.e_ref, ...), custom_call_target="tpu_custom_call" | custom-call | tf_op jit(solution)/shard_map/attn_bwd/pallas_call | solution.py:757
  140.2 24.0 %tokens_grad.1 = (f32[3152,384]{1,0:T(8,128)}, f32[24,640]{1,0:T(8,128)}, f32[16,384]{1,0:T(8,128)}) custom-call(bf16[16,208,1152]{2,1,0:T(8,128)(2,1)} %get-tuple-element.73.g_ref, f32[16,208,384]{2,1,0:T(8,128)} %get-tuple-element.68.normed_ref, f32[16,208,128]{2,1,0:T(8,128)} %get-tuple-element.74.inv_ref, f32[16,208,384]{2,1,0:T(8,128)} %get-tuple-element.75.gres_ref, ...), custom_call_target="tpu_custom_call" | custom-call | tf_op jit(solution)/shard_map/tokens_grad/pallas_call | solution.py:870
  164.2 1.7 split.1
  165.9 4.9 %copy.35 = f32[3152,384]{1,0:T(8,128)} copy(f32[3152,384]{1,0:T(8,128)} %get-tuple-element.115) | data formatting | bytes 9682944

commit v5 on v4

--- a/solution.py
+++ b/solution.py
@@ -534,7 +534,7 @@
 
 
 class Reduction:
-    def __init__(self, dims, copies, packed, bufs, cut):
+    def __init__(self, dims, copies, tag, packed, bufs, cut):
         self.dims, self.copies, self.packed, self.cut = dims, copies, packed, cut
         self.place = place_of(dims)
         self.along, self.other = peers_of(dims, self.place)
@@ -542,24 +542,24 @@
         self.p, self.a1, self.b1, self.ra1, self.rb1, self.ra2, self.rb2, self.f, self.rz = bufs
         low, high = pl.ds(0, cut), pl.ds(cut, packed.shape[-1] - cut)
         along = self.along
-        copies.plan("pair", [lambda: (packed.at[1 - mp], self.p, self.other)])
-        copies.plan("1l", [
+        copies.plan(tag + "pair", [lambda: (packed.at[1 - mp], self.p, self.other)])
+        copies.plan(tag + "1l", [
             lambda o=o, c=c, d=d: (self.p.at[EVERY, EVERY, c, EVERY, low], self.ra1.at[o], d)
             for o, (c, d) in enumerate(along["x"])
         ])
-        copies.plan("1h", [
+        copies.plan(tag + "1h", [
             lambda o=o, b=b, d=d: (self.p.at[EVERY, b, EVERY, EVERY, high], self.rb1.at[o], d)
             for o, (b, d) in enumerate(along["y"])
         ])
-        copies.plan("2l", [
+        copies.plan(tag + "2l", [
             lambda o=o, b=b, d=d: (self.a1.at[EVERY, b], self.ra2.at[o], d)
             for o, (b, d) in enumerate(along["y"])
         ])
-        copies.plan("2h", [
+        copies.plan(tag + "2h", [
             lambda o=o, c=c, d=d: (self.b1.at[EVERY, c], self.rb2.at[o], d)
             for o, (c, d) in enumerate(along["x"])
         ])
-        copies.plan("3", [
+        copies.plan(tag + "3", [
             lambda o=o, a=a, d=d: (self.f.at[a], self.rz.at[o], d)
             for o, (a, d) in enumerate(along["z"])
         ])
@@ -631,93 +631,109 @@
         return total
 
 
-def attn_bwd_kernel(
-    dims, n, qkv_ref, e_ref, mixed_ref, linv_ref, gmix_ref, normed_ref, w_ref, vec_ref, dvec2_ref,
-    dbup_ref, packed, *refs,
+def backward_kernel(
+    dims, n, qkv_ref, e_ref, mixed_ref, linv_ref, gmix_ref, normed_ref, inv_ref, gres_ref, w_ref,
+    vec_ref, dvec2_ref, dbup_ref, packed, gtok_ref, narrow_ref, wide_ref, total_ref, *refs,
 ):
-    g_ref, narrow_ref, sums_ref, sum_ref = refs[:4]
-    acc_ref, gsum_ref, bufs, mine, send, recv, sem = refs[4], refs[5], refs[6:15], *refs[15:]
+    g_ref, acc_ref, gsum_ref, narrow, sums, vs, vr = refs[:7]
+    wide_bufs, mine, narrow_bufs = refs[7:16], refs[16], refs[17:26]
+    send, recv, sem = refs[26:]
     i = pl.program_id(0)
     copies = Copies(send, recv)
-    red = Reduction(dims, copies, packed, bufs, WIDE_CUT)
-    keep = pltpu.make_async_copy(packed.at[red.place[3]], mine, sem)
+    wide = Reduction(dims, copies, "w", packed, wide_bufs, WIDE_CUT)
+    thin = Reduction(dims, copies, "n", narrow, narrow_bufs, NARROW_CUT)
+    mp = wide.place[3]
+    keep = pltpu.make_async_copy(packed.at[mp], mine, sem)
+    stages = [[wide.other], *([d for _, d in wide.along[axis]] for axis in "xyz")]
+    bases = [sum(len(s) for s in stages[:k]) for k in range(4)]
+    for k, devices in enumerate(stages):
+        copies.plan("v%d" % k, [
+            lambda k=k, o=o, d=d: (sums if k == 0 else vs.at[k - 1], vr.at[bases[k] + o], d)
+            for o, d in enumerate(devices)
+        ])
+
+    def vec_add(k):
+        total = sums[...] if k == 0 else vs[k - 1]
+        for o in range(len(stages[k])):
+            total = total + vr[bases[k] + o]
+        if k < 3:
+            vs[k] = total
+        else:
+            total_ref[...] = total
 
     @pl.when(i == 0)
     def _():
+        greet(wide.along, wide.other)
+        keep.start()
         acc_ref[...] = jnp.zeros_like(acc_ref)
         gsum_ref[...] = jnp.zeros_like(gsum_ref)
-        greet(red.along, red.other)
-        keep.start()
-
-    @pl.when(i == 1)
-    def _():
-        met(red.along)
-        copies.start("pair")
-
-    @pl.when(i == 3)
+        met(wide.along)
+        copies.start("wpair")
+
+    @pl.when(i == 2)
     def _():
         keep.wait()
-        copies.arrived("pair")
-        red.add_pair(mine)
-        copies.start("1l", "1h")
-
-    @pl.when(i == n // 2 - 1)
-    def _():
-        copies.arrived("1l", "1h")
-        red.add_first_low()
-        red.add_first_high()
-        copies.start("2l", "2h")
-
-    @pl.when(i == n // 2 + 2)
-    def _():
-        copies.arrived("2l", "2h")
-        red.add_second()
-        copies.start("3")
-
-    lane = lax.broadcasted_iota(jnp.int32, (SP, 2 * HD), 1)
-    zero = jnp.zeros((SP, 2 * HD), BF)
-    minus = jnp.full((SP, 2 * HD), -1.0, BF)
-    for p in range(PAIRS):
-        lo, hi = 2 * HD * p, 2 * HD * (p + 1)
-        q = qkv_ref[0, :, lo:hi]
-        k = qkv_ref[0, :, D + lo : D + hi]
-        v = qkv_ref[0, :, 2 * D + lo : 2 * D + hi]
-        go_f = gmix_ref[0, :, lo:hi].astype(F32) * linv_ref[0, :, lo:hi]
-        go = go_f.astype(BF)
-        god = jnp.concatenate(
-            [go, (go_f * mixed_ref[0, :, lo:hi].astype(F32)).astype(BF)], axis=1
-        )
-        gq = gk = gv = None
-        for h in range(2):
-            own = (lane < HD) if h == 0 else (lane >= HD)
-            e = e_ref[0, 2 * p + h]
-            vd = jnp.concatenate(
-                [jnp.where(own, v, zero), jnp.where(own, minus, zero)], axis=1
+        copies.arrived("wpair")
+        wide.add_pair(mine)
+        copies.start("w1l", "w1h")
+
+    @pl.when(i == n // 2)
+    def _():
+        copies.arrived("w1l", "w1h")
+        wide.add_first_low()
+        wide.add_first_high()
+        copies.start("w2l", "w2h")
+
+    @pl.when(i == (3 * n) // 4)
+    def _():
+        copies.arrived("w2l", "w2h")
+        wide.add_second()
+        copies.start("w3")
+
+    @pl.when(i < n)
+    def _():
+        lane = lax.broadcasted_iota(jnp.int32, (SP, 2 * HD), 1)
+        zero = jnp.zeros((SP, 2 * HD), BF)
+        minus = jnp.full((SP, 2 * HD), -1.0, BF)
+        for p in range(PAIRS):
+            lo, hi = 2 * HD * p, 2 * HD * (p + 1)
+            q = qkv_ref[0, :, lo:hi]
+            k = qkv_ref[0, :, D + lo : D + hi]
+            v = qkv_ref[0, :, 2 * D + lo : 2 * D + hi]
+            go_f = gmix_ref[0, :, lo:hi].astype(F32) * linv_ref[0, :, lo:hi]
+            go = go_f.astype(BF)
+            god = jnp.concatenate(
+                [go, (go_f * mixed_ref[0, :, lo:hi].astype(F32)).astype(BF)], axis=1
             )
-            ds = e * dot_nt(god, vd).astype(BF)
-            part_q = dot_nn(ds, jnp.where(own, k, zero))
-            part_k = dot_tn(ds, jnp.where(own, q, zero))
-            part_v = dot_tn(e, jnp.where(own, go, zero))
-            gq = part_q if gq is None else gq + part_q
-            gk = part_k if gk is None else gk + part_k
-            gv = part_v if gv is None else gv + part_v
-        gq = gq * (1.0 / math.sqrt(HD))
-        gk = gk * (1.0 / LOG2E)
-        for j, grad in enumerate((gq, gk, gv)):
-            gsum_ref[0:1, D * j + lo : D * j + hi] += row_sum(grad)
-            g_ref[0, :, D * j + lo : D * j + hi] = grad.astype(BF)
-    acc_ref[...] += dot_tn(normed_ref[0].astype(BF), g_ref[0])
+            gq = gk = gv = None
+            for h in range(2):
+                own = (lane < HD) if h == 0 else (lane >= HD)
+                e = e_ref[0, 2 * p + h]
+                vd = jnp.concatenate(
+                    [jnp.where(own, v, zero), jnp.where(own, minus, zero)], axis=1
+                )
+                ds = e * dot_nt(god, vd).astype(BF)
+                part_q = dot_nn(ds, jnp.where(own, k, zero))
+                part_k = dot_tn(ds, jnp.where(own, q, zero))
+                part_v = dot_tn(e, jnp.where(own, go, zero))
+                gq = part_q if gq is None else gq + part_q
+                gk = part_k if gk is None else gk + part_k
+                gv = part_v if gv is None else gv + part_v
+            gq = gq * (1.0 / math.sqrt(HD))
+            gk = gk * (1.0 / LOG2E)
+            for j, grad in enumerate((gq, gk, gv)):
+                gsum_ref[:, D * j + lo : D * j + hi] += fold(grad)
+                g_ref[i, :, D * j + lo : D * j + hi] = grad.astype(BF)
+        acc_ref[...] += dot_tn(normed_ref[0].astype(BF), g_ref[i])
 
     @pl.when(i == n - 1)
     def _():
-        copies.arrived("3")
-        sum_ref[...] = red.add_third()
         nz, ny, nx = dims
-        rows = narrow_ref.shape[4]
+        rows = narrow.shape[4]
         spots = [(a, b, c) for a in range(nz) for b in range(ny) for c in range(nx)]
         group = 48 // rows
         turned = vec_ref[...].T
-        gsum = gsum_ref[0:1, :]
+        gsum = row_sum(gsum_ref[...])
         gains = []
         for t in range(len(spots) // group):
             at = slice(48 * t, 48 * (t + 1))
@@ -729,169 +745,121 @@
                 parts.append(jnp.zeros((48, NARROW - 3 * THIRD), F32))
                 block = jnp.concatenate(parts, axis=1)
                 for k in range(group):
-                    narrow_ref[(m,) + spots[t * group + k]] = block[
+                    narrow[(m,) + spots[t * group + k]] = block[
                         k * rows : (k + 1) * rows
                     ].astype(BF)
         high = gsum.astype(BF)
         low = (gsum - high.astype(F32)).astype(BF)
         row = lax.broadcasted_iota(jnp.int32, (16, 3 * D), 0)
         both = jnp.where(row == 0, high, jnp.where(row == 1, low, jnp.zeros((16, 3 * D), BF)))
-        sums_ref[0:1] = gsum[:, :D]
-        sums_ref[1:2] = gsum[:, 2 * D :]
+        sums[0:1] = gsum[:, :D]
+        sums[1:2] = gsum[:, 2 * D :]
         gain = jnp.broadcast_to(jnp.concatenate(gains, axis=0), (D, 128)).T
-        sums_ref[2:3] = gain[0:1, :]
-        sums_ref[3:4] = row_sum(dot_nt(both, w_ref[...]))
-        sums_ref[4:8] = dvec2_ref[0:4]
+        sums[2:3] = gain[0:1, :]
+        sums[3:4] = row_sum(dot_nt(both, w_ref[...]))
+        sums[4:8] = dvec2_ref[0:4]
         for j in range(FF // D):
-            sums_ref[8 + j : 9 + j] = dbup_ref[:, D * j : D * (j + 1)]
-        sums_ref[12:16] = jnp.zeros((4, D), F32)
+            sums[8 + j : 9 + j] = dbup_ref[:, D * j : D * (j + 1)]
+        sums[12:16] = jnp.zeros((4, D), F32)
+        copies.start("npair", "v0")
+
+    @pl.when(i == n + 3)
+    def _():
+        copies.arrived("npair", "v0")
+        thin.add_pair(narrow.at[mp])
+        vec_add(0)
+        copies.start("n1l", "n1h", "v1")
+
+    @pl.when(i == n + 5)
+    def _():
+        copies.arrived("w3")
+        wide_ref[...] = wide.add_third()
+
+    @pl.when(i == n + 8)
+    def _():
+        copies.arrived("n1l", "v1")
+        thin.add_first_low()
+        vec_add(1)
+        copies.start("n2l", "v2")
+        copies.arrived("n1h")
+        thin.add_first_high()
+        copies.start("n2h")
+
+    @pl.when(i == n + 12)
+    def _():
+        copies.arrived("n2l", "n2h", "v2")
+        thin.add_second()
+        vec_add(2)
+        copies.start("n3", "v3")
+
+    @pl.when(i >= n)
+    def _():
+        image = i - n
+        inv = inv_ref[0]
+        inv = jnp.concatenate([inv, inv, inv], axis=1)
+        gh1 = dot_nt(g_ref[jnp.maximum(image, 0)], w_ref[...])
+        gtok = gres_ref[0] + norm_backward(gh1, normed_ref[0], inv, vec_ref[0:1, :])
+        store_image(gtok_ref, jnp.maximum(image, 0), gtok)
+
+    @pl.when(i == 2 * n - 1)
+    def _():
+        copies.arrived("n3", "v3")
+        narrow_ref[...] = thin.add_third()
+        vec_add(3)
         copies.left(*copies.groups)
 
 
-def attn_bwd(qkv, e, mixed, linv, gmix, normed, wqkv, vec, dvec2, dbup, packed, dp):
+def backward(qkv, e, mixed, linv, gmix, normed, inv, gres, wqkv, vec, dvec2, dbup, packed, tall, dp):
     dims = chip_grid(dp)
+    nz, ny, nx = dims
     n = qkv.shape[0]
     rows = D // dp
-    count = Reduction.count(dims)
-    narrow = (2, *dims, rows, NARROW)
+    count = 2 * Reduction.count(dims) + nz + ny + nx - 2
+
+    def heads(*shape):
+        return pl.BlockSpec((1, *shape), lambda i: (jnp.minimum(i, n - 1),) + (0,) * len(shape))
+
+    def after(*shape):
+        return pl.BlockSpec((1, *shape), lambda i: (jnp.maximum(i - n, 0),) + (0,) * len(shape))
+
+    def twice(*shape):
+        return pl.BlockSpec((1, *shape), lambda i: (i % n,) + (0,) * len(shape))
+
     return pl.pallas_call(
-        functools.partial(attn_bwd_kernel, dims, n),
-        grid=(n,),
+        functools.partial(backward_kernel, dims, n),
+        grid=(2 * n,),
         in_specs=[
-            per_image(SP, 3 * D), per_image(HEADS, SP, SP), per_image(SP, D), per_image(SP, D),
-            per_image(SP, D), per_image(SP, D), whole((D, 3 * D)), whole((8, D)), whole((8, D)),
-            whole((1, FF)), pl.BlockSpec(memory_space=pl.ANY),
+            heads(SP, 3 * D), heads(HEADS, SP, SP), heads(SP, D), heads(SP, D), heads(SP, D),
+            twice(SP, D), after(SP, 128), after(SP, D), whole((D, 3 * D)), whole((8, D)),
+            whole((8, D)), whole((1, FF)), pl.BlockSpec(memory_space=pl.ANY),
         ],
         out_specs=[
-            per_image(SP, 3 * D), whole(narrow), whole((16, D)), whole((rows, WIDE)),
+            whole((tall, D)), whole((rows, NARROW)), whole((rows, WIDE)), whole((16, D)),
         ],
         out_shape=[
-            jax.ShapeDtypeStruct((n, SP, 3 * D), BF),
-            jax.ShapeDtypeStruct(narrow, BF),
+            jax.ShapeDtypeStruct((tall, D), F32),
+            jax.ShapeDtypeStruct((rows, NARROW), F32),
+            jax.ShapeDtypeStruct((rows, WIDE), F32),
             jax.ShapeDtypeStruct((16, D), F32),
-            jax.ShapeDtypeStruct((rows, WIDE), F32),
         ],
         scratch_shapes=[
+            pltpu.VMEM((n, SP, 3 * D), BF),
             pltpu.VMEM((D, 3 * D), F32),
             pltpu.VMEM((8, 3 * D), F32),
+            pltpu.VMEM((2, *dims, rows, NARROW), BF),
+            pltpu.VMEM((16, D), F32),
+            pltpu.VMEM((3, 16, D), F32),
+            pltpu.VMEM((nz + ny + nx - 2, 16, D), F32),
             *Reduction.scratch(dims, rows, WIDE, WIDE_CUT),
             pltpu.VMEM((*dims, rows, WIDE), BF),
+            *Reduction.scratch(dims, rows, NARROW, NARROW_CUT),
             pltpu.SemaphoreType.DMA((count,)),
             pltpu.SemaphoreType.DMA((count,)),
             pltpu.SemaphoreType.DMA,
         ],
         compiler_params=params(collective_id=1),
-        name="attn_bwd",
-    )(qkv, e, mixed, linv, gmix, normed, wqkv, vec, dvec2, dbup, packed)
-
-
-def tokens_kernel(
-    dims, n, g_ref, normed_ref, inv_ref, gres_ref, w_ref, vec_ref, sums, packed, *refs
-):
-    gtok_ref, sum_ref, total_ref = refs[:3]
-    bufs, mine, vs, vr, send, recv, sem = refs[3:12], *refs[12:]
-    i = pl.program_id(0)
-    copies = Copies(send, recv)
-    red = Reduction(dims, copies, packed, bufs, NARROW_CUT)
-    keep = pltpu.make_async_copy(packed.at[red.place[3]], mine, sem)
-    stages = [[red.other], *([d for _, d in red.along[axis]] for axis in "xyz")]
-    bases = [sum(len(s) for s in stages[:k]) for k in range(4)]
-    for k, devices in enumerate(stages):
-        copies.plan("v%d" % k, [
-            lambda k=k, o=o, d=d: (sums if k == 0 else vs.at[k - 1], vr.at[bases[k] + o], d)
-            for o, d in enumerate(devices)
-        ])
-
-    def vec_add(k):
-        total = sums[...] if k == 0 else vs[k - 1]
-        for o in range(len(stages[k])):
-            total = total + vr[bases[k] + o]
-        if k < 3:
-            vs[k] = total
-        else:
-            total_ref[...] = total
-
-    @pl.when(i == 0)
-    def _():
-        greet(red.along, red.other)
-        keep.start()
-
-    @pl.when(i == 2)
-    def _():
-        met(red.along)
-        copies.start("pair", "v0")
-
-    @pl.when(i == 5)
-    def _():
-        keep.wait()
-        copies.arrived("pair", "v0")
-        red.add_pair(mine)
-        vec_add(0)
-        copies.start("1l", "1h", "v1")
-
-    @pl.when(i == n - 6)
-    def _():
-        copies.arrived("1l", "v1")
-        red.add_first_low()
-        vec_add(1)
-        copies.start("2l", "v2")
-        copies.arrived("1h")
-        red.add_first_high()
-        copies.start("2h")
-
-    @pl.when(i == n - 2)
-    def _():
-        copies.arrived("2l", "2h", "v2")
-        red.add_second()
-        vec_add(2)
-        copies.start("3", "v3")
-
-    inv = inv_ref[0]
-    inv = jnp.concatenate([inv, inv, inv], axis=1)
-    gh1 = dot_nt(g_ref[0], w_ref[...])
-    store_image(
-        gtok_ref, i, gres_ref[0] + norm_backward(gh1, normed_ref[0], inv, vec_ref[0:1, :])
-    )
-
-    @pl.when(i == n - 1)
-    def _():
-        copies.arrived("3", "v3")
-        sum_ref[...] = red.add_third()
-        vec_add(3)
-        copies.left(*copies.groups)
-
-
-def tokens_grad(g, normed, inv, gres, wqkv, vec, sums, packed, rows, dp):
-    dims = chip_grid(dp)
-    nz, ny, nx = dims
-    n = g.shape[0]
-    part = D // dp
-    count = Reduction.count(dims) + nz + ny + nx - 2
-    return pl.pallas_call(
-        functools.partial(tokens_kernel, dims, n),
-        grid=(n,),
-        in_specs=[
-            per_image(SP, 3 * D), per_image(SP, D), per_image(SP, 128), per_image(SP, D),
-            whole((D, 3 * D)), whole((8, D)), whole((16, D)), pl.BlockSpec(memory_space=pl.ANY),
-        ],
-        out_specs=[whole((rows, D)), whole((part, NARROW)), whole((16, D))],
-        out_shape=[
-            jax.ShapeDtypeStruct((rows, D), F32),
-            jax.ShapeDtypeStruct((part, NARROW), F32),
-            jax.ShapeDtypeStruct((16, D), F32),
-        ],
-        scratch_shapes=[
-            *Reduction.scratch(dims, part, NARROW, NARROW_CUT),
-            pltpu.VMEM((*dims, part, NARROW), BF),
-            pltpu.VMEM((3, 16, D), F32),
-            pltpu.VMEM((nz + ny + nx - 2, 16, D), F32),
-            pltpu.SemaphoreType.DMA((count,)),
-            pltpu.SemaphoreType.DMA((count,)),
-            pltpu.SemaphoreType.DMA,
-        ],
-        compiler_params=params(collective_id=2),
-        name="tokens_grad",
-    )(g, normed, inv, gres, wqkv, vec, sums, packed)
+        name="backward",
+    )(qkv, e, mixed, linv, gmix, normed, inv, gres, wqkv, vec, dvec2, dbup, packed)
 
 
 def split_kernel(n, narrow_ref, wide_ref, vec_ref, *outs):
@@ -951,11 +919,9 @@
     out, gres, gmix, packed, dvec2, dbup = mlp(
         tok, cot, mixed, wide.reshape(2, D, WIDE), vec, bup, tokens.shape[0], dp
     )
-    g, packed, sums, wide_sum = attn_bwd(
-        qkv, e, mixed, linv, gmix, normed, wqkv, vec, dvec2, dbup, packed, dp
-    )
-    gtok, narrow_sum, sums = tokens_grad(
-        g, normed, inv, gres, wqkv, vec, sums, packed, tokens.shape[0], dp
+    gtok, narrow_sum, wide_sum, sums = backward(
+        qkv, e, mixed, linv, gmix, normed, inv, gres, wqkv, vec, dvec2, dbup, packed,
+        tokens.shape[0], dp,
     )
     grads = split(narrow_sum, wide_sum, sums, dp * lax.axis_size("mp"))
     vecs = [v.reshape(-1) for v in grads[6:]]

time: 171 us -> 167 us (0.977)
  Pallas kernels: 165 us -> 161 us
    pallas_call x2 -> x1, Pallas kernels: 62.3 us -> 58.3 us  [backward(): pl.pallas_call(functools.partial(backward_kernel, dims, n), grid=(2 * n,)...]
where the time goes in v5:
time: 167 us
  Pallas kernels  161 us (96%)
  local copies, waits for them, and re-layouts  4.91 us (3%)
    pallas_call x1, Pallas kernels, backward(): pl.pallas_call(functools.partial(backward_kernel, dims, n), grid=(2 * n,)...  58.3 us
    pallas_call x1, Pallas kernels, mlp(): pl.pallas_call(functools.partial(mlp_kernel, dims, n), grid=(n,), in_spec...  53.9 us
    pallas_call x1, Pallas kernels, attn_fwd(): pl.pallas_call(functools.partial(attn_fwd_kernel, dims, n), grid=(n,), in...  47.2 us
    unnamed x1, local copies, waits for them, and re-layouts  4.91 us

profile of v5, /device:TPU:0, one launch (start us, length us, event | category | flops | bytes accessed | tf_op | source)
XLA Modules:
  0.0 166.7 jit_solution(2636262890743673910)
XLA Ops:
  0.7 47.2 %attn_fwd.1 = (bf16[16,208,1152]{2,1,0:T(8,128)(2,1)}, bf16[16,6,208,208]{3,2,1,0:T(8,128)(2,1)}, bf16[16,208,384]{2,1,0:T(8,128)(2,1)}, f32[16,208,384]{2,1,0:T...) custom-call(bf16[24,192]{1,0:T(8,128)(2,1)} %refs_0_.1, ...), custom_call_target="tpu_custom_call" | custom-call | tf_op jit(solution)/shard_map/attn_fwd/pallas_call | solution.py:341
  47.9 53.9 %mlp.1 = (bf16[3152,384]{1,0:T(8,128)(2,1)}, f32[16,208,384]{2,1,0:T(8,128)}, bf16[16,208,384]{2,1,0:T(8,128)(2,1)}, bf16[2,4,2,2,24,1792]{5,4,3,2,1,0:T(8,128)(...) custom-call(bf16[16,208,384]{2,1,0:T(8,128)(2,1)} %get-tuple-element.54.tok_ref, ...), custom_call_target="tpu_custom_call" | custom-call | tf_op jit(solution)/shard_map/mlp/pallas_call | solution.py:506
  101.8 58.3 %backward.1 = (f32[3152,384]{1,0:T(8,128)}, f32[24,640]{1,0:T(8,128)}, f32[24,1792]{1,0:T(8,128)}, f32[16,384]{1,0:T(8,128)}) custom-call(bf16[16,208,1152]{2,1,0:T(8,128)(2,1)} %get-tuple-element.61.qkv_ref, bf16[16,6,208,208]{3,2,1,0:T(8,128)(2,1)} %get-tuple-element.62.e_ref, bf16[16,208,384]{2,1,0:T(8,128)(2,1)} %get-tuple-element.56.mixed_ref, ...), custom_call_target="tpu_custom_call" | custom-call | tf_op jit(solution)/shard_map/backward/pallas_call | solution.py:828
  160.1 1.7 %split.1 = (f32[24,192]{1,0:T(8,128)}, f32[24,192]{1,0:T(8,128)}, f32[24,192]{1,0:T(8,128)}, f32[24,192]{1,0:T(8,128)}, f32[24,768]{1,0:T(8,128)}, /*index=5*/f3...) custom-call(f32[24,640]{1,0:T(8,128)} %get-tuple-element.73.narrow_r, ...), custom_call_target="tpu_custom_call" | custom-call | tf_op jit(solution)/shard_map/split/pallas_call | solution.py:885
  161.8 4.9 %copy.35 = f32[3152,384]{1,0:T(8,128)} copy(f32[3152,384]{1,0:T(8,128)} %get-tuple-element.109) | data formatting | bytes 9682944

commit v6 on v5

--- a/solution.py
+++ b/solution.py
@@ -17,6 +17,7 @@
 
 SP = 208
 WIN = 224
+G = 2
 
 EPS = 1e-06
 RSQRT2 = 0.7071067811865476
@@ -205,6 +206,7 @@
     ) = refs[17:29]
     narrow, v, own, normed_all, inv_all, tok_all, cot_all, send, recv, sem = refs[29:]
     i = pl.program_id(0)
+    steps = n // G
     nz, ny, nx = dims
     place = place_of(dims)
     z, y, x, mp = place
@@ -281,51 +283,54 @@
                     [half[:, cols] for half in block], axis=1
                 ).astype(BF)
 
-    @pl.when(i == 3)
+    @pl.when(i == 2)
     def _():
         copies.arrived("w2l", "w2h")
         copies.start("w3l", "w3h", "ws2l", "ws2h")
 
-    normed = normed_all[i]
-    normed_ref[0] = normed
-    inv_ref[0] = inv_all[i]
-    tokp_ref[0] = tok_all[i]
-    cotp_ref[0] = cot_all[i]
-    h1 = (normed * vec_ref[0:1, :] + vec_ref[1:2, :]).astype(BF)
+    images = pl.ds(G * i, G)
+    normed = normed_all[images]
+    normed_ref[...] = normed
+    inv_ref[...] = inv_all[images]
+    tokp_ref[...] = tok_all[images]
+    cotp_ref[...] = cot_all[images]
+    h1 = (normed * vec_ref[0:1, :] + vec_ref[1:2, :]).astype(BF).reshape(G * SP, D)
     q = ((dot_nn(h1, w_ref[:, 0:D]) + vec_ref[2:3, :]) * Q_SCALE).astype(BF)
     k = dot_nn(h1, w_ref[:, D : 2 * D]).astype(BF)
     value = (dot_nn(h1, w_ref[:, 2 * D :]) + vec_ref[3:4, :]).astype(BF)
-    qkv_ref[0, :, 0:D] = q
-    qkv_ref[0, :, D : 2 * D] = k
-    qkv_ref[0, :, 2 * D :] = value
+    for j, x in enumerate((q, k, value)):
+        for b in range(G):
+            qkv_ref[b, :, D * j : D * (j + 1)] = x[SP * b : SP * (b + 1)]
     lane = lax.broadcasted_iota(jnp.int32, (SP, 2 * HD), 1)
     is_key = lax.broadcasted_iota(jnp.int32, (SP, SP), 1) < S
     zero = jnp.zeros((SP, 2 * HD), BF)
     one = jnp.ones((SP, 2 * HD), BF)
     for p in range(PAIRS):
         cols = slice(2 * HD * p, 2 * HD * (p + 1))
-        total = None
-        for h in range(2):
-            mine = (lane < HD) if h == 0 else (lane >= HD)
-            kh = jnp.where(mine, k[:, cols], zero)
-            vh = jnp.where(mine, value[:, cols], zero)
-            scores = dot_nt(q[:, cols], kh)
-            scores = jnp.where(is_key, scores, -1e30)
-            top = jnp.max(scores, axis=-1, keepdims=True)
-            e = jnp.exp2(scores - top).astype(BF)
-            e_ref[0, 2 * p + h] = e
-            part = dot_nn(e, jnp.concatenate([vh, jnp.where(mine, one, zero)], axis=1))
-            total = part if total is None else total + part
-        linv = 1.0 / total[:, 2 * HD :]
-        linv_ref[0, :, cols] = linv
-        mixed_ref[0, :, cols] = (total[:, : 2 * HD] * linv).astype(BF)
-
-    @pl.when(i == n - 5)
+        for b in range(G):
+            qp, kp, vp = (x[SP * b : SP * (b + 1), cols] for x in (q, k, value))
+            total = None
+            for h in range(2):
+                mine = (lane < HD) if h == 0 else (lane >= HD)
+                kh = jnp.where(mine, kp, zero)
+                vh = jnp.where(mine, vp, zero)
+                scores = dot_nt(qp, kh)
+                scores = jnp.where(is_key, scores, -1e30)
+                top = jnp.max(scores, axis=-1, keepdims=True)
+                e = jnp.exp2(scores - top).astype(BF)
+                e_ref[b, 2 * p + h] = e
+                part = dot_nn(e, jnp.concatenate([vh, jnp.where(mine, one, zero)], axis=1))
+                total = part if total is None else total + part
+            linv = 1.0 / total[:, 2 * HD :]
+            linv_ref[b, :, cols] = linv
+            mixed_ref[b, :, cols] = (total[:, : 2 * HD] * linv).astype(BF)
+
+    @pl.when(i == steps - 2)
     def _():
         copies.arrived("w3l", "w3h")
         copies.start("ws3l", "ws3h")
 
-    @pl.when(i == n - 1)
+    @pl.when(i == steps - 1)
     def _():
         copies.arrived("ws1", "ws2l", "ws2h", "ws3l", "ws3h")
         copies.left(*copies.groups)
@@ -340,11 +345,11 @@
     inputs = (*mats, *vectors, bup, tokens, cot)
     return pl.pallas_call(
         functools.partial(attn_fwd_kernel, dims, n),
-        grid=(n,),
+        grid=(n // G,),
         in_specs=[whole(a.shape) for a in inputs],
         out_specs=[
-            per_image(SP, 3 * D), per_image(HEADS, SP, SP), per_image(SP, D), per_image(SP, D),
-            per_image(SP, D), per_image(SP, 128), per_image(SP, D), per_image(SP, D),
+            per_step(SP, 3 * D), per_step(HEADS, SP, SP), per_step(SP, D), per_step(SP, D),
+            per_step(SP, D), per_step(SP, 128), per_step(SP, D), per_step(SP, D),
             whole((D, 3 * D)), whole((8, D)), whole((1, FF)), pl.BlockSpec(memory_space=pl.ANY),
         ],
         out_shape=[
@@ -639,6 +644,7 @@
     wide_bufs, mine, narrow_bufs = refs[7:16], refs[16], refs[17:26]
     send, recv, sem = refs[26:]
     i = pl.program_id(0)
+    steps = n // G
     copies = Copies(send, recv)
     wide = Reduction(dims, copies, "w", packed, wide_bufs, WIDE_CUT)
     thin = Reduction(dims, copies, "n", narrow, narrow_bufs, NARROW_CUT)
@@ -670,63 +676,64 @@
         met(wide.along)
         copies.start("wpair")
 
-    @pl.when(i == 2)
+    @pl.when(i == 1)
     def _():
         keep.wait()
         copies.arrived("wpair")
         wide.add_pair(mine)
         copies.start("w1l", "w1h")
 
-    @pl.when(i == n // 2)
+    @pl.when(i == steps // 2)
     def _():
         copies.arrived("w1l", "w1h")
         wide.add_first_low()
         wide.add_first_high()
         copies.start("w2l", "w2h")
 
-    @pl.when(i == (3 * n) // 4)
+    @pl.when(i == (3 * steps) // 4)
     def _():
         copies.arrived("w2l", "w2h")
         wide.add_second()
         copies.start("w3")
 
-    @pl.when(i < n)
+    @pl.when(i < steps)
     def _():
         lane = lax.broadcasted_iota(jnp.int32, (SP, 2 * HD), 1)
         zero = jnp.zeros((SP, 2 * HD), BF)
         minus = jnp.full((SP, 2 * HD), -1.0, BF)
         for p in range(PAIRS):
             lo, hi = 2 * HD * p, 2 * HD * (p + 1)
-            q = qkv_ref[0, :, lo:hi]
-            k = qkv_ref[0, :, D + lo : D + hi]
-            v = qkv_ref[0, :, 2 * D + lo : 2 * D + hi]
-            go_f = gmix_ref[0, :, lo:hi].astype(F32) * linv_ref[0, :, lo:hi]
-            go = go_f.astype(BF)
-            god = jnp.concatenate(
-                [go, (go_f * mixed_ref[0, :, lo:hi].astype(F32)).astype(BF)], axis=1
-            )
-            gq = gk = gv = None
-            for h in range(2):
-                own = (lane < HD) if h == 0 else (lane >= HD)
-                e = e_ref[0, 2 * p + h]
-                vd = jnp.concatenate(
-                    [jnp.where(own, v, zero), jnp.where(own, minus, zero)], axis=1
+            for b in range(G):
+                q = qkv_ref[b, :, lo:hi]
+                k = qkv_ref[b, :, D + lo : D + hi]
+                v = qkv_ref[b, :, 2 * D + lo : 2 * D + hi]
+                go_f = gmix_ref[b, :, lo:hi].astype(F32) * linv_ref[b, :, lo:hi]
+                go = go_f.astype(BF)
+                god = jnp.concatenate(
+                    [go, (go_f * mixed_ref[b, :, lo:hi].astype(F32)).astype(BF)], axis=1
                 )
-                ds = e * dot_nt(god, vd).astype(BF)
-                part_q = dot_nn(ds, jnp.where(own, k, zero))
-                part_k = dot_tn(ds, jnp.where(own, q, zero))
-                part_v = dot_tn(e, jnp.where(own, go, zero))
-                gq = part_q if gq is None else gq + part_q
-                gk = part_k if gk is None else gk + part_k
-                gv = part_v if gv is None else gv + part_v
-            gq = gq * (1.0 / math.sqrt(HD))
-            gk = gk * (1.0 / LOG2E)
-            for j, grad in enumerate((gq, gk, gv)):
-                gsum_ref[:, D * j + lo : D * j + hi] += fold(grad)
-                g_ref[i, :, D * j + lo : D * j + hi] = grad.astype(BF)
-        acc_ref[...] += dot_tn(normed_ref[0].astype(BF), g_ref[i])
-
-    @pl.when(i == n - 1)
+                gq = gk = gv = None
+                for h in range(2):
+                    own = (lane < HD) if h == 0 else (lane >= HD)
+                    e = e_ref[b, 2 * p + h]
+                    vd = jnp.concatenate(
+                        [jnp.where(own, v, zero), jnp.where(own, minus, zero)], axis=1
+                    )
+                    ds = e * dot_nt(god, vd).astype(BF)
+                    part_q = dot_nn(ds, jnp.where(own, k, zero))
+                    part_k = dot_tn(ds, jnp.where(own, q, zero))
+                    part_v = dot_tn(e, jnp.where(own, go, zero))
+                    gq = part_q if gq is None else gq + part_q
+                    gk = part_k if gk is None else gk + part_k
+                    gv = part_v if gv is None else gv + part_v
+                gq = gq * (1.0 / math.sqrt(HD))
+                gk = gk * (1.0 / LOG2E)
+                for j, grad in enumerate((gq, gk, gv)):
+                    gsum_ref[:, D * j + lo : D * j + hi] += fold(grad)
+                    g_ref[i, SP * b : SP * (b + 1), D * j + lo : D * j + hi] = grad.astype(BF)
+        acc_ref[...] += dot_tn(normed_ref[...].reshape(G * SP, D).astype(BF), g_ref[i])
+
+    @pl.when(i == steps - 1)
     def _():
         nz, ny, nx = dims
         rows = narrow.shape[4]
@@ -763,19 +770,19 @@
         sums[12:16] = jnp.zeros((4, D), F32)
         copies.start("npair", "v0")
 
-    @pl.when(i == n + 3)
+    @pl.when(i == steps + 2)
     def _():
         copies.arrived("npair", "v0")
         thin.add_pair(narrow.at[mp])
         vec_add(0)
         copies.start("n1l", "n1h", "v1")
 
-    @pl.when(i == n + 5)
+    @pl.when(i == steps + 3)
     def _():
         copies.arrived("w3")
         wide_ref[...] = wide.add_third()
 
-    @pl.when(i == n + 8)
+    @pl.when(i == steps + 4)
     def _():
         copies.arrived("n1l", "v1")
         thin.add_first_low()
@@ -785,23 +792,29 @@
         thin.add_first_high()
         copies.start("n2h")
 
-    @pl.when(i == n + 12)
+    @pl.when(i == steps + 6)
     def _():
         copies.arrived("n2l", "n2h", "v2")
         thin.add_second()
         vec_add(2)
         copies.start("n3", "v3")
 
-    @pl.when(i >= n)
-    def _():
-        image = i - n
-        inv = inv_ref[0]
-        inv = jnp.concatenate([inv, inv, inv], axis=1)
-        gh1 = dot_nt(g_ref[jnp.maximum(image, 0)], w_ref[...])
-        gtok = gres_ref[0] + norm_backward(gh1, normed_ref[0], inv, vec_ref[0:1, :])
-        store_image(gtok_ref, jnp.maximum(image, 0), gtok)
-
-    @pl.when(i == 2 * n - 1)
+    @pl.when(i >= steps)
+    def _():
+        group = jnp.maximum(i - steps, 0)
+        gh1 = dot_nt(g_ref[group], w_ref[...])
+        for b in range(G):
+            parts = []
+            for c in range(0, SP, CHUNK):
+                at = slice(c, c + CHUNK)
+                back = norm_backward(
+                    gh1[SP * b + c : SP * b + c + CHUNK], normed_ref[b, at, :],
+                    inv_ref[b, at, 0:1], vec_ref[0:1, :],
+                )
+                parts.append(gres_ref[b, at, :] + back)
+            store_image(gtok_ref, G * group + b, jnp.concatenate(parts, axis=0))
+
+    @pl.when(i == 2 * steps - 1)
     def _():
         copies.arrived("n3", "v3")
         narrow_ref[...] = thin.add_third()
@@ -813,21 +826,22 @@
     dims = chip_grid(dp)
     nz, ny, nx = dims
     n = qkv.shape[0]
+    steps = n // G
     rows = D // dp
     count = 2 * Reduction.count(dims) + nz + ny + nx - 2
 
     def heads(*shape):
-        return pl.BlockSpec((1, *shape), lambda i: (jnp.minimum(i, n - 1),) + (0,) * len(shape))
+        return pl.BlockSpec((G, *shape), lambda i: (jnp.minimum(i, steps - 1),) + (0,) * len(shape))
 
     def after(*shape):
-        return pl.BlockSpec((1, *shape), lambda i: (jnp.maximum(i - n, 0),) + (0,) * len(shape))
+        return pl.BlockSpec((G, *shape), lambda i: (jnp.maximum(i - steps, 0),) + (0,) * len(shape))
 
     def twice(*shape):
-        return pl.BlockSpec((1, *shape), lambda i: (i % n,) + (0,) * len(shape))
+        return pl.BlockSpec((G, *shape), lambda i: (i % steps,) + (0,) * len(shape))
 
     return pl.pallas_call(
         functools.partial(backward_kernel, dims, n),
-        grid=(2 * n,),
+        grid=(2 * steps,),
         in_specs=[
             heads(SP, 3 * D), heads(HEADS, SP, SP), heads(SP, D), heads(SP, D), heads(SP, D),
             twice(SP, D), after(SP, 128), after(SP, D), whole((D, 3 * D)), whole((8, D)),
@@ -843,7 +857,7 @@
             jax.ShapeDtypeStruct((16, D), F32),
         ],
         scratch_shapes=[
-            pltpu.VMEM((n, SP, 3 * D), BF),
+            pltpu.VMEM((steps, G * SP, 3 * D), BF),
             pltpu.VMEM((D, 3 * D), F32),
             pltpu.VMEM((8, 3 * D), F32),
             pltpu.VMEM((2, *dims, rows, NARROW), BF),
@@ -897,6 +911,10 @@
 
 def per_image(*shape):
     return pl.BlockSpec((1, *shape), lambda i: (i,) + (0,) * len(shape))
+
+
+def per_step(*shape):
+    return pl.BlockSpec((G, *shape), lambda i: (i,) + (0,) * len(shape))
 
 
 def params(collective_id=None):

time: 167 us -> 160 us (0.958)
  Pallas kernels: 161 us -> 154 us
    pallas_call x2, Pallas kernels: 105 us -> 98.5 us  [the longest x1 53.4 us: backward(): pl.pallas_call(functools.partial(backward_kernel, dims, n), grid=(2 * ste...]
where the time goes in v6:
time: 160 us
  Pallas kernels  154 us (96%)
  local copies, waits for them, and re-layouts  4.91 us (3%)
    pallas_call x1, Pallas kernels, mlp(): pl.pallas_call(functools.partial(mlp_kernel, dims, n), grid=(n,), in_spec...  53.9 us
    pallas_call x1, Pallas kernels, backward(): pl.pallas_call(functools.partial(backward_kernel, dims, n), grid=(2 * ste...  53.4 us
    pallas_call x1, Pallas kernels, attn_fwd(): pl.pallas_call(functools.partial(attn_fwd_kernel, dims, n), grid=(n // G,...  45.1 us
    unnamed x1, local copies, waits for them, and re-layouts  4.91 us

profile of v6, /device:TPU:0, one launch (start us, length us, event | category | flops | bytes accessed | tf_op | source)
XLA Modules:
  0.0 159.7 jit_solution(5327376921503555686)
XLA Ops:
  0.7 45.1 %attn_fwd.1 = (bf16[16,208,1152]{2,1,0:T(8,128)(2,1)}, bf16[16,6,208,208]{3,2,1,0:T(8,128)(2,1)}, bf16[16,208,384]{2,1,0:T(8,128)(2,1)}, f32[16,208,384]{2,1,0:T...) custom-call(bf16[24,192]{1,0:T(8,128)(2,1)} %refs_0_.1, ...), custom_call_target="tpu_custom_call" | custom-call | tf_op jit(solution)/shard_map/attn_fwd/pallas_call | solution.py:346
  45.8 53.9 %mlp.1 = (bf16[3152,384]{1,0:T(8,128)(2,1)}, f32[16,208,384]{2,1,0:T(8,128)}, bf16[16,208,384]{2,1,0:T(8,128)(2,1)}, bf16[2,4,2,2,24,1792]{5,4,3,2,1,0:T(8,128)(...) custom-call(bf16[16,208,384]{2,1,0:T(8,128)(2,1)} %get-tuple-element.54.tok_ref, ...), custom_call_target="tpu_custom_call" | custom-call | tf_op jit(solution)/shard_map/mlp/pallas_call | solution.py:511
  99.7 53.4 %backward.1 = (f32[3152,384]{1,0:T(8,128)}, f32[24,640]{1,0:T(8,128)}, f32[24,1792]{1,0:T(8,128)}, f32[16,384]{1,0:T(8,128)}) custom-call(bf16[16,208,1152]{2,1,0:T(8,128)(2,1)} %get-tuple-element.61.qkv_ref, bf16[16,6,208,208]{3,2,1,0:T(8,128)(2,1)} %get-tuple-element.62.e_ref, bf16[16,208,384]{2,1,0:T(8,128)(2,1)} %get-tuple-element.56.mixed_ref, ...), custom_call_target="tpu_custom_call" | custom-call | tf_op jit(solution)/shard_map/backward/pallas_call | solution.py:842
  153.1 1.7 %split.1 = (f32[24,192]{1,0:T(8,128)}, f32[24,192]{1,0:T(8,128)}, f32[24,192]{1,0:T(8,128)}, f32[24,192]{1,0:T(8,128)}, f32[24,768]{1,0:T(8,128)}, /*index=5*/f3...) custom-call(f32[24,640]{1,0:T(8,128)} %get-tuple-element.73.narrow_r, ...), custom_call_target="tpu_custom_call" | custom-call | tf_op jit(solution)/shard_map/split/pallas_call | solution.py:899
  154.8 4.9 %copy.35 = f32[3152,384]{1,0:T(8,128)} copy(f32[3152,384]{1,0:T(8,128)} %get-tuple-element.109) | data formatting | bytes 9682944

commit v7 on v6

--- a/solution.py
+++ b/solution.py
@@ -199,12 +199,12 @@
 
 def attn_fwd_kernel(dims, n, *refs):
     (wq, wk, wv, wot, wu, wdt), vectors, bup_in = refs[:6], refs[6:14], refs[14]
-    tok_ref, cot_ref = refs[15:17]
+    tok_hbm, cot_hbm = refs[15:17]
     (
         qkv_ref, e_ref, mixed_ref, linv_ref, normed_ref, inv_ref, tokp_ref, cotp_ref, w_ref, vec_ref,
         bup_ref, wide,
     ) = refs[17:29]
-    narrow, v, own, normed_all, inv_all, tok_all, cot_all, send, recv, sem = refs[29:]
+    narrow, v, own, normed_all, inv_all, tok_all, cot_all, tok_ref, cot_ref, send, recv, sem = refs[29:]
     i = pl.program_id(0)
     steps = n // G
     nz, ny, nx = dims
@@ -222,7 +222,11 @@
     copies.plan("v1", vec_spread((z, y, x), "z"))
     copies.plan("v2", vec_spread((EVERY, y, x), "y"))
     copies.plan("v3", vec_spread((EVERY, EVERY, x), "x"))
-    keep = pltpu.make_async_copy(own, wide.at[mp, z, y, x], sem)
+    keep = pltpu.make_async_copy(own, wide.at[mp, z, y, x], sem.at[0])
+    fetch = [
+        pltpu.make_async_copy(tok_hbm, tok_ref, sem.at[1]),
+        pltpu.make_async_copy(cot_hbm, cot_ref, sem.at[2]),
+    ]
 
     def norms(first, last):
         @pl.loop(first, last)
@@ -236,6 +240,8 @@
 
     @pl.when(i == 0)
     def _():
+        for copy in fetch:
+            copy.start()
         narrow[mp, z, y, x] = jnp.concatenate(
             [wq[...], wk[...], wv[...], jnp.zeros((rows, NARROW - 3 * THIRD), BF)], axis=1
         )
@@ -248,6 +254,8 @@
         v[z, y, x, 8:9, : bup_in.shape[1]] = bup_in[...].astype(F32)
         greet(along, other)
         keep.start()
+        for copy in fetch:
+            copy.wait()
         norms(0, n // 4)
         met(along)
         copies.start("v1", "n1")
@@ -346,7 +354,7 @@
     return pl.pallas_call(
         functools.partial(attn_fwd_kernel, dims, n),
         grid=(n // G,),
-        in_specs=[whole(a.shape) for a in inputs],
+        in_specs=[whole(a.shape) for a in inputs[:-2]] + [pl.BlockSpec(memory_space=pl.ANY)] * 2,
         out_specs=[
             per_step(SP, 3 * D), per_step(HEADS, SP, SP), per_step(SP, D), per_step(SP, D),
             per_step(SP, D), per_step(SP, 128), per_step(SP, D), per_step(SP, D),
@@ -374,9 +382,11 @@
             pltpu.VMEM((n, SP, 128), F32),
             pltpu.VMEM((n, SP, D), BF),
             pltpu.VMEM((n, SP, D), BF),
+            pltpu.VMEM(tokens.shape, BF),
+            pltpu.VMEM(tokens.shape, BF),
             pltpu.SemaphoreType.DMA((count,)),
             pltpu.SemaphoreType.DMA((count,)),
-            pltpu.SemaphoreType.DMA,
+            pltpu.SemaphoreType.DMA((3,)),
         ],
         compiler_params=params(collective_id=0),
         name="attn_fwd",
@@ -400,7 +410,12 @@
     i = pl.program_id(0)
     step = 256
     tiles = FF // step
-    chunks = [slice(c, c + CHUNK) for c in range(0, SP, CHUNK)]
+    steps = n // G
+    chunks = [slice(c, c + CHUNK) for c in range(0, G * SP, CHUNK)]
+
+    def spot(c):
+        image, row = divmod(c.start, SP)
+        return image, slice(row, row + CHUNK)
 
     @pl.when(i == 0)
     def _():
@@ -416,31 +431,37 @@
         dwup_ref[:, cols] += dot_nn(h2t_ref[...], gp_ref[:, cols])
         dwdt_ref[:, cols] += dot_nn(cott_ref[...], act_ref[:, cols])
 
-    def finish(image, beside):
+    def finish(group, beside):
         beside(0)
-        slot = image % 2
+        slot = G * (group % 2)
         for at in chunks:
             gh2, normed, cot = gh2_ref[at, :], norm_ref[at, :], cotf_ref[at, :]
             gres = cot + norm_backward(gh2, normed, inv_ref[at, 0:1], vec_ref[5:6, :])
-            gres_ref[slot, at, :] = gres
+            image, row = spot(at)
+            gres_ref[slot + image, row, :] = gres
             gr_ref[at, :] = gres.astype(BF)
             sums_ref[0] += fold(gres)
             sums_ref[1] += fold(gh2 * normed)
             sums_ref[2] += fold(gh2)
             sums_ref[3] += fold(cot)
         beside(1)
-        gmix_ref[slot] = dot_nn(gr_ref[...], wot_ref[...]).astype(BF)
+        gmix = dot_nn(gr_ref[...], wot_ref[...]).astype(BF)
+        for b in range(G):
+            gmix_ref[slot + b] = gmix[SP * b : SP * (b + 1)]
         beside(2)
-        store_image(outf_ref, image, out_old[...])
+        for b in range(G):
+            store_image(outf_ref, G * group + b, out_old[SP * b : SP * (b + 1), :])
         dwot_ref[...] += dot_tn(gr_ref[...], mix_ref[...])
         beside(3)
 
     finish(jnp.maximum(i - 1, 0), weight_tile)
     weight_tile(4)
-    attended = dot_nt(mixed_ref[0], wot_ref[...])
+    mixed = mixed_ref[...].reshape(G * SP, D)
+    attended = dot_nt(mixed, wot_ref[...])
     for at in chunks:
-        cot = cot_ref[0, at, :].astype(F32)
-        resid = tok_ref[0, at, :].astype(F32) + attended[at] + vec_ref[4:5, :]
+        image, row = spot(at)
+        cot = cot_ref[image, row, :].astype(F32)
+        resid = tok_ref[image, row, :].astype(F32) + attended[at] + vec_ref[4:5, :]
         normed, inv = norm_stats(resid)
         h2_ref[at, :] = (normed * vec_ref[5:6, :] + vec_ref[6:7, :]).astype(BF)
         cotf_ref[at, :] = cot
@@ -448,9 +469,9 @@
         inv_ref[at, :] = jnp.broadcast_to(inv, (CHUNK, 128))
         out_old[at, :] = resid + vec_ref[7:8, :]
     weight_tile(5)
-    mix_ref[...] = mixed_ref[0]
+    mix_ref[...] = mixed
     h2 = h2_ref[...]
-    cot = cot_ref[0]
+    cot = cot_ref[...].reshape(G * SP, D)
     h2t_ref[...] = h2.T
     cott_ref[...] = cot.T
     for j in range(tiles):
@@ -473,7 +494,7 @@
     out_old[...] = out
     gh2_ref[...] = gh2
 
-    @pl.when(i == n - 1)
+    @pl.when(i == steps - 1)
     def _():
         finish(i, weight_tile)
         weight_tile(4)
@@ -507,12 +528,12 @@
     dims = chip_grid(dp)
     n = rows // S
     packed = (2, *dims, D // dp, WIDE)
-    late = pl.BlockSpec((2, SP, D), lambda i: (jnp.maximum(i - 1, 0) // 2, 0, 0))
+    late = pl.BlockSpec((2 * G, SP, D), lambda i: (jnp.maximum(i - 1, 0) // 2, 0, 0))
     return pl.pallas_call(
         functools.partial(mlp_kernel, dims, n),
-        grid=(n,),
+        grid=(n // G,),
         in_specs=[
-            per_image(SP, D), per_image(SP, D), per_image(SP, D), whole((2, D, WIDE)), whole((8, D)),
+            per_step(SP, D), per_step(SP, D), per_step(SP, D), whole((2, D, WIDE)), whole((8, D)),
             whole((1, FF)),
         ],
         out_specs=[whole((rows, D)), late, late, whole(packed), whole((8, D)), whole((1, FF))],
@@ -525,12 +546,12 @@
             jax.ShapeDtypeStruct((1, FF), F32),
         ],
         scratch_shapes=[
-            pltpu.VMEM((SP, FF), BF), pltpu.VMEM((SP, FF), BF), pltpu.VMEM((D, D), BF),
+            pltpu.VMEM((G * SP, FF), BF), pltpu.VMEM((G * SP, FF), BF), pltpu.VMEM((D, D), BF),
             pltpu.VMEM((D, D), F32), pltpu.VMEM((D, FF), F32), pltpu.VMEM((D, FF), F32),
-            pltpu.VMEM((SP, D), BF), pltpu.VMEM((D, SP), BF), pltpu.VMEM((D, SP), BF),
-            pltpu.VMEM((SP, D), BF), pltpu.VMEM((SP, D), BF), pltpu.VMEM((rows, D), F32),
-            pltpu.VMEM((SP, D), F32), pltpu.VMEM((SP, D), F32), pltpu.VMEM((SP, D), F32),
-            pltpu.VMEM((SP, D), F32), pltpu.VMEM((SP, 128), F32), pltpu.VMEM((4, 8, D), F32),
+            pltpu.VMEM((G * SP, D), BF), pltpu.VMEM((D, G * SP), BF), pltpu.VMEM((D, G * SP), BF),
+            pltpu.VMEM((G * SP, D), BF), pltpu.VMEM((G * SP, D), BF), pltpu.VMEM((rows, D), F32),
+            pltpu.VMEM((G * SP, D), F32), pltpu.VMEM((G * SP, D), F32), pltpu.VMEM((G * SP, D), F32),
+            pltpu.VMEM((G * SP, D), F32), pltpu.VMEM((G * SP, 128), F32), pltpu.VMEM((4, 8, D), F32),
             pltpu.VMEM((8, FF), F32),
         ],
         compiler_params=params(),
@@ -876,33 +897,40 @@
     )(qkv, e, mixed, linv, gmix, normed, inv, gres, wqkv, vec, dvec2, dbup, packed)
 
 
-def split_kernel(n, narrow_ref, wide_ref, vec_ref, *outs):
-    for j in range(3):
-        outs[j][...] = narrow_ref[:, THIRD * j : THIRD * (j + 1)]
-    outs[3][...] = wide_ref[:, :THIRD]
-    outs[4][...] = wide_ref[:, OUT_PAD : OUT_PAD + HALF]
-    outs[5][...] = wide_ref[:, OUT_PAD + HALF :]
-    index = lax.axis_index("dp") * 2 + lax.axis_index("mp")
-    per = D // n
-    vec = pltpu.roll(vec_ref[...], D - index * per, axis=1)
-    for row, out in zip((2, 3, 0, 1, 4, 5, 6, 7), outs[6:]):
-        out[...] = vec[row : row + 1, :per]
-    wide = jnp.concatenate([vec_ref[8 + j : 9 + j, :] for j in range(FF // D)], axis=1)
-    wide = pltpu.roll(jnp.broadcast_to(wide, (8, FF)), FF - index * (FF // n), axis=1)
-    outs[14][...] = wide[0:1, : FF // n]
-
-
-def split(narrow, wide, vec, n):
+def split_kernel(n, gtok_in, narrow_ref, wide_ref, vec_ref, gtok_ref, *outs):
+    gtok_ref[...] = gtok_in[...]
+
+    @pl.when(pl.program_id(0) == 0)
+    def _():
+        for j in range(3):
+            outs[j][...] = narrow_ref[:, THIRD * j : THIRD * (j + 1)]
+        outs[3][...] = wide_ref[:, :THIRD]
+        outs[4][...] = wide_ref[:, OUT_PAD : OUT_PAD + HALF]
+        outs[5][...] = wide_ref[:, OUT_PAD + HALF :]
+        index = lax.axis_index("dp") * 2 + lax.axis_index("mp")
+        per = D // n
+        vec = pltpu.roll(vec_ref[...], D - index * per, axis=1)
+        for row, out in zip((2, 3, 0, 1, 4, 5, 6, 7), outs[6:]):
+            out[...] = vec[row : row + 1, :per]
+        wide = jnp.concatenate([vec_ref[8 + j : 9 + j, :] for j in range(FF // D)], axis=1)
+        wide = pltpu.roll(jnp.broadcast_to(wide, (8, FF)), FF - index * (FF // n), axis=1)
+        outs[14][...] = wide[0:1, : FF // n]
+
+
+def split(gtok, narrow, wide, vec, n):
     rows = narrow.shape[0]
-    vmem = pl.BlockSpec(memory_space=pltpu.VMEM)
+    tall = gtok.shape[0]
     shapes = [(rows, THIRD)] * 4 + [(rows, HALF)] * 2 + [(1, D // n)] * 8 + [(1, FF // n)]
+    half = pl.BlockSpec((tall // 2, D), lambda i: (i, 0))
     return pl.pallas_call(
         functools.partial(split_kernel, n),
-        in_specs=[vmem] * 3,
-        out_specs=[vmem] * 15,
-        out_shape=[jax.ShapeDtypeStruct(s, F32) for s in shapes],
+        grid=(2,),
+        in_specs=[half] + [whole(a.shape) for a in (narrow, wide, vec)],
+        out_specs=[half] + [whole(s) for s in shapes],
+        out_shape=[jax.ShapeDtypeStruct(s, F32) for s in [(tall, D), *shapes]],
+        compiler_params=params(),
         name="split",
-    )(narrow, wide, vec)
+    )(gtok, narrow, wide, vec)
 
 
 def whole(shape):
@@ -941,7 +969,7 @@
         qkv, e, mixed, linv, gmix, normed, inv, gres, wqkv, vec, dvec2, dbup, packed,
         tokens.shape[0], dp,
     )
-    grads = split(narrow_sum, wide_sum, sums, dp * lax.axis_size("mp"))
+    gtok, *grads = split(gtok, narrow_sum, wide_sum, sums, dp * lax.axis_size("mp"))
     vecs = [v.reshape(-1) for v in grads[6:]]
     return (
         out, gtok, grads[0], grads[1], grads[2], grads[3].T, grads[4], grads[5].T,

time: 160 us -> 155 us (0.969)
  local copies, waits for them, and re-layouts: 4.91 us -> 0 us
    unnamed x1 -> x0, local copies, waits for them, and re-layouts: 4.91 us -> none
where the time goes in v7:
time: 155 us
  Pallas kernels  154 us (99%)
    pallas_call x1, Pallas kernels, backward(): pl.pallas_call(functools.partial(backward_kernel, dims, n), grid=(2 * ste...  52.7 us
    pallas_call x1, Pallas kernels, mlp(): pl.pallas_call(functools.partial(mlp_kernel, dims, n), grid=(n // G,), in...  51.1 us
    pallas_call x1, Pallas kernels, attn_fwd(): pl.pallas_call(functools.partial(attn_fwd_kernel, dims, n), grid=(n // G,...  45.9 us
    pallas_call x1, Pallas kernels, split(): pl.pallas_call(functools.partial(split_kernel, n), grid=(2,), in_specs=[h...  4.34 us

profile of v7, /device:TPU:0, one launch (start us, length us, event | category | flops | bytes accessed | tf_op | source)
XLA Modules:
  0.0 154.9 jit_solution(2915734525729899671)
XLA Ops:
  0.7 45.9 %attn_fwd.1 = (bf16[16,208,1152]{2,1,0:T(8,128)(2,1)}, bf16[16,6,208,208]{3,2,1,0:T(8,128)(2,1)}, bf16[16,208,384]{2,1,0:T(8,128)(2,1)}, f32[16,208,384]{2,1,0:T...) custom-call(bf16[24,192]{1,0:T(8,128)(2,1)} %refs_0_.1, ...), custom_call_target="tpu_custom_call" | custom-call | tf_op jit(solution)/shard_map/attn_fwd/pallas_call | solution.py:354
  46.6 51.1 %mlp.1 = (bf16[3152,384]{1,0:T(8,128)(2,1)}, f32[16,208,384]{2,1,0:T(8,128)}, bf16[16,208,384]{2,1,0:T(8,128)(2,1)}, bf16[2,4,2,2,24,1792]{5,4,3,2,1,0:T(8,128)(...) custom-call(bf16[16,208,384]{2,1,0:T(8,128)(2,1)} %get-tuple-element.55.tok_ref, ...), custom_call_target="tpu_custom_call" | custom-call | tf_op jit(solution)/shard_map/mlp/pallas_call | solution.py:532
  97.7 52.7 %backward.1 = (f32[3152,384]{1,0:T(8,128)}, f32[24,640]{1,0:T(8,128)}, f32[24,1792]{1,0:T(8,128)}, f32[16,384]{1,0:T(8,128)}) custom-call(bf16[16,208,1152]{2,1,0:T(8,128)(2,1)} %get-tuple-element.62.qkv_ref, bf16[16,6,208,208]{3,2,1,0:T(8,128)(2,1)} %get-tuple-element.63.e_ref, bf16[16,208,384]{2,1,0:T(8,128)(2,1)} %get-tuple-element.57.mixed_ref, ...), custom_call_target="tpu_custom_call" | custom-call | tf_op jit(solution)/shard_map/backward/pallas_call | solution.py:863
  150.4 4.3 %split.1 = (f32[3152,384]{1,0:T(8,128)}, f32[24,192]{1,0:T(8,128)}, f32[24,192]{1,0:T(8,128)}, f32[24,192]{1,0:T(8,128)}, f32[24,192]{1,0:T(8,128)}, /*index=5*/...) custom-call(f32[3152,384]{1,0:T(8,128)} %get-tuple-element.73.gtok_i, ...), custom_call_target="tpu_custom_call" | custom-call | tf_op jit(solution)/shard_map/split/pallas_call | solution.py:925

commit v8 on v7

--- a/solution.py
+++ b/solution.py
@@ -313,25 +313,42 @@
     is_key = lax.broadcasted_iota(jnp.int32, (SP, SP), 1) < S
     zero = jnp.zeros((SP, 2 * HD), BF)
     one = jnp.ones((SP, 2 * HD), BF)
-    for p in range(PAIRS):
+    work = [(p, b) for p in range(PAIRS) for b in range(G)]
+
+    def own_lanes(h):
+        return (lane < HD) if h == 0 else (lane >= HD)
+
+    def weigh(turn):
+        p, b = work[turn]
         cols = slice(2 * HD * p, 2 * HD * (p + 1))
-        for b in range(G):
-            qp, kp, vp = (x[SP * b : SP * (b + 1), cols] for x in (q, k, value))
-            total = None
-            for h in range(2):
-                mine = (lane < HD) if h == 0 else (lane >= HD)
-                kh = jnp.where(mine, kp, zero)
-                vh = jnp.where(mine, vp, zero)
-                scores = dot_nt(qp, kh)
-                scores = jnp.where(is_key, scores, -1e30)
-                top = jnp.max(scores, axis=-1, keepdims=True)
-                e = jnp.exp2(scores - top).astype(BF)
-                e_ref[b, 2 * p + h] = e
-                part = dot_nn(e, jnp.concatenate([vh, jnp.where(mine, one, zero)], axis=1))
-                total = part if total is None else total + part
-            linv = 1.0 / total[:, 2 * HD :]
-            linv_ref[b, :, cols] = linv
-            mixed_ref[b, :, cols] = (total[:, : 2 * HD] * linv).astype(BF)
+        rows_of = slice(SP * b, SP * (b + 1))
+        for h in range(2):
+            scores = dot_nt(q[rows_of, cols], jnp.where(own_lanes(h), k[rows_of, cols], zero))
+            scores = jnp.where(is_key, scores, -1e30)
+            top = jnp.max(scores, axis=-1, keepdims=True)
+            e_ref[b, 2 * p + h] = jnp.exp2(scores - top).astype(BF)
+
+    def mix(turn):
+        p, b = work[turn]
+        cols = slice(2 * HD * p, 2 * HD * (p + 1))
+        total = None
+        for h in range(2):
+            mine = own_lanes(h)
+            vh = jnp.where(mine, value[SP * b : SP * (b + 1), cols], zero)
+            part = dot_nn(
+                e_ref[b, 2 * p + h],
+                jnp.concatenate([vh, jnp.where(mine, one, zero)], axis=1),
+            )
+            total = part if total is None else total + part
+        linv = 1.0 / total[:, 2 * HD :]
+        linv_ref[b, :, cols] = linv
+        mixed_ref[b, :, cols] = (total[:, : 2 * HD] * linv).astype(BF)
+
+    weigh(0)
+    for turn in range(len(work)):
+        if turn + 1 < len(work):
+            weigh(turn + 1)
+        mix(turn)
 
     @pl.when(i == steps - 2)
     def _():
@@ -661,9 +678,9 @@
     dims, n, qkv_ref, e_ref, mixed_ref, linv_ref, gmix_ref, normed_ref, inv_ref, gres_ref, w_ref,
     vec_ref, dvec2_ref, dbup_ref, packed, gtok_ref, narrow_ref, wide_ref, total_ref, *refs,
 ):
-    g_ref, acc_ref, gsum_ref, narrow, sums, vs, vr = refs[:7]
-    wide_bufs, mine, narrow_bufs = refs[7:16], refs[16], refs[17:26]
-    send, recv, sem = refs[26:]
+    g_ref, acc_ref, gsum_ref, ds_ref, go_ref, narrow, sums, vs, vr = refs[:9]
+    wide_bufs, mine, narrow_bufs = refs[9:18], refs[18], refs[19:28]
+    send, recv, sem = refs[28:]
     i = pl.program_id(0)
     steps = n // G
     copies = Copies(send, recv)
@@ -722,36 +739,52 @@
         lane = lax.broadcasted_iota(jnp.int32, (SP, 2 * HD), 1)
         zero = jnp.zeros((SP, 2 * HD), BF)
         minus = jnp.full((SP, 2 * HD), -1.0, BF)
-        for p in range(PAIRS):
+        work = [(p, b) for p in range(PAIRS) for b in range(G)]
+
+        def scores_grad(turn):
+            p, b = work[turn]
             lo, hi = 2 * HD * p, 2 * HD * (p + 1)
-            for b in range(G):
-                q = qkv_ref[b, :, lo:hi]
-                k = qkv_ref[b, :, D + lo : D + hi]
-                v = qkv_ref[b, :, 2 * D + lo : 2 * D + hi]
-                go_f = gmix_ref[b, :, lo:hi].astype(F32) * linv_ref[b, :, lo:hi]
-                go = go_f.astype(BF)
-                god = jnp.concatenate(
-                    [go, (go_f * mixed_ref[b, :, lo:hi].astype(F32)).astype(BF)], axis=1
+            v = qkv_ref[b, :, 2 * D + lo : 2 * D + hi]
+            go_f = gmix_ref[b, :, lo:hi].astype(F32) * linv_ref[b, :, lo:hi]
+            go = go_f.astype(BF)
+            go_ref[turn % 2] = go
+            god = jnp.concatenate(
+                [go, (go_f * mixed_ref[b, :, lo:hi].astype(F32)).astype(BF)], axis=1
+            )
+            for h in range(2):
+                own = (lane < HD) if h == 0 else (lane >= HD)
+                vd = jnp.concatenate(
+                    [jnp.where(own, v, zero), jnp.where(own, minus, zero)], axis=1
                 )
-                gq = gk = gv = None
-                for h in range(2):
-                    own = (lane < HD) if h == 0 else (lane >= HD)
-                    e = e_ref[b, 2 * p + h]
-                    vd = jnp.concatenate(
-                        [jnp.where(own, v, zero), jnp.where(own, minus, zero)], axis=1
-                    )
-                    ds = e * dot_nt(god, vd).astype(BF)
-                    part_q = dot_nn(ds, jnp.where(own, k, zero))
-                    part_k = dot_tn(ds, jnp.where(own, q, zero))
-                    part_v = dot_tn(e, jnp.where(own, go, zero))
-                    gq = part_q if gq is None else gq + part_q
-                    gk = part_k if gk is None else gk + part_k
-                    gv = part_v if gv is None else gv + part_v
-                gq = gq * (1.0 / math.sqrt(HD))
-                gk = gk * (1.0 / LOG2E)
-                for j, grad in enumerate((gq, gk, gv)):
-                    gsum_ref[:, D * j + lo : D * j + hi] += fold(grad)
-                    g_ref[i, SP * b : SP * (b + 1), D * j + lo : D * j + hi] = grad.astype(BF)
+                ds_ref[turn % 2, h] = e_ref[b, 2 * p + h] * dot_nt(god, vd).astype(BF)
+
+        def inputs_grad(turn):
+            p, b = work[turn]
+            lo, hi = 2 * HD * p, 2 * HD * (p + 1)
+            q = qkv_ref[b, :, lo:hi]
+            k = qkv_ref[b, :, D + lo : D + hi]
+            go = go_ref[turn % 2]
+            gq = gk = gv = None
+            for h in range(2):
+                own = (lane < HD) if h == 0 else (lane >= HD)
+                ds = ds_ref[turn % 2, h]
+                part_q = dot_nn(ds, jnp.where(own, k, zero))
+                part_k = dot_tn(ds, jnp.where(own, q, zero))
+                part_v = dot_tn(e_ref[b, 2 * p + h], jnp.where(own, go, zero))
+                gq = part_q if gq is None else gq + part_q
+                gk = part_k if gk is None else gk + part_k
+                gv = part_v if gv is None else gv + part_v
+            gq = gq * (1.0 / math.sqrt(HD))
+            gk = gk * (1.0 / LOG2E)
+            for j, grad in enumerate((gq, gk, gv)):
+                gsum_ref[:, D * j + lo : D * j + hi] += fold(grad)
+                g_ref[i, SP * b : SP * (b + 1), D * j + lo : D * j + hi] = grad.astype(BF)
+
+        scores_grad(0)
+        for turn in range(len(work)):
+            if turn + 1 < len(work):
+                scores_grad(turn + 1)
+            inputs_grad(turn)
         acc_ref[...] += dot_tn(normed_ref[...].reshape(G * SP, D).astype(BF), g_ref[i])
 
     @pl.when(i == steps - 1)
@@ -762,12 +795,9 @@
         group = 48 // rows
         turned = vec_ref[...].T
         gsum = row_sum(gsum_ref[...])
-        gains = []
         for t in range(len(spots) // group):
             at = slice(48 * t, 48 * (t + 1))
-            acc = acc_ref[at, :]
-            gains.append(jnp.sum(acc * w_ref[at, :].astype(F32), axis=1, keepdims=True))
-            dw = acc * turned[at, 0:1] + turned[at, 1:2] * gsum
+            dw = acc_ref[at, :] * turned[at, 0:1] + turned[at, 1:2] * gsum
             for m in range(2):
                 parts = [dw[:, D * j + THIRD * m : D * j + THIRD * (m + 1)] for j in range(3)]
                 parts.append(jnp.zeros((48, NARROW - 3 * THIRD), F32))
@@ -776,6 +806,13 @@
                     narrow[(m,) + spots[t * group + k]] = block[
                         k * rows : (k + 1) * rows
                     ].astype(BF)
+        copies.start("npair")
+        gains = [
+            jnp.sum(
+                acc_ref[c : c + 48, :] * w_ref[c : c + 48, :].astype(F32), axis=1, keepdims=True
+            )
+            for c in range(0, D, 48)
+        ]
         high = gsum.astype(BF)
         low = (gsum - high.astype(F32)).astype(BF)
         row = lax.broadcasted_iota(jnp.int32, (16, 3 * D), 0)
@@ -789,7 +826,7 @@
         for j in range(FF // D):
             sums[8 + j : 9 + j] = dbup_ref[:, D * j : D * (j + 1)]
         sums[12:16] = jnp.zeros((4, D), F32)
-        copies.start("npair", "v0")
+        copies.start("v0")
 
     @pl.when(i == steps + 2)
     def _():
@@ -881,6 +918,8 @@
             pltpu.VMEM((steps, G * SP, 3 * D), BF),
             pltpu.VMEM((D, 3 * D), F32),
             pltpu.VMEM((8, 3 * D), F32),
+            pltpu.VMEM((2, 2, SP, SP), BF),
+            pltpu.VMEM((2, SP, 2 * HD), BF),
             pltpu.VMEM((2, *dims, rows, NARROW), BF),
             pltpu.VMEM((16, D), F32),
             pltpu.VMEM((3, 16, D), F32),

time: 155 us -> 152 us (0.981)
  Pallas kernels: 154 us -> 150 us
    pallas_call x1, Pallas kernels: 52.7 us -> 49.2 us  [backward(): pl.pallas_call(functools.partial(backward_kernel, dims, n), grid=(2 * ste...]
where the time goes in v8:
time: 152 us; the launch traced here: 151 us
  Pallas kernels  150 us (99%)
    pallas_call x1, Pallas kernels, mlp(): pl.pallas_call(functools.partial(mlp_kernel, dims, n), grid=(n // G,), in...  51.1 us
    pallas_call x1, Pallas kernels, backward(): pl.pallas_call(functools.partial(backward_kernel, dims, n), grid=(2 * ste...  49.2 us
    pallas_call x1, Pallas kernels, attn_fwd(): pl.pallas_call(functools.partial(attn_fwd_kernel, dims, n), grid=(n // G,...  45.8 us
    pallas_call x1, Pallas kernels, split(): pl.pallas_call(functools.partial(split_kernel, n), grid=(2,), in_specs=[h...  4.34 us

profile of v8, /device:TPU:0, one launch (start us, length us, event | category | flops | bytes accessed | tf_op | source)
XLA Modules:
  0.0 151.3 jit_solution(580894764948314810)
XLA Ops:
  0.7 45.8 %attn_fwd.1 = (bf16[16,208,1152]{2,1,0:T(8,128)(2,1)}, bf16[16,6,208,208]{3,2,1,0:T(8,128)(2,1)}, bf16[16,208,384]{2,1,0:T(8,128)(2,1)}, f32[16,208,384]{2,1,0:T...) custom-call(bf16[24,192]{1,0:T(8,128)(2,1)} %refs_0_.1, ...), custom_call_target="tpu_custom_call" | custom-call | tf_op jit(solution)/shard_map/attn_fwd/pallas_call | solution.py:371
  46.5 51.1 %mlp.1 = (bf16[3152,384]{1,0:T(8,128)(2,1)}, f32[16,208,384]{2,1,0:T(8,128)}, bf16[16,208,384]{2,1,0:T(8,128)(2,1)}, bf16[2,4,2,2,24,1792]{5,4,3,2,1,0:T(8,128)(...) custom-call(bf16[16,208,384]{2,1,0:T(8,128)(2,1)} %get-tuple-element.55.tok_ref, ...), custom_call_target="tpu_custom_call" | custom-call | tf_op jit(solution)/shard_map/mlp/pallas_call | solution.py:549
  97.6 49.2 %backward.1 = (f32[3152,384]{1,0:T(8,128)}, f32[24,640]{1,0:T(8,128)}, f32[24,1792]{1,0:T(8,128)}, f32[16,384]{1,0:T(8,128)}) custom-call(bf16[16,208,1152]{2,1,0:T(8,128)(2,1)} %get-tuple-element.62.qkv_ref, bf16[16,6,208,208]{3,2,1,0:T(8,128)(2,1)} %get-tuple-element.63.e_ref, bf16[16,208,384]{2,1,0:T(8,128)(2,1)} %get-tuple-element.57.mixed_ref, ...), custom_call_target="tpu_custom_call" | custom-call | tf_op jit(solution)/shard_map/backward/pallas_call | solution.py:900
  146.8 4.3 %split.1 = (f32[3152,384]{1,0:T(8,128)}, f32[24,192]{1,0:T(8,128)}, f32[24,192]{1,0:T(8,128)}, f32[24,192]{1,0:T(8,128)}, f32[24,192]{1,0:T(8,128)}, /*index=5*/...) custom-call(f32[3152,384]{1,0:T(8,128)} %get-tuple-element.73.gtok_i, ...), custom_call_target="tpu_custom_call" | custom-call | tf_op jit(solution)/shard_map/split/pallas_call | solution.py:964
